TPU v7x, 128 devices: a whole 4x4x4 slice. The times are simulated.
128 devices in a mesh: sp: 8 (over z, core), tp: 16 (over x, y).
Axes of the slice: x: 4, y: 4, z: 4, core: 2. Of those that a mesh axis runs over, the one named last changes fastest.
Arguments:
- tokens: bfloat16 [16384, 2048], P(('sp', 'tp')), may hold values from -3 to 3
- queries: bfloat16 [16384, 2048], P(('sp', 'tp')), may hold values from -140 to 140
- keys: bfloat16 [16384, 1024], P(('sp', 'tp')), may hold values from -6 to 6
- values: bfloat16 [16384, 1024], P(('sp', 'tp')), may hold values from -6 to 6
- out_weight: bfloat16 [2048, 2048], P('sp', 'tp'), may hold values from -0.25 to 0.25
- norm_gain: bfloat16 [2048], replicated, may hold values from 0.099609375 to 1.8984375
- gate_weight: bfloat16 [2048, 7168], P('sp', 'tp'), may hold values from -0.125 to 0.125
- up_weight: bfloat16 [2048, 7168], P('sp', 'tp'), may hold values from -0.125 to 0.125
- down_weight: bfloat16 [7168, 2048], P('tp', 'sp'), may hold values from -0.125 to 0.125
Outputs:
- attended: bfloat16 [16384, 2048], P(('sp', 'tp'))
- layer_out: bfloat16 [16384, 2048], P(('sp', 'tp'))
All inputs are finite; a program needn't handle non-finite values.
Results may differ from a plain program's by a relative error of at most 0.023.
Values may be sent and summed in bfloat16 or wider, within the bound.
No kernel may reach another device: no remote copies, remote signals or barrier semaphores. Data moves between devices by JAX's collectives and lax.ppermute only.
A program may use at most 128 MiB of HBM per device.

v0:
```python
import jax
import jax.numpy as jnp
from jax import lax
from jax.sharding import PartitionSpec as P

HEAD_DIM = 128


norm_eps = 1e-05


def side_by_side(arrays, axis, dim, along):
    both = jnp.concatenate(arrays, axis=along)
    result, at, done = (lax.all_gather(both, axis, axis=dim, tiled=True), 0, [])
    for a in arrays:
        done.append(lax.slice_in_dim(result, at, at + a.shape[along], axis=along))
        at += a.shape[along]
    return tuple(done)


def sent_to_all(array, axis):
    copies = jnp.broadcast_to(array, (lax.axis_size(axis), *array.shape))
    return lax.all_to_all(copies, axis, split_axis=0, concat_axis=0, tiled=True)


def joined_along(blocks, dim):
    dims = list(blocks.shape[1:])
    dims[dim] *= blocks.shape[0]
    return jnp.moveaxis(blocks, 0, dim).reshape(dims)


def gather_directly(array, axis, dim):
    blocks = sent_to_all(array, axis)
    return joined_along(blocks, dim)


def attend(q_block, query_pos, k_block, v_block, key_pos, kv_local):
    row_count = q_block.shape[0]
    key_count = k_block.shape[0]
    q_four = q_block.reshape(row_count, kv_local, -1, HEAD_DIM)
    k_three = k_block.reshape(key_count, kv_local, HEAD_DIM)
    v_three = v_block.reshape(key_count, kv_local, HEAD_DIM)
    scores = jnp.einsum(
        "qhgd,khd->hgqk", q_four, k_three, preferred_element_type=jnp.float32
    ) * HEAD_DIM ** (-0.5)
    causal = key_pos[None, :] <= query_pos[:, None]
    scores = jnp.where(causal[None, None, :, :], scores, -1e30)
    row_peak = jnp.max(scores, axis=-1, keepdims=True)
    exp_terms = jnp.exp(scores - row_peak)
    probs = (exp_terms / jnp.sum(exp_terms, axis=-1, keepdims=True)).astype(jnp.bfloat16)
    mixed_out = jnp.einsum("hgqk,khd->qhgd", probs, v_three, preferred_element_type=jnp.float32)
    return mixed_out.astype(jnp.bfloat16).reshape(row_count, -1)


def add_rows(all_rows, weight_piece):
    return jnp.dot(all_rows, weight_piece, preferred_element_type=jnp.float32)


def shards(
    tokens, queries, keys, values, out_weight, norm_gain, gate_weight, up_weight, down_weight
):
    shard_rows = tokens.shape[0]
    sp_count = lax.axis_size("sp")
    tp_count = lax.axis_size("tp")
    segment_len = shard_rows * tp_count
    seq_len = segment_len * sp_count
    local_q = lax.all_to_all(queries, "sp", split_axis=1, concat_axis=0, tiled=True)
    part_keys, part_values = (
        lax.all_to_all(keys, "sp", split_axis=1, concat_axis=0, tiled=True),
        lax.all_to_all(values, "sp", split_axis=1, concat_axis=0, tiled=True),
    )
    width_kv = part_keys.shape[1]
    grid_keys, grid_values = side_by_side(
        (
            part_keys.reshape(sp_count, shard_rows, width_kv),
            part_values.reshape(sp_count, shard_rows, width_kv),
        ),
        "tp",
        1,
        0,
    )
    all_keys = grid_keys.reshape(seq_len, width_kv)
    all_values = grid_values.reshape(seq_len, width_kv)
    kv_local = all_keys.shape[1] // HEAD_DIM
    query_index = jnp.arange(sp_count * shard_rows, dtype=jnp.int32)
    query_pos = (
        query_index // shard_rows * segment_len
        + lax.axis_index("tp") * shard_rows
        + query_index % shard_rows
    )
    key_pos = jnp.arange(seq_len, dtype=jnp.int32)
    pieces_out = []
    for segment in range(sp_count):
        first_row = segment * shard_rows
        key_reach = (segment + 1) * segment_len
        pieces_out.append(
            attend(
                local_q[first_row : first_row + shard_rows],
                query_pos[first_row : first_row + shard_rows],
                all_keys[:key_reach],
                all_values[:key_reach],
                key_pos[:key_reach],
                kv_local,
            )
        )
    attn = jnp.concatenate(pieces_out, axis=0)
    wo_full = lax.all_gather(out_weight, "tp", axis=1, tiled=True)
    block_rows = attn
    attn_part = lax.psum_scatter(
        jnp.dot(block_rows, wo_full, preferred_element_type=jnp.float32).astype(jnp.bfloat16),
        "sp",
        scatter_dimension=0,
        tiled=True,
    ).astype(jnp.float32)
    attended = (tokens.astype(jnp.float32) + attn_part).astype(jnp.bfloat16)
    attended_wide = attended.astype(jnp.float32)
    inverse_rms = lax.rsqrt(
        jnp.mean(attended_wide * attended_wide, axis=1, keepdims=True) + norm_eps
    )
    normed = (attended_wide * inverse_rms * norm_gain.astype(jnp.float32)).astype(jnp.bfloat16)
    all_rows = lax.all_gather(normed, "tp", axis=0, tiled=True)

    def add_single(weight_piece):
        return add_rows(all_rows, weight_piece)

    gate_sum = add_single(gather_directly(gate_weight, "sp", 0))
    up_sum = add_single(lax.all_gather(up_weight, "sp", axis=0, tiled=True))
    hidden = (jax.nn.silu(gate_sum) * up_sum).astype(jnp.bfloat16)
    down_full = lax.all_gather(down_weight, "sp", axis=1, tiled=True)
    block_rows = hidden
    ffn_part = lax.psum_scatter(
        jnp.dot(block_rows, down_full, preferred_element_type=jnp.float32).astype(jnp.bfloat16),
        "tp",
        scatter_dimension=0,
        tiled=True,
    ).astype(jnp.float32)
    layer_out = (attended_wide + ffn_part).astype(jnp.bfloat16)
    return (attended, layer_out)


def solution(mesh):
    return jax.shard_map(
        shards,
        mesh=mesh,
        in_specs=(
            P(("sp", "tp"), None),
            P(("sp", "tp"), None),
            P(("sp", "tp"), None),
            P(("sp", "tp"), None),
            P("sp", "tp"),
            P(),
            P("sp", "tp"),
            P("sp", "tp"),
            P("tp", "sp"),
        ),
        out_specs=(P(("sp", "tp"), None), P(("sp", "tp"), None)),
        check_vma=False,
    )
```

profile of v0, /device:TPU:0, one launch (start us, length us, event | category | flops | bytes accessed | tf_op | source)
XLA Modules:
  0.0 448.5 jit_solution(11308070882767555244)
XLA Ops:
  9.2 5.4 %all-to-all-start.1 = ((bf16[128,8,128]{2,0,1:T(8,128)(2,1)}), bf16[128,8,128]{2,0,1:T(8,128)(2,1)S(1)}, u32[]{:S(2)}, u32[]{:S(2)}) async-start(bf16[128,8,128]{2,0,1:T(8,128)(2,1)} %copy.90), calls=%async_computation.1 | async-start | bytes 524288 | tf_op jit(solution)/shard_map/all_to_all | solution.py:70
  16.0 6.1 %all-to-all-done.1 = bf16[128,8,128]{2,0,1:T(8,128)(2,1)S(1)} async-done(((bf16[128,8,128]{2,0,1:T(8,128)(2,1)}), bf16[128,8,128]{2,0,1:T(8,128)(2,1)S(1)}, u32[]{:S(2)}, u32[]{:S(2)}) %all-to-all-start.1) | async-done | bytes 262176 | tf_op jit(solution)/shard_map/all_to_all | solution.py:70
  22.1 9.9 %all_to_all.53 = bf16[128,8,128]{2,0,1:T(8,128)(2,1)S(1)} all-to-all(bf16[128,8,128]{2,0,1:T(8,128)(2,1)S(1)} %copy.88), channel_id=1, replica_groups=mesh['sp'=8,'tp'=16] {'sp'}, dimensions={1} | all-to-all | bytes 524288 | tf_op jit(solution)/shard_map/all_to_all | solution.py:69
  33.9 3.5 all-to-all-start.2
  38.3 2.4 iota_compare_fusion
  42.6 3.4 broadcast_compare_fusion.4
  46.0 4.4 broadcast_compare_fusion.3
  50.4 5.5 %broadcast_compare_fusion.2 = pred[128,10240]{0,1:T(8,128)(4,1)} fusion(s32[128]{0:T(128)S(1)} %get-tuple-element.29, s32[10240]{0:T(1024)S(1)} %iota_add_fusion.2), kind=kLoop, calls=%fused_computation.62 | loop fusion | flops 1310720 | bytes 1352192 | tf_op jit(solution)/shard_map/le | solution.py:46
  55.9 6.4 %broadcast_compare_fusion.1 = pred[128,12288]{0,1:T(8,128)(4,1)} fusion(s32[128]{0:T(128)S(1)} %get-tuple-element.28, s32[12288]{0:T(1024)S(1)} %iota_add_fusion.1), kind=kLoop, calls=%fused_computation.59 | loop fusion | flops 1572864 | bytes 1622528 | tf_op jit(solution)/shard_map/le | solution.py:46
  62.3 7.0 %broadcast_compare_fusion = pred[128,14336]{0,1:T(8,128)(4,1)S(1)} fusion(s32[128]{0:T(128)S(1)} %get-tuple-element.27, s32[14336]{0:T(1024)S(1)} %iota_add_fusion), kind=kLoop, calls=%fused_computation.56 | loop fusion | flops 1835008 | bytes 1892864 | tf_op jit(solution)/shard_map/le | solution.py:46
  70.4 32.9 %all-gather.6.cloned.1.call-done = bf16[16,2048,128]{2,1,0:T(8,128)(2,1)} async-done(((bf16[16,128,128]{2,1,0:T(8,128)(2,1)}), bf16[16,2048,128]{2,1,0:T(8,128)(2,1)}) %all-gather.6.cloned.1.call-update) | async-done | bytes 8388624 | tf_op jit(solution)/shard_map/all_gather | solution.py:14
  123.1 2.2 fusion.87
  130.2 2.7 fusion.88
  134.7 2.5 fusion.50
  137.7 6.8 %fusion.89 = (f32[2,128]{1,0:T(2,128)S(1)}, f32[1,2,128,14336]{2,3,1,0:T(8,128)}) fusion(bf16[14336,128,1]{1,0,2:T(8,128)(2,1)S(1)} %bitcast.229, bf16[128,2,128]{0,2,1:T(8,128)(2,1)S(1)} %bitcast.247, pred[128,14336]{0,1:T(8,128)(4,1)S(1)} %broadcast_compare_fusion), kind=kOutput, calls=%fused_computation.138 | convolution fusion | flops 950533888 | bytes 20251648 | tf_op jit(solution)/shard_map/qhgd,khd->hgqk/dot_general | solution.py:43
  144.6 7.4 %fusion.8 = f32[2,128]{1,0:T(2,128)S(1)} fusion(f32[1,2,128,14336]{2,3,1,0:T(8,128)} %get-tuple-element.47, f32[2,128]{1,0:T(2,128)S(1)} %get-tuple-element.46), kind=kLoop, calls=%fused_computation.16 | loop fusion | flops 7339776 | bytes 14682112 | tf_op jit(solution)/shard_map/reduce_sum | solution.py:50
  152.0 6.7 %fusion.53 = bf16[128,2,128]{2,0,1:T(8,128)(2,1)S(1)} fusion(bf16[14336,128,1]{1,0,2:T(8,128)(2,1)S(1)} %bitcast.228, f32[2,128]{1,0:T(2,128)S(1)} %fusion.8, f32[1,2,128,14336]{2,3,1,0:T(8,128)} %get-tuple-element.47, f32[2,128]{1,0:T(2,128)S(1)} %get-tuple-element.46), kind=kOutput, calls=%fused_computation.79 | convolution fusion | flops 950566912 | bytes 18417664 | tf_op jit(solution)/shard_map/hgqk,khd->qhgd/dot_general | solution.py:51
  158.7 2.2 fusion.74
  161.0 5.2 %fusion.90 = (f32[2,128]{1,0:T(2,128)S(1)}, f32[1,2,128,16384]{2,3,1,0:T(8,128)S(1)}) fusion(bf16[16384,128,1]{1,0,2:T(8,128)(2,1)} %bitcast.227, bf16[128,2,128]{0,2,1:T(8,128)(2,1)S(1)} %bitcast.246, pred[128,16384]{0,1:T(8,128)(4,1)S(1)} %copy-done.2), kind=kOutput, calls=%fused_computation.139 | convolution fusion | flops 1086324480 | bytes 23135232 | tf_op jit(solution)/shard_map/qhgd,khd->hgqk/dot_general | solution.py:43
  166.2 4.4 fusion.6
  170.6 3.2 fusion.56
  173.9 4.5 %convolution_convert_fusion.1 = bf16[1024,2048]{1,0:T(8,128)(2,1)} fusion(bf16[1024,256]{0,1:T(8,128)(2,1)S(1)} %constant_dynamic-update-slice_fusion, bf16[256,2048]{1,0:T(8,128)(2,1)} %all-gather.8.cloned.1.call-done), kind=kOutput, calls=%fused_computation.53 | convolution fusion | flops 1075838976 | bytes 5767168 | tf_op jit(solution)/shard_map/dot_general | solution.py:110
  178.5 38.0 %reduce-scatter.3.cloned.1.call-done = bf16[128,2048]{1,0:T(8,128)(2,1)} async-done(((bf16[1024,2048]{1,0:T(8,128)(2,1)}), bf16[128,2048]{1,0:T(8,128)(2,1)}) %reduce-scatter.3.cloned.1.call-update) | async-done | bytes 524304 | tf_op jit(solution)/shard_map/reduce_scatter | solution.py:109
  220.9 3.6 all-to-all-start.3
  225.4 23.4 %all-to-all-done.3 = bf16[8,256,448]{1,2,0:T(8,128)(2,1)S(1)} async-done(((bf16[8,256,448]{1,2,0:T(8,128)(2,1)}), bf16[8,256,448]{1,2,0:T(8,128)(2,1)S(1)}, u32[]{:S(2)}, u32[]{:S(2)}) %all-to-all-start.3) | async-done | bytes 1835040 | tf_op jit(solution)/shard_map/all_to_all | solution.py:23
  250.3 38.3 %all-gather.10.cloned.1.call-done = bf16[2048,2048]{1,0:T(8,128)(2,1)} async-done(((bf16[128,2048]{1,0:T(8,128)(2,1)}), bf16[2048,2048]{1,0:T(8,128)(2,1)}) %all-gather.10.cloned.1.call-update) | async-done | bytes 8388624 | tf_op jit(solution)/shard_map/all_gather | solution.py:121
  288.5 9.7 %fusion.91 = f32[2048,448]{0,1:T(8,128)} fusion(bf16[2048,2048]{1,0:T(8,128)(2,1)} %all-gather.10.cloned.1.call-done, bf16[2048,448]{0,1:T(8,128)(2,1)} %bitcast.237), kind=kOutput, calls=%fused_computation.140 | convolution fusion | flops 3758096384 | bytes 13893632 | tf_op jit(solution)/shard_map/dot_general | solution.py:56
  298.2 17.6 %all-gather.12.cloned.1.call-done = bf16[2048,448]{0,1:T(8,128)(2,1)} async-done(((bf16[256,448]{0,1:T(8,128)(2,1)}), bf16[2048,448]{0,1:T(8,128)(2,1)}) %all-gather.12.cloned.1.call-update) | async-done | bytes 1835024 | tf_op jit(solution)/shard_map/all_gather | solution.py:127
  315.9 9.1 %multiply_convert_fusion = bf16[2048,448]{0,1:T(8,128)(2,1)S(1)} fusion(f32[2048,448]{0,1:T(8,128)} %fusion.91, bf16[2048,2048]{1,0:T(8,128)(2,1)} %all-gather.10.cloned.1.call-done, bf16[2048,448]{0,1:T(8,128)(2,1)} %all-gather.12.cloned.1.call-done), kind=kOutput, calls=%fused_computation.55 | convolution fusion | flops 3763601408 | bytes 15728640 | tf_op jit(solution)/shard_map/dot_general | solution.py:56
  325.0 19.3 %all-gather.14.cloned.1.call-done = bf16[448,2048]{1,0:T(8,128)(2,1)} async-done(((bf16[448,256]{1,0:T(8,128)(2,1)}), bf16[448,2048]{1,0:T(8,128)(2,1)}) %all-gather.14.cloned.1.call-update) | async-done | bytes 1835024 | tf_op jit(solution)/shard_map/all_gather | solution.py:129
  344.3 8.3 %convolution_convert_fusion = bf16[2048,2048]{1,0:T(8,128)(2,1)} fusion(bf16[2048,448]{0,1:T(8,128)(2,1)S(1)} %multiply_convert_fusion, bf16[448,2048]{1,0:T(8,128)(2,1)} %all-gather.14.cloned.1.call-done), kind=kOutput, calls=%fused_computation.34 | convolution fusion | flops 3762290688 | bytes 12058624 | tf_op jit(solution)/shard_map/dot_general | solution.py:132
  352.6 86.6 %reduce-scatter.5.cloned.1.call-done = bf16[128,2048]{1,0:T(8,128)(2,1)} async-done(((bf16[2048,2048]{1,0:T(8,128)(2,1)}), bf16[128,2048]{1,0:T(8,128)(2,1)}) %reduce-scatter.5.cloned.1.call-update) | async-done | bytes 524304 | tf_op jit(solution)/shard_map/reduce_scatter | solution.py:131
  (104 shorter events, 44.7 us)
Async XLA Ops:
  7.2 25.7 %copy-start.7 = (bf16[128,2048]{1,0:T(8,128)(2,1)S(1)}, bf16[128,2048]{1,0:T(8,128)(2,1)}, u32[]{:S(2)}) copy-start(bf16[128,2048]{1,0:T(8,128)(2,1)} %param.10) | copy-start | bytes 1572868
  9.2 12.9 %all-to-all-start.1 = ((bf16[128,8,128]{2,0,1:T(8,128)(2,1)}), bf16[128,8,128]{2,0,1:T(8,128)(2,1)S(1)}, u32[]{:S(2)}, u32[]{:S(2)}) async-start(bf16[128,8,128]{2,0,1:T(8,128)(2,1)} %copy.90), calls=%async_computation.1 | async-start | bytes 524288 | tf_op jit(solution)/shard_map/all_to_all | solution.py:70
  14.6 88.6 %all-gather.6.cloned.1.call-start = ((), (), s32[]{:S(2)}) async-start(), calls=%async_computation.6 | async-start | bytes 8912896 | tf_op jit(solution)/shard_map/all_gather | solution.py:14
  33.9 35.7 %all-to-all-start.2 = ((bf16[128,8,256]{0,2,1:T(8,128)(2,1)}), bf16[128,8,256]{0,2,1:T(8,128)(2,1)S(1)}, u32[]{:S(2)}, u32[]{:S(2)}) async-start(bf16[128,8,256]{0,2,1:T(8,128)(2,1)} %bitcast.8), calls=%async_computation.2 | async-start | bytes 1048576 | tf_op jit(solution)/shard_map/all_to_all | solution.py:67
  37.4 136.5 %all-gather.8.cloned.1.call-start = ((), (), s32[]{:S(2)}) async-start(), calls=%async_computation.7 | async-start | bytes 1114112 | tf_op jit(solution)/shard_map/all_gather | solution.py:107
  38.2 178.4 %reduce-scatter.3.cloned.1.call-start = ((), (), s32[]{:S(2)}) async-start(), calls=%async_computation.8 | async-start | bytes 4718592 | tf_op jit(solution)/shard_map/reduce_scatter | solution.py:109
  105.1 3.5 copy-start
  106.8 1.9 copy-start.15
  111.2 1.1 copy-start.6
  111.2 1.1 copy-start.14
  115.9 1.2 copy-start.5
  115.9 1.2 copy-start.13
  121.7 1.3 copy-start.4
  121.7 1.3 copy-start.12
  128.8 1.4 copy-start.3
  128.8 1.4 copy-start.11
  158.7 2.3 copy-start.2
  158.7 2.3 copy-start.10
  173.9 4.6 %copy-start.16 = (bf16[2048]{0:T(1024)(128)(2,1)S(1)}, bf16[2048]{0:T(1024)(128)(2,1)}, u32[]{:S(2)}) copy-start(bf16[2048]{0:T(1024)(128)(2,1)} %param.14) | copy-start | bytes 12292
  173.9 42.7 %copy-start.8 = (bf16[128,2048]{1,0:T(8,128)(2,1)S(1)}, bf16[128,2048]{1,0:T(8,128)(2,1)}, u32[]{:S(2)}) copy-start(bf16[128,2048]{1,0:T(8,128)(2,1)} %param.9) | copy-start | bytes 1572868
  178.4 41.1 %copy-start.9 = (bf16[256,448]{0,1:T(8,128)(2,1)S(1)}, bf16[256,448]{0,1:T(8,128)(2,1)}, u32[]{:S(2)}) copy-start(bf16[256,448]{0,1:T(8,128)(2,1)} %param.15) | copy-start | bytes 688132
  178.4 110.1 %all-gather.10.cloned.1.call-start = ((), (), s32[]{:S(2)}) async-start(), calls=%async_computation.9 | async-start | bytes 8912896 | tf_op jit(solution)/shard_map/all_gather | solution.py:121
  217.9 221.4 %copy-start.1 = (bf16[128,2048]{1,0:T(8,128)(2,1)}, bf16[128,2048]{1,0:T(8,128)(2,1)S(1)}, u32[]{:S(2)}) copy-start(bf16[128,2048]{1,0:T(8,128)(2,1)S(1)} %get-tuple-element.3) | copy-start | bytes 1572868
  218.9 97.0 %all-gather.12.cloned.1.call-start = ((), (), s32[]{:S(2)}) async-start(), calls=%async_computation.10 | async-start | bytes 2064384 | tf_op jit(solution)/shard_map/all_gather | solution.py:127
  220.9 27.9 %all-to-all-start.3 = ((bf16[8,256,448]{1,2,0:T(8,128)(2,1)}), bf16[8,256,448]{1,2,0:T(8,128)(2,1)S(1)}, u32[]{:S(2)}, u32[]{:S(2)}) async-start(bf16[8,256,448]{1,2,0:T(8,128)(2,1)} %broadcast_in_dim.157), calls=%async_computation.4 | async-start | bytes 3670016 | tf_op jit(solution)/shard_map/all_to_all | solution.py:23
  224.5 119.8 %all-gather.14.cloned.1.call-start = ((), (), s32[]{:S(2)}) async-start(), calls=%async_computation.11 | async-start | bytes 2064384 | tf_op jit(solution)/shard_map/all_gather | solution.py:129
  225.1 214.1 %reduce-scatter.5.cloned.1.call-start = ((), (), s32[]{:S(2)}) async-start(), calls=%async_computation.12 | async-start | bytes 8912896 | tf_op jit(solution)/shard_map/reduce_scatter | solution.py:131
Sparse Core Ops, SparseCore 0:
  33.0 70.1 all-gather.5
  105.3 42.6 all-gather.7
  178.6 37.9 reduce-scatter.2
  219.1 69.3 all-gather.9
  290.1 25.7 all-gather.11
  317.4 26.8 all-gather.13
  352.7 86.4 reduce-scatter.4
where the time goes:
time: 454 us; the launch traced here: 448 us
  waiting for transfers between devices  264 us (58%)
  matrix products  74.3 us (16%)
  other arithmetic  54.2 us (12%)
  local copies, waits for them, and re-layouts  17.9 us (4%)
  between operations  15.1 us (3%)
  starting transfers between devices  13 us (3%)
  blocking collectives  9.9 us (2%)
    reduce_scatter x1, waiting for transfers between devices, shards(): lax.psum_scatter(jnp.dot(block_rows, down_full, preferred_element_type=jn...  86.6 us
    all_gather x1, waiting for transfers between devices, shards(): all_rows = lax.all_gather(normed, 'tp', axis=0, tiled=True)  38.3 us
    reduce_scatter x1, waiting for transfers between devices, shards(): lax.psum_scatter(jnp.dot(block_rows, wo_full, preferred_element_type=jnp....  38 us
    all_gather x1, waiting for transfers between devices, side_by_side(): result, at, done = (lax.all_gather(both, axis, axis=dim, tiled=True), 0, [])  32.9 us
    le x8, other arithmetic, attend(): causal = key_pos[None, :] <= query_pos[:, None]  31.3 us
    all_to_all x1, waiting for transfers between devices, sent_to_all(): return lax.all_to_all(copies, axis, split_axis=0, concat_axis=0, tiled=True)  23.4 us
    dot_general x8, matrix products, attend(): jnp.einsum('qhgd,khd->hgqk', q_four, k_three, preferred_element_type=jnp....  22.5 us
    dot_general x8, matrix products, attend(): jnp.einsum('hgqk,khd->qhgd', probs, v_three, preferred_element_type=jnp.f...  20.2 us
  transfers between devices with their start and end apart: 10, of which 8 were waited for; matrix products, arithmetic and copies ran while one was open for 27% of the time, Pallas kernels for 0%

commit v1 on v0

v1 whole, which is shorter than its diff:
```python
import functools

import jax
import jax.numpy as jnp
import numpy as np
from jax import lax
from jax.experimental import pallas as pl
from jax.experimental.pallas import tpu as pltpu
from jax.sharding import Mesh
from jax.sharding import PartitionSpec as P

HEAD_DIM = 128
EPS = 1e-05
ROWS = 128
Z, C, X, Y = 4, 2, 4, 4
HEADS = Z * X
BLOCK = X * ROWS
LOCAL = Z * BLOCK
SCALE = float(HEAD_DIM**-0.5 * np.log2(np.e))
VMEM = 58 * 1024 * 1024
F32 = jnp.float32
BF16 = jnp.bfloat16


def params():
    return pltpu.CompilerParams(vmem_limit_bytes=VMEM)


def along_y(array, step):
    return lax.ppermute(array, "y", [(i, (i + step) % Y) for i in range(Y)])


def other_core(array):
    return lax.ppermute(array, "c", [(0, 1), (1, 0)])


def attend_body(first, last, n_pairs, where_ref, q_ref, *refs):
    kv_refs = refs[: 2 * n_pairs]
    refs = refs[2 * n_pairs :]
    if first:
        m_in = l_in = a_in = None
    else:
        m_in, l_in, a_in = refs[:3]
        refs = refs[3:]
    if last:
        (o_ref,) = refs[:1]
        kv_s, m_s, l_s, a_s = refs[1:]
    else:
        m_s, l_s, a_s = refs[:3]
        (kv_s,) = refs[3:]
    for i in range(2 * n_pairs):
        kv_s[i] = kv_refs[i][...]
    c_q = where_ref[0]
    y_q = where_ref[1]

    def scores(q, pair, zk, core):
        k = kv_s[2 * pair + core, pl.ds(zk * BLOCK, BLOCK), :HEAD_DIM]
        return lax.dot_general(q, k, (((1,), (1,)), ((), ())), preferred_element_type=F32) * SCALE

    def accumulate(rows, s_two, pair, zk):
        m_old = m_s[rows, :]
        peak = jnp.maximum(
            jnp.max(s_two[0], axis=1, keepdims=True), jnp.max(s_two[1], axis=1, keepdims=True)
        )
        m_new = jnp.maximum(m_old, jnp.broadcast_to(peak, m_old.shape))
        alpha = jnp.exp2(m_old - m_new)
        l_new = l_s[rows, :] * alpha
        a_new = a_s[rows, :] * alpha
        for core in range(2):
            p = jnp.exp2(s_two[core] - m_new[:, :1])
            for lane in range(BLOCK // 128):
                l_new = l_new + p[:, lane * 128 : (lane + 1) * 128]
            v = kv_s[2 * pair + core, pl.ds(zk * BLOCK, BLOCK), HEAD_DIM:]
            a_new = a_new + lax.dot_general(
                p.astype(BF16), v, (((1,), (0,)), ((), ())), preferred_element_type=F32
            )
        m_s[rows, :] = m_new
        l_s[rows, :] = l_new
        a_s[rows, :] = a_new

    q_row = lax.broadcasted_iota(jnp.int32, (BLOCK, BLOCK), 0)
    k_row = lax.broadcasted_iota(jnp.int32, (BLOCK, BLOCK), 1)
    ahead = (k_row // ROWS - q_row // ROWS) * (Y * ROWS) + (k_row % ROWS - q_row % ROWS)

    def per_z(zq, _):
        rows = pl.ds(zq * BLOCK, BLOCK)
        q = q_ref[rows, :]
        if first:
            m_s[rows, :] = jnp.full((BLOCK, 128), -1e30, F32)
            l_s[rows, :] = jnp.zeros((BLOCK, 128), F32)
            a_s[rows, :] = jnp.zeros((BLOCK, HEAD_DIM), F32)
        else:
            m_s[rows, :] = m_in[rows, :]
            l_s[rows, :] = l_in[rows, :]
            a_s[rows, :] = a_in[rows, :]

        def per_pair(pair, _):
            y_k = where_ref[2 + pair]
            s_two = []
            for core in range(2):
                cores = 0 if core == 0 else 1 - 2 * c_q
                gap = cores * (X * Y * ROWS) + (y_k - y_q) * ROWS
                s_two.append(jnp.where(ahead + gap <= 0, scores(q, pair, zq, core), -1e30))
            accumulate(rows, s_two, pair, zq)

            def per_key(zk, _):
                accumulate(rows, [scores(q, pair, zk, core) for core in range(2)], pair, zk)
                return 0

            lax.fori_loop(0, zq, per_key, 0)
            return 0

        lax.fori_loop(0, n_pairs, per_pair, 0)
        if last:
            total = jnp.sum(l_s[rows, :], axis=1, keepdims=True)
            o_ref[rows, :] = (a_s[rows, :] / total).astype(BF16)
        return 0

    lax.fori_loop(0, Z, per_z, 0)


def attend(where, q, chunks, state, last):
    n_pairs = len(chunks) // 2
    first = state is None
    wide = jax.ShapeDtypeStruct((LOCAL, 128), F32)
    vmem = pl.BlockSpec(memory_space=pltpu.VMEM)
    scratch = [pltpu.VMEM((2 * n_pairs, LOCAL, 2 * HEAD_DIM), BF16)]
    if last:
        out_shape = [jax.ShapeDtypeStruct((LOCAL, HEAD_DIM), BF16)]
        scratch = scratch + [pltpu.VMEM((LOCAL, 128), F32)] * 3
    else:
        out_shape = [wide] * 3
    args = [where, q, *chunks] + ([] if first else list(state))
    pairs = LOCAL * LOCAL * n_pairs * 5 // 4
    return pl.pallas_call(
        functools.partial(attend_body, first, last, n_pairs),
        out_shape=out_shape,
        in_specs=[pl.BlockSpec(memory_space=pltpu.SMEM)] + [vmem] * (len(args) - 1),
        out_specs=[vmem] * len(out_shape),
        scratch_shapes=scratch,
        compiler_params=params(),
        cost_estimate=pl.CostEstimate(
            flops=pairs * 4 * HEAD_DIM, transcendentals=pairs, bytes_accessed=n_pairs * 2 * LOCAL * 512
        ),
    )(*args)


def project_body(attn_ref, wo_ref, tokens_ref, gain_ref, attended_ref, normed_ref, wide_s):
    rows = jnp.concatenate([attn_ref[h] for h in range(HEADS)], axis=1)
    n_k, n_j = wo_ref.shape[0], wo_ref.shape[1]
    for j in range(0, n_j, 2):
        weight = jnp.concatenate(
            [jnp.concatenate([wo_ref[k, j], wo_ref[k, j + 1]], axis=1) for k in range(n_k)], axis=0
        )
        cols = slice(j * 128, (j + 2) * 128)
        share = jnp.dot(rows, weight, preferred_element_type=F32)
        kept = (tokens_ref[:, cols].astype(F32) + share).astype(BF16)
        attended_ref[:, cols] = kept
        wide_s[:, cols] = kept.astype(F32)
    wide = wide_s[...]
    inverse = lax.rsqrt(jnp.mean(wide * wide, axis=1, keepdims=True) + EPS)
    normed_ref[...] = (wide * inverse * gain_ref[...].astype(F32)).astype(BF16)


def project(attn, wo, tokens, gain):
    d = tokens.shape[1]
    vmem = pl.BlockSpec(memory_space=pltpu.VMEM)
    out = jax.ShapeDtypeStruct((ROWS, d), BF16)
    return pl.pallas_call(
        project_body,
        out_shape=[out, out],
        in_specs=[vmem] * 4,
        out_specs=[vmem] * 2,
        scratch_shapes=[pltpu.VMEM((ROWS, d), F32)],
        compiler_params=params(),
        cost_estimate=pl.CostEstimate(
            flops=2 * ROWS * d * d, transcendentals=0, bytes_accessed=2 * d * d
        ),
    )(attn, wo, tokens, gain)


def ffn_body(n_chunks, w_ref, *refs):
    x_refs = refs[:n_chunks]
    o_ref = refs[n_chunks]
    x_s = refs[n_chunks + 1]
    for i in range(n_chunks):
        x_s[i * ROWS : (i + 1) * ROWS, :] = x_refs[i][...]
    tile = 2 * ROWS
    half = w_ref.shape[3]

    def weight(kind, x):
        return jnp.concatenate(
            [w_ref[z * X + x, kind, c] for z in range(Z) for c in range(C)], axis=1
        )

    def per_tile(t, _):
        rows = x_s[pl.ds(t * tile, tile), :]
        acc = None
        for x in range(X):
            nt = (((1,), (1,)), ((), ()))
            gate = lax.dot_general(rows, weight(0, x), nt, preferred_element_type=F32)
            up = lax.dot_general(rows, weight(1, x), nt, preferred_element_type=F32)
            hidden = (gate / (1.0 + jnp.exp(-gate)) * up).astype(BF16)
            part = jnp.dot(hidden, weight(2, x), preferred_element_type=F32)
            acc = part if acc is None else acc + part
        o_ref[pl.ds(t * tile, tile), :] = acc.astype(BF16)
        return 0

    lax.fori_loop(0, n_chunks * ROWS // tile, per_tile, 0)


def ffn(w, chunks):
    d = chunks[0].shape[1]
    n = len(chunks)
    vmem = pl.BlockSpec(memory_space=pltpu.VMEM)
    return pl.pallas_call(
        functools.partial(ffn_body, n),
        out_shape=jax.ShapeDtypeStruct((n * ROWS, d), BF16),
        in_specs=[vmem] * (n + 1),
        out_specs=vmem,
        scratch_shapes=[pltpu.VMEM((n * ROWS, d), BF16)],
        compiler_params=params(),
        cost_estimate=pl.CostEstimate(
            flops=6 * n * ROWS * d * X * w.shape[3],
            transcendentals=n * ROWS * X * w.shape[3],
            bytes_accessed=2 * w.size,
        ),
    )(w, *chunks)


def gather_ring(own):
    half = own.shape[0] // 2
    before = along_y(own, 1)
    after = along_y(own, -1)
    own_c = other_core(own)
    top = along_y(before[:half], 1)
    bottom = along_y(after[half:], -1)
    before_c = other_core(before)
    after_c = other_core(after)
    far = jnp.concatenate([top, bottom], axis=0)
    far_c = other_core(far)
    return (own, own_c), (before, before_c), (after, after_c), (far, far_c)


def reduce_ring(mine, theirs):
    half = ROWS // 2
    got_far = other_core(theirs[3])
    got_near = other_core(theirs[1:3])
    got_own = other_core(theirs[0])

    def add(a, b):
        return a.astype(F32) + b.astype(F32)

    far = add(mine[3], got_far).astype(BF16)
    far_top = along_y(far[:half], 1)
    far_bottom = along_y(far[half:], -1)
    before = add(mine[1], got_near[0])
    after = add(mine[2], got_near[1])
    early_after = along_y(after[half:].astype(BF16), 1)
    early_before = along_y(before[:half].astype(BF16), -1)
    late_after = along_y(add(after[:half], far_top).astype(BF16), 1)
    late_before = along_y(add(before[half:], far_bottom).astype(BF16), -1)
    own = add(mine[0], got_own)
    return jnp.concatenate(
        [
            own[:half] + late_after.astype(F32) + early_before.astype(F32),
            own[half:] + early_after.astype(F32) + late_before.astype(F32),
        ],
        axis=0,
    )


def shards(
    tokens, queries, keys, values, out_weight, norm_gain, gate_weight, up_weight, down_weight
):
    d = tokens.shape[1]
    core = lax.axis_index("c")
    y = lax.axis_index("y")
    group = HEADS // (keys.shape[1] // HEAD_DIM)

    wo = lax.all_gather(out_weight, ("z", "c", "x", "y"), axis=0, tiled=True)
    wo = wo.reshape(Z * C, X * Y, out_weight.shape[0], out_weight.shape[1])

    packed = jnp.stack([gate_weight.T, up_weight.T, down_weight])
    packed = packed.reshape(3, 2, packed.shape[1] // 2, packed.shape[2])
    keep = lax.dynamic_index_in_dim(packed, core, 1, keepdims=False)
    send = lax.dynamic_index_in_dim(packed, 1 - core, 1, keepdims=False)
    got = other_core(send)
    both = jnp.stack([jnp.where(core == 0, keep, got), jnp.where(core == 0, got, keep)], axis=1)
    w = lax.all_gather(both.reshape(-1, both.shape[-1]), ("z", "x"), axis=0, tiled=True)
    w = w.reshape(Z * X, *both.shape)

    def by_head(array, times):
        out = array.reshape(ROWS, -1, 1, HEAD_DIM)
        return jnp.broadcast_to(out, (ROWS, out.shape[1], times, HEAD_DIM)).reshape(ROWS, HEADS, HEAD_DIM)

    kv = jnp.concatenate([by_head(keys, group), by_head(values, group)], axis=2)
    kv = lax.all_to_all(kv.transpose(1, 0, 2), ("z", "x"), split_axis=0, concat_axis=0, tiled=True)
    kv = kv.reshape(LOCAL, 2 * HEAD_DIM)
    q = by_head(queries, 1).transpose(1, 0, 2)
    q = lax.all_to_all(q, ("z", "x"), split_axis=0, concat_axis=0, tiled=True)
    q = q.reshape(LOCAL, HEAD_DIM)

    own, before, after, far = gather_ring(kv)

    def where(*steps):
        return jnp.stack([core, y] + [(y + s) % Y for s in steps]).astype(jnp.int32)

    state = attend(where(0), q, own, None, False)
    state = attend(where(-1, 1), q, before + after, state, False)
    (attn,) = attend(where(2), q, far, state, True)

    attn = lax.all_to_all(
        attn.reshape(HEADS, ROWS, HEAD_DIM), ("z", "x"), split_axis=0, concat_axis=0, tiled=True
    )
    attended, normed = project(attn, wo, tokens, norm_gain.reshape(1, d))

    rows = gather_ring(normed)
    partial = ffn(w, [pair[0] for pair in rows] + [pair[1] for pair in rows])
    partial = partial.reshape(2, 4, ROWS, d)
    layer_out = (attended.astype(F32) + reduce_ring(partial[0], partial[1])).astype(BF16)
    return attended, layer_out


def solution(mesh):
    grid = Mesh(mesh.devices.reshape(Z, C, X, Y), ("z", "c", "x", "y"))
    rows = P(("z", "c", "x", "y"), None)
    block = P(("z", "c"), ("x", "y"))
    return jax.shard_map(
        shards,
        mesh=grid,
        in_specs=(rows, rows, rows, rows, block, P(), block, block, P(("x", "y"), ("z", "c"))),
        out_specs=(rows, rows),
        check_vma=False,
    )
```

time: 454 us -> 294 us (0.65); the launches traced: 448 us -> 293 us
  waiting for transfers between devices: 264 us -> 85.2 us
  Pallas kernels: 0 us -> 113 us
  matrix products: 74.3 us -> 0 us
  other arithmetic: 54.2 us -> 6.2 us
  starting transfers between devices: 13 us -> 34.7 us
  blocking collectives: 9.9 us -> 25.9 us
    reduce_scatter x2 -> x0, waiting for transfers between devices: 125 us -> none  [the longest x1 86.6 us: shards(): lax.psum_scatter(jnp.dot(block_rows, down_full, preferred_element_type=jn...]
    pallas_call x0 -> x5, Pallas kernels: none -> 113 us  [the longest x3 84.4 us: attend(): pl.pallas_call(functools.partial(attend_body, first, last, n_pairs), out_...]
    all_gather x5 -> x2, waiting for transfers between devices: 108 us -> 0.01 us  [the longest x1 0.01 us: shards(): wo = lax.all_gather(out_weight, ('z', 'c', 'x', 'y'), axis=0, tiled=True)]
    dot_general x20 -> x0, matrix products: 74.3 us -> none  [the longest x8 22.5 us: attend(): jnp.einsum('qhgd,khd->hgqk', q_four, k_three, preferred_element_type=jnp....]
    ppermute x0 -> x26, waiting for transfers between devices: none -> 72.9 us  [the longest x14 68.2 us: along_y(): return lax.ppermute(array, 'y', [(i, (i + step) % Y) for i in range(Y)])]
    le x8 -> x0, other arithmetic: 31.3 us -> none  [attend(): causal = key_pos[None, :] <= query_pos[:, None]]
    ppermute x0 -> x26, starting transfers between devices: none -> 24.5 us  [the longest x14 22.5 us: along_y(): return lax.ppermute(array, 'y', [(i, (i + step) % Y) for i in range(Y)])]
    reduce_sum x9 -> x0, other arithmetic: 19.1 us -> none  [the longest x8 17.8 us: attend(): jnp.sum(exp_terms, axis=-1, keepdims=True)]
  transfers between devices with their start and end apart: 10 -> 30, of which waited for: 8 -> 14; matrix products, arithmetic and copies ran while one was open for 27% -> 4% of each run, Pallas kernels for 0% -> 31%
where the time goes in v1:
time: 294 us; the launch traced here: 293 us
  Pallas kernels  113 us (38%)
  waiting for transfers between devices  85.2 us (29%)
  starting transfers between devices  34.7 us (12%)
  blocking collectives  25.9 us (9%)
  between operations  14.5 us (5%)
  local copies, waits for them, and re-layouts  13.8 us (5%)
  other arithmetic  6.2 us (2%)
    pallas_call x3, Pallas kernels, attend(): pl.pallas_call(functools.partial(attend_body, first, last, n_pairs), out_...  84.4 us
    ppermute x14, waiting for transfers between devices, along_y(): return lax.ppermute(array, 'y', [(i, (i + step) % Y) for i in range(Y)])  68.2 us
    all_to_all x1, blocking collectives, shards(): lax.all_to_all(kv.transpose(1, 0, 2), ('z', 'x'), split_axis=0, concat_ax...  25.9 us
    pallas_call x1, Pallas kernels, ffn(): pl.pallas_call(functools.partial(ffn_body, n), out_shape=jax.ShapeDtypeSt...  22.6 us
    ppermute x14, starting transfers between devices, along_y(): return lax.ppermute(array, 'y', [(i, (i + step) % Y) for i in range(Y)])  22.5 us
    all_to_all x1, waiting for transfers between devices, shards(): lax.all_to_all(attn.reshape(HEADS, ROWS, HEAD_DIM), ('z', 'x'), split_axi...  11.6 us
    all_to_all x1, starting transfers between devices, shards(): lax.all_to_all(attn.reshape(HEADS, ROWS, HEAD_DIM), ('z', 'x'), split_axi...  6.48 us
    pallas_call x1, Pallas kernels, project(): pl.pallas_call(project_body, out_shape=[out, out], in_specs=[vmem] * 4, o...  5.92 us
  transfers between devices with their start and end apart: 30, of which 14 were waited for; matrix products, arithmetic and copies ran while one was open for 4% of the time, Pallas kernels for 31%

profile of v1, /device:TPU:0, one launch (start us, length us, event | category | flops | bytes accessed | tf_op | source)
XLA Modules:
  0.0 293.2 jit_solution(5442570209650484449)
XLA Ops:
  8.0 1.2 pad_maximum_fusion
  9.4 1.6 collective-permute-done.8
  12.5 25.9 %all_to_all.15 = bf16[16,128,256]{2,1,0:T(8,128)(2,1)S(1)} all-to-all(bf16[16,128,256]{2,1,0:T(8,128)(2,1)S(1)} %maximum_bitcast_fusion), channel_id=1, replica_groups=mesh['z'=4,'c'=2,'x'=4,'y'=4] {'z','x'}, dimensions={0} | all-to-all | bytes 2097152 | tf_op jit(solution)/shard_map/all_to_all | solution.py:298
  38.4 1.6 collective-permute-start
  40.0 1.6 collective-permute-start.2
  41.6 24.8 %collective-permute-done.refs_0_ = bf16[2048,256]{1,0:T(8,128)(2,1)} collective-permute-done((bf16[2048,256]{1,0:T(8,128)(2,1)S(1)}, bf16[2048,256]{1,0:T(8,128)(2,1)}, u32[]{:S(2)}, u32[]{:S(2)}) %collective-permute-start) | collective-permute-done | bytes 1048608 | tf_op jit(solution)/shard_map/ppermute | solution.py:30
  67.8 2.0 slice.108
  69.9 2.9 collective-permute-start.3
  74.2 3.7 %all-to-all-start = ((bf16[16,128,128]{2,1,0:T(8,128)(2,1)}), bf16[16,128,128]{2,1,0:T(8,128)(2,1)S(1)}, u32[]{:S(2)}, u32[]{:S(2)}) async-start(bf16[16,128,128]{2,1,0:T(8,128)(2,1)} %bitcast_bitcast_fusion), calls=%async_computation | async-start | bytes 1048576 | tf_op jit(solution)/shard_map/all_to_all | solution.py:301
  78.0 13.5 %collective-permute-done.1 = bf16[1024,256]{1,0:T(8,128)(2,1)S(1)} collective-permute-done((bf16[1024,256]{1,0:T(8,128)(2,1)S(1)}, bf16[1024,256]{1,0:T(8,128)(2,1)S(1)}, u32[]{:S(2)}, u32[]{:S(2)}) %collective-permute-start.1) | collective-permute-done | bytes 524320 | tf_op jit(solution)/shard_map/ppermute | solution.py:30
  96.2 21.3 %shard_map.104 = (f32[2048,128]{1,0:T(8,128)}, f32[2048,128]{1,0:T(8,128)}, f32[2048,128]{1,0:T(8,128)}) custom-call(s32[3]{0:T(128)} %pad_add_fusion.3.where_ref, bf16[2048,128]{1,0:T(8,128)(2,1)} %bitcast.75, bf16[2048,256]{1,0:T(8,128)(2,1)} %bitcast.73, bf16[2048,256]{1,0:T(8,128)(2,1)} %collective-permute-done.7.refs_1_), custom_call_target="tpu_custom_call" | custom-call | flops 2684354560 | bytes 2097152 | tf_op jit(solution)/shard_map/pallas_call | solution.py:135
  117.5 41.1 %shard_map.105 = (f32[2048,128]{1,0:T(8,128)}, f32[2048,128]{1,0:T(8,128)}, f32[2048,128]{1,0:T(8,128)}) custom-call(s32[4]{0:T(128)} %pad_add_fusion.2.where_ref, bf16[2048,128]{1,0:T(8,128)(2,1)} %bitcast.76, bf16[2048,256]{1,0:T(8,128)(2,1)} %collective-permute-done.refs_0_, bf16[2048,256]{1,0:T(8,128)(2,1)} %collective-permute-done.5.refs_1_, ...), custom_call_target="tpu_custom_call" | custom-call | flops 5368709120 | bytes 4194304 | tf_op jit(solution)/shard_map/pallas_call | solution.py:135
  159.6 22.0 %shard_map.106 = bf16[2048,128]{1,0:T(8,128)(2,1)} custom-call(s32[3]{0:T(128)} %pad_add_fusion.where_ref, bf16[2048,128]{1,0:T(8,128)(2,1)} %bitcast.77, bf16[2048,256]{1,0:T(8,128)(2,1)} %constant_dynamic-update-slice_fusion.refs_0_, bf16[2048,256]{1,0:T(8,128)(2,1)} %copy-done.13, f32[2048,128]{1,0:T(8,128)} %get-tuple-element.13.refs_2_, ...), custom_call_target="tpu_custom_call" | custom-call | flops 2684354560 | bytes 2097152 | tf_op jit(solution)/shard_map/pallas_call | solution.py:135
  181.6 6.5 %all-to-all-start.2 = ((bf16[16,128,128]{2,1,0:T(8,128)(2,1)}), bf16[16,128,128]{2,1,0:T(8,128)(2,1)S(1)}, u32[]{:S(2)}, u32[]{:S(2)}) async-start(bf16[16,128,128]{2,1,0:T(8,128)(2,1)} %bitcast.78), calls=%async_computation.2 | async-start | bytes 1048576 | tf_op jit(solution)/shard_map/all_to_all | solution.py:313
  188.7 11.6 %all-to-all-done.2.attn_ref = bf16[16,128,128]{2,1,0:T(8,128)(2,1)S(1)} async-done(((bf16[16,128,128]{2,1,0:T(8,128)(2,1)}), bf16[16,128,128]{2,1,0:T(8,128)(2,1)S(1)}, u32[]{:S(2)}, u32[]{:S(2)}) %all-to-all-start.2) | async-done | bytes 524320 | tf_op jit(solution)/shard_map/all_to_all | solution.py:313
  201.1 5.9 %shard_map.107 = (bf16[128,2048]{1,0:T(8,128)(2,1)}, bf16[128,2048]{1,0:T(8,128)(2,1)}) custom-call(bf16[16,128,128]{2,1,0:T(8,128)(2,1)} %copy-done.3, bf16[8,16,256,128]{3,2,1,0:T(8,128)(2,1)} %bitcast.66, bf16[128,2048]{1,0:T(8,128)(2,1)} %tokens_ref.1, bf16[1,2048]{1,0:T(2,128)(2,1)} %reshape.70.gain_ref), custom_call_target="tpu_custom_call" | custom-call | flops 1073741824 | bytes 8388608 | tf_op jit(solution)/shard_map/pallas_call | solution.py:169
  207.0 1.6 collective-permute-start.9
  208.6 1.7 collective-permute-start.10
  210.2 11.1 %collective-permute-done.9.refs_1_ = bf16[128,2048]{1,0:T(8,128)(2,1)S(1)} collective-permute-done((bf16[128,2048]{1,0:T(8,128)(2,1)}, bf16[128,2048]{1,0:T(8,128)(2,1)S(1)}, u32[]{:S(2)}, u32[]{:S(2)}) %collective-permute-start.9) | collective-permute-done | bytes 524320 | tf_op jit(solution)/shard_map/ppermute | solution.py:30
  221.7 3.0 %collective-permute-start.12 = (bf16[64,2048]{1,0:T(8,128)(2,1)S(1)}, bf16[64,2048]{1,0:T(8,128)(2,1)S(1)}, u32[]{:S(2)}, u32[]{:S(2)}) collective-permute-start(bf16[64,2048]{1,0:T(8,128)(2,1)S(1)} %slice.110), channel_id=1, source_target_pairs={{0,3},{1,0},{2,1},{3,2},{4,7},{5,4},{6,5},{7,6},{8,11},{9,8},{10,9... | collective-permute-start | bytes 786440 | tf_op jit(solution)/shard_map/ppermute | solution.py:30
  225.2 3.8 %collective-permute-done.11 = bf16[64,2048]{1,0:T(8,128)(2,1)S(1)} collective-permute-done((bf16[64,2048]{1,0:T(8,128)(2,1)S(1)}, bf16[64,2048]{1,0:T(8,128)(2,1)S(1)}, u32[]{:S(2)}, u32[]{:S(2)}) %collective-permute-start.11) | collective-permute-done | bytes 262176 | tf_op jit(solution)/shard_map/ppermute | solution.py:30
  231.8 22.6 %shard_map.108 = bf16[1024,2048]{1,0:T(8,128)(2,1)} custom-call(bf16[16,3,2,224,256]{4,3,2,1,0:T(8,128)(2,1)} %bitcast.82, bf16[128,2048]{1,0:T(8,128)(2,1)} %get-tuple-element.17.refs_0_, bf16[128,2048]{1,0:T(8,128)(2,1)} %copy-done.9, bf16[128,2048]{1,0:T(8,128)(2,1)} %copy-done.10, bf16[128,2048]{1,0:T(8,128)(2,1)} %copy-done.11, ...), custom_call_target="tpu_custom_call" | custom-call | flops 11274289152 | bytes 11010048 | tf_op jit(solution)/shard_map/pallas_call | solution.py:216
  254.5 1.4 slice.115
  256.1 1.3 fusion.7
  258.0 1.4 collective-permute-done.19
  261.7 2.8 collective-permute-start.22
  264.5 2.0 collective-permute-start.24
  266.6 4.9 %collective-permute-done.20 = bf16[64,2048]{1,0:T(8,128)(2,1)S(1)} collective-permute-done((bf16[64,2048]{1,0:T(8,128)(2,1)S(1)}, bf16[64,2048]{1,0:T(8,128)(2,1)S(1)}, u32[]{:S(2)}, u32[]{:S(2)}) %collective-permute-start.20) | collective-permute-done | bytes 262176 | tf_op jit(solution)/shard_map/ppermute | solution.py:30
  271.6 4.6 %collective-permute-done.24 = bf16[64,2048]{1,0:T(8,128)(2,1)S(1)} collective-permute-done((bf16[64,2048]{1,0:T(8,128)(2,1)S(1)}, bf16[64,2048]{1,0:T(8,128)(2,1)S(1)}, u32[]{:S(2)}, u32[]{:S(2)}) %collective-permute-start.24) | collective-permute-done | bytes 262176 | tf_op jit(solution)/shard_map/ppermute | solution.py:30
  276.2 3.8 %collective-permute-start.25 = (bf16[64,2048]{1,0:T(8,128)(2,1)S(1)}, bf16[64,2048]{1,0:T(8,128)(2,1)S(1)}, u32[]{:S(2)}, u32[]{:S(2)}) collective-permute-start(bf16[64,2048]{1,0:T(8,128)(2,1)S(1)} %fusion.1), channel_id=1, source_target_pairs={{0,3},{1,0},{2,1},{3,2},{4,7},{5,4},{6,5},{7,6},{8,11},{9,8},{10,9... | collective-permute-start | bytes 786440 | tf_op jit(solution)/shard_map/ppermute | solution.py:30
  280.0 2.4 collective-permute-done.21
  282.4 2.8 collective-permute-done.25
  (104 shorter events, 20.4 us)
Async XLA Ops:
  7.2 66.1 %copy-start = (bf16[128,2048]{1,0:T(8,128)(2,1)S(1)}, bf16[128,2048]{1,0:T(8,128)(2,1)}, u32[]{:S(2)}) copy-start(bf16[128,2048]{1,0:T(8,128)(2,1)} %param.10) | copy-start | bytes 1572868
  7.2 193.1 %all-gather.3.cloned.1.call-start = ((), (), s32[]{:S(2)}) async-start(), calls=%async_computation.3 | async-start | bytes 8454144 | tf_op jit(solution)/shard_map/all_gather | solution.py:281
  7.9 223.1 %all-gather.5.cloned.1.call-start = ((), (), s32[]{:S(2)}) async-start(), calls=%async_computation.4 | async-start | bytes 11698176 | tf_op jit(solution)/shard_map/all_gather | solution.py:290
  9.3 1.7 collective-permute-start.8
  38.3 57.0 %copy-start.4 = (bf16[16,128,256]{2,1,0:T(8,128)(2,1)}, bf16[16,128,256]{2,1,0:T(8,128)(2,1)S(1)}, u32[]{:S(2)}) copy-start(bf16[16,128,256]{2,1,0:T(8,128)(2,1)S(1)} %all_to_all.15) | copy-start | bytes 3145732
  38.4 28.0 %collective-permute-start = (bf16[2048,256]{1,0:T(8,128)(2,1)S(1)}, bf16[2048,256]{1,0:T(8,128)(2,1)}, u32[]{:S(2)}, u32[]{:S(2)}) collective-permute-start(bf16[2048,256]{1,0:T(8,128)(2,1)S(1)} %bitcast.70), channel_id=1, source_target_pairs={{0,1},{1,2},{2,3},{3,0},{4,5},{5,6},{6,7},{7,4},{8,9},{9,10},{10,1... | collective-permute-start | bytes 3145736 | tf_op jit(solution)/shard_map/ppermute | solution.py:30
  40.0 27.9 %collective-permute-start.2 = (bf16[2048,256]{1,0:T(8,128)(2,1)S(1)}, bf16[2048,256]{1,0:T(8,128)(2,1)}, u32[]{:S(2)}, u32[]{:S(2)}) collective-permute-start(bf16[2048,256]{1,0:T(8,128)(2,1)S(1)} %bitcast.71), channel_id=1, source_target_pairs={{0,3},{1,0},{2,1},{3,2},{4,7},{5,4},{6,5},{7,6},{8,11},{9,8},{10,9... | collective-permute-start | bytes 3145736 | tf_op jit(solution)/shard_map/ppermute | solution.py:30
  67.5 24.1 %collective-permute-start.1 = (bf16[1024,256]{1,0:T(8,128)(2,1)S(1)}, bf16[1024,256]{1,0:T(8,128)(2,1)S(1)}, u32[]{:S(2)}, u32[]{:S(2)}) collective-permute-start(bf16[1024,256]{1,0:T(8,128)(2,1)S(1)} %slice.107), channel_id=1, source_target_pairs={{0,1},{1,2},{2,3},{3,0},{4,5},{5,6},{6,7},{7,4},{8,9},{9,10},{10,1... | collective-permute-start | bytes 1572872 | tf_op jit(solution)/shard_map/ppermute | solution.py:30
  67.8 27.5 %collective-permute-start.7 = (bf16[2048,256]{1,0:T(8,128)(2,1)S(1)}, bf16[2048,256]{1,0:T(8,128)(2,1)}, u32[]{:S(2)}, u32[]{:S(2)}) collective-permute-start(bf16[2048,256]{1,0:T(8,128)(2,1)S(1)} %bitcast.72), channel_id=1, source_target_pairs={{0,16},{16,0},{1,17},{17,1},{2,18},{18,2},{3,19},{19,3},{4,20},{20... | collective-permute-start | bytes 3145736 | tf_op jit(solution)/shard_map/ppermute | solution.py:34
  69.9 22.8 %collective-permute-start.3 = (bf16[1024,256]{1,0:T(8,128)(2,1)}, bf16[1024,256]{1,0:T(8,128)(2,1)S(1)}, u32[]{:S(2)}, u32[]{:S(2)}) collective-permute-start(bf16[1024,256]{1,0:T(8,128)(2,1)} %slice.108), channel_id=1, source_target_pairs={{0,3},{1,0},{2,1},{3,2},{4,7},{5,4},{6,5},{7,6},{8,11},{9,8},{10,9... | collective-permute-start | bytes 1572872 | tf_op jit(solution)/shard_map/ppermute | solution.py:30
  72.8 44.7 %collective-permute-start.5 = (bf16[2048,256]{1,0:T(8,128)(2,1)}, bf16[2048,256]{1,0:T(8,128)(2,1)}, u32[]{:S(2)}, u32[]{:S(2)}) collective-permute-start(bf16[2048,256]{1,0:T(8,128)(2,1)} %collective-permute-done.refs_0_), channel_id=1, source_target_pairs={{0,16},{16,0},{1,17},{17,1},{2,18},{18,2},{3,19},{19,3},{4,20},{20... | collective-permute-start | bytes 3145736 | tf_op jit(solution)/shard_map/ppermute | solution.py:34
  73.0 44.5 %collective-permute-start.6 = (bf16[2048,256]{1,0:T(8,128)(2,1)}, bf16[2048,256]{1,0:T(8,128)(2,1)}, u32[]{:S(2)}, u32[]{:S(2)}) collective-permute-start(bf16[2048,256]{1,0:T(8,128)(2,1)} %collective-permute-done.2.refs_2_), channel_id=1, source_target_pairs={{0,16},{16,0},{1,17},{17,1},{2,18},{18,2},{3,19},{19,3},{4,20},{20... | collective-permute-start | bytes 3145736 | tf_op jit(solution)/shard_map/ppermute | solution.py:34
  74.2 21.1 %all-to-all-start = ((bf16[16,128,128]{2,1,0:T(8,128)(2,1)}), bf16[16,128,128]{2,1,0:T(8,128)(2,1)S(1)}, u32[]{:S(2)}, u32[]{:S(2)}) async-start(bf16[16,128,128]{2,1,0:T(8,128)(2,1)} %bitcast_bitcast_fusion), calls=%async_computation | async-start | bytes 1048576 | tf_op jit(solution)/shard_map/all_to_all | solution.py:301
  93.5 65.1 %collective-permute-start.4 = (bf16[2048,256]{1,0:T(8,128)(2,1)}, bf16[2048,256]{1,0:T(8,128)(2,1)S(1)}, u32[]{:S(2)}, u32[]{:S(2)}) collective-permute-start(bf16[2048,256]{1,0:T(8,128)(2,1)} %constant_dynamic-update-slice_fusion.refs_0_), channel_id=1, source_target_pairs={{0,16},{16,0},{1,17},{17,1},{2,18},{18,2},{3,19},{19,3},{4,20},{20... | collective-permute-start | bytes 3145736 | tf_op jit(solution)/shard_map/ppermute | solution.py:34
  181.6 18.7 %all-to-all-start.2 = ((bf16[16,128,128]{2,1,0:T(8,128)(2,1)}), bf16[16,128,128]{2,1,0:T(8,128)(2,1)S(1)}, u32[]{:S(2)}, u32[]{:S(2)}) async-start(bf16[16,128,128]{2,1,0:T(8,128)(2,1)} %bitcast.78), calls=%async_computation.2 | async-start | bytes 1048576 | tf_op jit(solution)/shard_map/all_to_all | solution.py:313
  207.0 14.3 %collective-permute-start.9 = (bf16[128,2048]{1,0:T(8,128)(2,1)}, bf16[128,2048]{1,0:T(8,128)(2,1)S(1)}, u32[]{:S(2)}, u32[]{:S(2)}) collective-permute-start(bf16[128,2048]{1,0:T(8,128)(2,1)} %get-tuple-element.17.refs_0_), channel_id=1, source_target_pairs={{0,1},{1,2},{2,3},{3,0},{4,5},{5,6},{6,7},{7,4},{8,9},{9,10},{10,1... | collective-permute-start | bytes 1572872 | tf_op jit(solution)/shard_map/ppermute | solution.py:30
  208.6 13.2 %collective-permute-start.10 = (bf16[128,2048]{1,0:T(8,128)(2,1)}, bf16[128,2048]{1,0:T(8,128)(2,1)S(1)}, u32[]{:S(2)}, u32[]{:S(2)}) collective-permute-start(bf16[128,2048]{1,0:T(8,128)(2,1)} %get-tuple-element.17.refs_0_), channel_id=1, source_target_pairs={{0,3},{1,0},{2,1},{3,2},{4,7},{5,4},{6,5},{7,6},{8,11},{9,8},{10,9... | collective-permute-start | bytes 1572872 | tf_op jit(solution)/shard_map/ppermute | solution.py:30
  221.3 7.7 %collective-permute-start.11 = (bf16[64,2048]{1,0:T(8,128)(2,1)S(1)}, bf16[64,2048]{1,0:T(8,128)(2,1)S(1)}, u32[]{:S(2)}, u32[]{:S(2)}) collective-permute-start(bf16[64,2048]{1,0:T(8,128)(2,1)S(1)} %slice.109), channel_id=1, source_target_pairs={{0,1},{1,2},{2,3},{3,0},{4,5},{5,6},{6,7},{7,4},{8,9},{9,10},{10,1... | collective-permute-start | bytes 786440 | tf_op jit(solution)/shard_map/ppermute | solution.py:30
  221.7 7.3 %collective-permute-start.12 = (bf16[64,2048]{1,0:T(8,128)(2,1)S(1)}, bf16[64,2048]{1,0:T(8,128)(2,1)S(1)}, u32[]{:S(2)}, u32[]{:S(2)}) collective-permute-start(bf16[64,2048]{1,0:T(8,128)(2,1)S(1)} %slice.110), channel_id=1, source_target_pairs={{0,3},{1,0},{2,1},{3,2},{4,7},{5,4},{6,5},{7,6},{8,11},{9,8},{10,9... | collective-permute-start | bytes 786440 | tf_op jit(solution)/shard_map/ppermute | solution.py:30
  224.7 4.4 %collective-permute-start.13 = (bf16[128,2048]{1,0:T(8,128)(2,1)}, bf16[128,2048]{1,0:T(8,128)(2,1)S(1)}, u32[]{:S(2)}, u32[]{:S(2)}) collective-permute-start(bf16[128,2048]{1,0:T(8,128)(2,1)} %get-tuple-element.17.refs_0_), channel_id=1, source_target_pairs={{0,16},{16,0},{1,17},{17,1},{2,18},{18,2},{3,19},{19,3},{4,20},{20... | collective-permute-start | bytes 1572872 | tf_op jit(solution)/shard_map/ppermute | solution.py:34
  224.7 4.5 %collective-permute-start.14 = (bf16[128,2048]{1,0:T(8,128)(2,1)S(1)}, bf16[128,2048]{1,0:T(8,128)(2,1)S(1)}, u32[]{:S(2)}, u32[]{:S(2)}) collective-permute-start(bf16[128,2048]{1,0:T(8,128)(2,1)S(1)} %collective-permute-done.9.refs_1_), channel_id=1, source_target_pairs={{0,16},{16,0},{1,17},{17,1},{2,18},{18,2},{3,19},{19,3},{4,20},{20... | collective-permute-start | bytes 1572872 | tf_op jit(solution)/shard_map/ppermute | solution.py:34
  225.2 4.0 %collective-permute-start.15 = (bf16[128,2048]{1,0:T(8,128)(2,1)S(1)}, bf16[128,2048]{1,0:T(8,128)(2,1)S(1)}, u32[]{:S(2)}, u32[]{:S(2)}) collective-permute-start(bf16[128,2048]{1,0:T(8,128)(2,1)S(1)} %collective-permute-done.10.refs_2_), channel_id=1, source_target_pairs={{0,16},{16,0},{1,17},{17,1},{2,18},{18,2},{3,19},{19,3},{4,20},{20... | collective-permute-start | bytes 1572872 | tf_op jit(solution)/shard_map/ppermute | solution.py:34
  229.1 2.0 collective-permute-start.16
  255.9 4.2 %collective-permute-start.18 = (bf16[2,128,2048]{2,1,0:T(8,128)(2,1)S(1)}, bf16[2,128,2048]{2,1,0:T(8,128)(2,1)S(1)}, u32[]{:S(2)}, u32[]{:S(2)}) collective-permute-start(bf16[2,128,2048]{2,1,0:T(8,128)(2,1)S(1)} %bitcast.74), channel_id=1, source_target_pairs={{0,16},{16,0},{1,17},{17,1},{2,18},{18,2},{3,19},{19,3},{4,20},{20... | collective-permute-start | bytes 3145736 | tf_op jit(solution)/shard_map/ppermute | solution.py:34
  257.4 2.0 collective-permute-start.19
  257.9 2.3 collective-permute-start.17
  261.0 10.5 %collective-permute-start.20 = (bf16[64,2048]{1,0:T(8,128)(2,1)S(1)}, bf16[64,2048]{1,0:T(8,128)(2,1)S(1)}, u32[]{:S(2)}, u32[]{:S(2)}) collective-permute-start(bf16[64,2048]{1,0:T(8,128)(2,1)S(1)} %get-tuple-element.28), channel_id=1, source_target_pairs={{0,1},{1,2},{2,3},{3,0},{4,5},{5,6},{6,7},{7,4},{8,9},{9,10},{10,1... | collective-permute-start | bytes 786440 | tf_op jit(solution)/shard_map/ppermute | solution.py:30
  261.7 18.3 %collective-permute-start.22 = (bf16[64,2048]{1,0:T(8,128)(2,1)S(1)}, bf16[64,2048]{1,0:T(8,128)(2,1)S(1)}, u32[]{:S(2)}, u32[]{:S(2)}) collective-permute-start(bf16[64,2048]{1,0:T(8,128)(2,1)S(1)} %slice.153), channel_id=1, source_target_pairs={{0,3},{1,0},{2,1},{3,2},{4,7},{5,4},{6,5},{7,6},{8,11},{9,8},{10,9... | collective-permute-start | bytes 786440 | tf_op jit(solution)/shard_map/ppermute | solution.py:30
  264.5 11.7 %collective-permute-start.24 = (bf16[64,2048]{1,0:T(8,128)(2,1)S(1)}, bf16[64,2048]{1,0:T(8,128)(2,1)S(1)}, u32[]{:S(2)}, u32[]{:S(2)}) collective-permute-start(bf16[64,2048]{1,0:T(8,128)(2,1)S(1)} %get-tuple-element.29), channel_id=1, source_target_pairs={{0,3},{1,0},{2,1},{3,2},{4,7},{5,4},{6,5},{7,6},{8,11},{9,8},{10,9... | collective-permute-start | bytes 786440 | tf_op jit(solution)/shard_map/ppermute | solution.py:30
  266.5 13.5 %collective-permute-start.23 = (bf16[64,2048]{1,0:T(8,128)(2,1)S(1)}, bf16[64,2048]{1,0:T(8,128)(2,1)S(1)}, u32[]{:S(2)}, u32[]{:S(2)}) collective-permute-start(bf16[64,2048]{1,0:T(8,128)(2,1)S(1)} %slice.152), channel_id=1, source_target_pairs={{0,1},{1,2},{2,3},{3,0},{4,5},{5,6},{6,7},{7,4},{8,9},{9,10},{10,1... | collective-permute-start | bytes 786440 | tf_op jit(solution)/shard_map/ppermute | solution.py:30
  271.5 10.9 %collective-permute-start.21 = (bf16[64,2048]{1,0:T(8,128)(2,1)S(1)}, bf16[64,2048]{1,0:T(8,128)(2,1)S(1)}, u32[]{:S(2)}, u32[]{:S(2)}) collective-permute-start(bf16[64,2048]{1,0:T(8,128)(2,1)S(1)} %fusion.3), channel_id=1, source_target_pairs={{0,1},{1,2},{2,3},{3,0},{4,5},{5,6},{6,7},{7,4},{8,9},{9,10},{10,1... | collective-permute-start | bytes 786440 | tf_op jit(solution)/shard_map/ppermute | solution.py:30
  276.2 9.0 %collective-permute-start.25 = (bf16[64,2048]{1,0:T(8,128)(2,1)S(1)}, bf16[64,2048]{1,0:T(8,128)(2,1)S(1)}, u32[]{:S(2)}, u32[]{:S(2)}) collective-permute-start(bf16[64,2048]{1,0:T(8,128)(2,1)S(1)} %fusion.1), channel_id=1, source_target_pairs={{0,3},{1,0},{2,1},{3,2},{4,7},{5,4},{6,5},{7,6},{8,11},{9,8},{10,9... | collective-permute-start | bytes 786440 | tf_op jit(solution)/shard_map/ppermute | solution.py:30
  (16 other events, 122.4 us)
Sparse Core Ops, SparseCore 0:
  11.2 81.8 all-gather.2
  95.1 84.6 all-gather.4

commit v2 on v1

v2 whole, which is shorter than its diff:
```python
import functools

import jax
import jax.numpy as jnp
import numpy as np
from jax import lax
from jax.experimental import pallas as pl
from jax.experimental.pallas import tpu as pltpu
from jax.sharding import Mesh
from jax.sharding import PartitionSpec as P


HEAD_DIM = 128
EPS = 1e-05
ROWS = 128
Z, C, X, Y = 4, 2, 4, 4
HEADS = Z * X
BLOCK = X * ROWS
LOCAL = Z * BLOCK
GROUP = 32
SCALE = float(HEAD_DIM**-0.5 * np.log2(np.e))
F32 = jnp.float32
BF16 = jnp.bfloat16


def params(mib):
    return pltpu.CompilerParams(vmem_limit_bytes=mib * 1024 * 1024)


def along(array, axis, step):
    return lax.ppermute(array, axis, [(i, (i + step) % 4) for i in range(4)])


def along_y(array, step):
    return along(array, "y", step)


def other_core(array):
    return lax.ppermute(array, "c", [(0, 1), (1, 0)])


def attend_body(first, last, n_pairs, where_ref, q_ref, *refs):
    kv_refs = refs[: 2 * n_pairs]
    refs = refs[2 * n_pairs :]
    given = () if first else refs[:3]
    refs = refs[len(given) :]
    if last:
        o_ref, *refs = refs
        kept = ()
    else:
        kept = refs[:3]
        refs = refs[3:]
    m_s, l_s, a_s, arrived, left = refs
    held = (m_s, l_s, a_s)

    def rows_of(zq):
        return pl.ds(pl.multiple_of(zq * BLOCK, BLOCK), BLOCK)

    def arriving(i, zq):
        rows = rows_of(zq)
        return pltpu.make_async_copy(given[i].at[rows], held[i].at[rows], arrived.at[i, zq])

    def leaving(i, zq):
        rows = rows_of(zq)
        return pltpu.make_async_copy(held[i].at[rows], kept[i].at[rows], left.at[i, zq])

    for zq in range(Z):
        for i in range(len(given)):
            arriving(i, zq).start()
    c_q = where_ref[0]
    y_q = where_ref[1]
    lanes = BLOCK // 128

    def accumulate(zq, zk):
        start = pl.multiple_of(zq * BLOCK, BLOCK)
        keys = pl.ds(pl.multiple_of(zk * BLOCK, BLOCK), BLOCK)
        q = q_ref[pl.ds(start, BLOCK), :]
        scores = [
            lax.dot_general(
                q, kv_refs[i][keys, :HEAD_DIM], (((1,), (1,)), ((), ())), preferred_element_type=F32
            )
            for i in range(2 * n_pairs)
        ]
        ahead = lax.broadcasted_iota(jnp.int32, (GROUP, 128), 1) - lax.broadcasted_iota(
            jnp.int32, (GROUP, 128), 0
        )
        probs = [[] for _ in range(2 * n_pairs)]
        for low in range(0, BLOCK, GROUP):
            rows = pl.ds(start + low, GROUP)
            tiles = []
            for i in range(2 * n_pairs):
                for lane in range(lanes):
                    tile = scores[i][low : low + GROUP, lane * 128 : (lane + 1) * 128] * SCALE
                    cores = C * (zk - zq) + (0 if i % 2 == 0 else 1 - 2 * c_q)
                    gap = cores * (X * Y * ROWS) + (where_ref[2 + i // 2] - y_q) * ROWS
                    gap = gap + (lane - low // ROWS) * (Y * ROWS) - low % ROWS
                    tiles.append(jnp.where(ahead <= -gap, tile, -1e30))
            m_old = m_s[rows, :]
            peak = jnp.max(functools.reduce(jnp.maximum, tiles), axis=1, keepdims=True)
            m_new = jnp.maximum(m_old, jnp.broadcast_to(peak, m_old.shape))
            alpha = jnp.exp2(m_old - m_new)
            terms = [jnp.exp2(tile - m_new) for tile in tiles]
            m_s[rows, :] = m_new
            l_s[rows, :] = l_s[rows, :] * alpha + functools.reduce(jnp.add, terms)
            a_s[rows, :] = a_s[rows, :] * alpha
            for i in range(2 * n_pairs):
                mine = [t.astype(BF16) for t in terms[i * lanes : (i + 1) * lanes]]
                probs[i].append(jnp.concatenate(mine, axis=1))
        mixed = None
        for i in range(2 * n_pairs):
            p = jnp.concatenate(probs[i], axis=0)
            part = jnp.dot(p, kv_refs[i][keys, HEAD_DIM:], preferred_element_type=F32)
            mixed = part if mixed is None else mixed + part
        a_s[pl.ds(start, BLOCK), :] = a_s[pl.ds(start, BLOCK), :] + mixed

    def per_z(zq, _):
        rows = pl.ds(pl.multiple_of(zq * BLOCK, BLOCK), BLOCK)
        if first:
            m_s[rows, :] = jnp.full((BLOCK, 128), -1e30, F32)
            l_s[rows, :] = jnp.zeros((BLOCK, 128), F32)
            a_s[rows, :] = jnp.zeros((BLOCK, HEAD_DIM), F32)
        else:
            for i in range(3):
                arriving(i, zq).wait()

        def per_key(zk, _):
            accumulate(zq, zk)
            return 0

        lax.fori_loop(0, zq + 1, per_key, 0)
        if last:
            total = jnp.sum(l_s[rows, :], axis=1, keepdims=True)
            o_ref[rows, :] = (a_s[rows, :] / total).astype(BF16)
        for i in range(len(kept)):
            leaving(i, zq).start()
        return 0

    lax.fori_loop(0, Z, per_z, 0)
    for zq in range(Z):
        for i in range(len(kept)):
            leaving(i, zq).wait()


def attend(where, q, chunks, state, last):
    n_pairs = len(chunks) // 2
    first = state is None
    wide = pltpu.HBM((LOCAL, 128), F32)
    vmem = pl.BlockSpec(memory_space=pltpu.VMEM)
    hbm = pl.BlockSpec(memory_space=pltpu.HBM)
    args = [where, q, *chunks]
    if not first:
        args += [pltpu.with_memory_space_constraint(a, pltpu.HBM) for a in state]
    n_vmem = 1 + len(chunks)
    pairs = LOCAL * LOCAL * n_pairs * 5 // 4
    return pl.pallas_call(
        functools.partial(attend_body, first, last, n_pairs),
        out_shape=jax.ShapeDtypeStruct((LOCAL, HEAD_DIM), BF16) if last else [wide] * 3,
        in_specs=[pl.BlockSpec(memory_space=pltpu.SMEM)]
        + [vmem] * n_vmem
        + [hbm] * (len(args) - 1 - n_vmem),
        out_specs=vmem if last else [hbm] * 3,
        scratch_shapes=[pltpu.VMEM((LOCAL, 128), F32)] * 3
        + [pltpu.SemaphoreType.DMA((3, Z))] * 2,
        compiler_params=params(22),
        cost_estimate=pl.CostEstimate(
            flops=pairs * 4 * HEAD_DIM, transcendentals=pairs, bytes_accessed=n_pairs * 2 * LOCAL * 512
        ),
    )(*args)


def project_body(where_ref, attn_ref, tokens_ref, gain_ref, *refs):
    wo_refs = refs[:8]
    attended_ref, normed_ref, wide_s = refs[8:]
    core, z_own, x_own = where_ref[0], where_ref[1], where_ref[2]
    heads = []
    for c in (core, 1 - core):
        for z in range(Z):
            for e in range(2):
                heads.append(attn_ref[2 * (2 * ((z_own - z) % Z) + c) + e])
    rows = jnp.concatenate(heads, axis=1)
    for i in range(Y):
        y = where_ref[3 + i]
        for x in range(0, X, 2):
            weight = jnp.concatenate(
                [
                    jnp.concatenate([ref[z * X + x], ref[z * X + x + 1]], axis=1)
                    for ref in wo_refs[2 * i : 2 * i + 2]
                    for z in range(Z)
                ],
                axis=0,
            )
            share = jnp.dot(rows, weight, preferred_element_type=F32)
            for side in range(2):
                column = (x_own - x - side) % X * Y + y
                cols = pl.ds(pl.multiple_of(column * 128, 128), 128)
                part = share[:, side * 128 : (side + 1) * 128]
                kept = (tokens_ref[:, cols].astype(F32) + part).astype(BF16)
                attended_ref[:, cols] = kept
                wide_s[:, cols] = kept.astype(F32)
    wide = wide_s[...]
    inverse = lax.rsqrt(jnp.mean(wide * wide, axis=1, keepdims=True) + EPS)
    normed_ref[...] = (wide * inverse * gain_ref[...].astype(F32)).astype(BF16)


def project(where, attn, wo, tokens, gain):
    d = tokens.shape[1]
    vmem = pl.BlockSpec(memory_space=pltpu.VMEM)
    out = jax.ShapeDtypeStruct((ROWS, d), BF16)
    return pl.pallas_call(
        project_body,
        out_shape=[out, out],
        in_specs=[pl.BlockSpec(memory_space=pltpu.SMEM)] + [vmem] * (3 + len(wo)),
        out_specs=[vmem] * 2,
        scratch_shapes=[pltpu.VMEM((ROWS, d), F32)],
        compiler_params=params(14),
        cost_estimate=pl.CostEstimate(
            flops=2 * ROWS * d * d, transcendentals=0, bytes_accessed=2 * d * d
        ),
    )(where, attn, tokens, gain, *wo)


def ffn_body(n_chunks, w_ref, *refs):
    x_refs = refs[:n_chunks]
    o_ref = refs[n_chunks]
    x_s = refs[n_chunks + 1]
    for i in range(n_chunks):
        x_s[i * ROWS : (i + 1) * ROWS, :] = x_refs[i][...]
    tile = 2 * ROWS

    def weight(kind, x):
        return jnp.concatenate(
            [w_ref[z * X + x, kind, c] for z in range(Z) for c in range(C)], axis=1
        )

    def per_tile(t, _):
        rows = x_s[pl.ds(pl.multiple_of(t * tile, tile), tile), :]
        acc = None
        for x in range(X):
            nt = (((1,), (1,)), ((), ()))
            gate = lax.dot_general(rows, weight(0, x), nt, preferred_element_type=F32)
            up = lax.dot_general(rows, weight(1, x), nt, preferred_element_type=F32)
            hidden = (gate / (1.0 + jnp.exp(-gate)) * up).astype(BF16)
            part = jnp.dot(hidden, weight(2, x), preferred_element_type=F32)
            acc = part if acc is None else acc + part
        o_ref[pl.ds(pl.multiple_of(t * tile, tile), tile), :] = acc.astype(BF16)
        return 0

    lax.fori_loop(0, n_chunks * ROWS // tile, per_tile, 0)


def ffn(w, chunks):
    d = chunks[0].shape[1]
    n = len(chunks)
    vmem = pl.BlockSpec(memory_space=pltpu.VMEM)
    return pl.pallas_call(
        functools.partial(ffn_body, n),
        out_shape=jax.ShapeDtypeStruct((n * ROWS, d), BF16),
        in_specs=[vmem] * (n + 1),
        out_specs=vmem,
        scratch_shapes=[pltpu.VMEM((n * ROWS, d), BF16)],
        compiler_params=params(26),
        cost_estimate=pl.CostEstimate(
            flops=6 * n * ROWS * d * X * w.shape[3],
            transcendentals=n * ROWS * X * w.shape[3],
            bytes_accessed=2 * w.size,
        ),
    )(w, *chunks)


def gather_near(own):
    before = along_y(own, 1)
    after = along_y(own, -1)
    return other_core(own), (before, other_core(before)), (after, other_core(after))


def gather_far(before, after):
    half = before.shape[0] // 2
    top = along_y(before[:half], 1)
    bottom = along_y(after[half:], -1)
    far = jnp.concatenate([top, bottom], axis=0)
    return far, other_core(far)


def wide_add(a, b):
    return a.astype(F32) + b.astype(F32)


def shards(
    tokens, queries, keys, values, out_weight, norm_gain, gate_weight, up_weight, down_weight
):
    d = tokens.shape[1]
    core = lax.axis_index("c")
    y = lax.axis_index("y")
    group = HEADS // (keys.shape[1] // HEAD_DIM)

    def by_head(array, times):
        out = array.reshape(ROWS, -1, 1, HEAD_DIM)
        out = jnp.broadcast_to(out, (ROWS, out.shape[1], times, HEAD_DIM))
        return out.reshape(ROWS, HEADS, HEAD_DIM)

    def regroup(array):
        return lax.all_to_all(array, ("z", "x"), split_axis=0, concat_axis=0, tiled=True)

    kv = jnp.concatenate([by_head(keys, group), by_head(values, group)], axis=2)
    kv = regroup(kv.transpose(1, 0, 2)).reshape(LOCAL, 2 * HEAD_DIM)
    kv_c, before, after = gather_near(kv)

    wo = jnp.stack([out_weight] + [along(out_weight, "x", i) for i in range(1, X)])
    wo = lax.optimization_barrier(wo)
    wo = jnp.stack([wo] + [along(wo, "z", i) for i in range(1, Z)])
    wo = wo.reshape(Z * X, *out_weight.shape)

    q = regroup(by_head(queries, 1).transpose(1, 0, 2)).reshape(LOCAL, HEAD_DIM)

    packed = jnp.stack([gate_weight.T, up_weight.T, down_weight])
    packed = packed.reshape(3, 2, packed.shape[1] // 2, packed.shape[2])
    keep = lax.dynamic_index_in_dim(packed, core, 1, keepdims=False)
    send = lax.dynamic_index_in_dim(packed, 1 - core, 1, keepdims=False)
    got = other_core(send)
    both = jnp.stack([jnp.where(core == 0, keep, got), jnp.where(core == 0, got, keep)], axis=1)
    w = lax.all_gather(both.reshape(-1, both.shape[-1]), ("z", "x"), axis=0, tiled=True)
    w = w.reshape(Z * X, *both.shape)

    def where(*steps):
        return jnp.stack([core, y] + [(y + s) % Y for s in steps]).astype(jnp.int32)

    state = attend(where(0), q, [kv, kv_c], None, False)
    far = gather_far(before[0], after[0])
    state = attend(where(-1, 1), q, [*before, *after], state, False)
    attn = attend(where(2), q, far, state, True)

    wo_c, wo_before, wo_after = gather_near(wo)
    wo_far = gather_far(wo_before[0], wo_after[0])
    attn = regroup(attn.reshape(HEADS, ROWS, HEAD_DIM))
    attn, w = lax.optimization_barrier((attn, w))
    attended, normed = project(
        jnp.stack(
            [core, lax.axis_index("z"), lax.axis_index("x")]
            + [(y + s) % Y for s in (0, -1, 1, 2)]
        ).astype(jnp.int32),
        attn,
        [wo, wo_c, *wo_before, *wo_after, *wo_far],
        tokens,
        norm_gain.reshape(1, d),
    )

    normed_c, before, after = gather_near(normed)
    own_part = ffn(w, [normed, normed_c])
    far = gather_far(before[0], after[0])
    near_part = ffn(w, [before[0], after[0], before[1], after[1]])
    far_part = ffn(w, far)

    half = ROWS // 2
    got_own = other_core(own_part[ROWS:])
    got_near = other_core(near_part[2 * ROWS :])
    before = wide_add(near_part[:ROWS], got_near[:ROWS])
    after = wide_add(near_part[ROWS : 2 * ROWS], got_near[ROWS:])
    early_after = along_y(after[half:].astype(BF16), 1)
    early_before = along_y(before[:half].astype(BF16), -1)
    far = wide_add(far_part[:ROWS], other_core(far_part[ROWS:])).astype(BF16)
    far_top = along_y(far[:half], 1)
    far_bottom = along_y(far[half:], -1)
    far_top, far_bottom = lax.optimization_barrier((far_top, far_bottom))
    late_after = along_y(wide_add(after[:half], far_top).astype(BF16), 1)
    late_before = along_y(wide_add(before[half:], far_bottom).astype(BF16), -1)
    own = wide_add(own_part[:ROWS], got_own)
    total = jnp.concatenate(
        [
            own[:half] + wide_add(late_after, early_before),
            own[half:] + wide_add(early_after, late_before),
        ],
        axis=0,
    )
    return attended, (attended.astype(F32) + total).astype(BF16)


def solution(mesh):
    grid = Mesh(mesh.devices.reshape(Z, C, X, Y), ("z", "c", "x", "y"))
    rows = P(("z", "c", "x", "y"), None)
    block = P(("z", "c"), ("x", "y"))
    return jax.shard_map(
        shards,
        mesh=grid,
        in_specs=(rows, rows, rows, rows, block, P(), block, block, P(("x", "y"), ("z", "c"))),
        out_specs=(rows, rows),
        check_vma=False,
    )
```

time: 294 us -> 277 us (0.942)
  Pallas kernels: 113 us -> 65.8 us
  waiting for transfers between devices: 85.2 us -> 114 us
  starting transfers between devices: 34.7 us -> 61.2 us
  blocking collectives: 25.9 us -> 0 us
    pallas_call x3, Pallas kernels: 84.4 us -> 45.4 us  [attend(): pl.pallas_call(functools.partial(attend_body, first, last, n_pairs), out_...]
    ppermute x14 -> x24, waiting for transfers between devices: 68.2 us -> 99.8 us  [along(): return lax.ppermute(array, axis, [(i, (i + step) % 4) for i in range(4)])]
    all_to_all x1 -> x0, blocking collectives: 25.9 us -> none  [shards(): lax.all_to_all(kv.transpose(1, 0, 2), ('z', 'x'), split_axis=0, concat_ax...]
    ppermute x14 -> x24, starting transfers between devices: 22.5 us -> 42.5 us  [along(): return lax.ppermute(array, axis, [(i, (i + step) % 4) for i in range(4)])]
    pallas_call x1 -> x3, Pallas kernels: 22.6 us -> 15.1 us  [ffn(): pl.pallas_call(functools.partial(ffn_body, n), out_shape=jax.ShapeDtypeSt...]
    all_to_all x2 -> x3, starting transfers between devices: 10.2 us -> 15.2 us  [regroup(): lax.all_to_all(array, ('z', 'x'), split_axis=0, concat_axis=0, tiled=True)]
    slice x9 -> x12, local copies, waits for them, and re-layouts: 5.96 us -> 4.87 us  [the longest x3 2.79 us: gather_far(): bottom = along_y(after[half:], -1)]
    all_to_all x2 -> x3, waiting for transfers between devices: 11.6 us -> 12.1 us  [regroup(): lax.all_to_all(array, ('z', 'x'), split_axis=0, concat_axis=0, tiled=True)]
  transfers between devices with their start and end apart: 30 -> 44, of which waited for: 14 -> 19; matrix products, arithmetic and copies ran while one was open for 4% -> 6% of each run, Pallas kernels for 31% -> 22%
where the time goes in v2:
time: 277 us; the launch traced here: 276 us
  waiting for transfers between devices  114 us (41%)
  Pallas kernels  65.8 us (24%)
  starting transfers between devices  61.2 us (22%)
  local copies, waits for them, and re-layouts  14.6 us (5%)
  between operations  14.6 us (5%)
  other arithmetic  5.61 us (2%)
    ppermute x24, waiting for transfers between devices, along(): return lax.ppermute(array, axis, [(i, (i + step) % 4) for i in range(4)])  99.8 us
    pallas_call x3, Pallas kernels, attend(): pl.pallas_call(functools.partial(attend_body, first, last, n_pairs), out_...  45.4 us
    ppermute x24, starting transfers between devices, along(): return lax.ppermute(array, axis, [(i, (i + step) % 4) for i in range(4)])  42.5 us
    all_to_all x3, starting transfers between devices, regroup(): lax.all_to_all(array, ('z', 'x'), split_axis=0, concat_axis=0, tiled=True)  15.2 us
    pallas_call x3, Pallas kernels, ffn(): pl.pallas_call(functools.partial(ffn_body, n), out_shape=jax.ShapeDtypeSt...  15.1 us
    all_to_all x3, waiting for transfers between devices, regroup(): lax.all_to_all(array, ('z', 'x'), split_axis=0, concat_axis=0, tiled=True)  12.1 us
  transfers between devices with their start and end apart: 44, of which 19 were waited for; matrix products, arithmetic and copies ran while one was open for 6% of the time, Pallas kernels for 22%

profile of v2, /device:TPU:0, one launch (start us, length us, event | category | flops | bytes accessed | tf_op | source)
XLA Modules:
  0.0 276.3 jit_solution(18416833080030072393)
XLA Ops:
  12.8 8.0 %all-to-all-start.1 = ((bf16[16,128,256]{2,1,0:T(8,128)(2,1)}), bf16[16,128,256]{2,1,0:T(8,128)(2,1)}, u32[]{:S(2)}, u32[]{:S(2)}) async-start(bf16[16,128,256]{2,1,0:T(8,128)(2,1)} %maximum_bitcast_fusion), calls=%async_computation.1 | async-start | bytes 2097152 | tf_op jit(solution)/shard_map/all_to_all | solution.py:302
  22.8 2.7 collective-permute-start.10
  27.0 17.9 %collective-permute-done.9 = bf16[256,128]{1,0:T(8,128)(2,1)S(1)} collective-permute-done((bf16[256,128]{1,0:T(8,128)(2,1)S(1)}, bf16[256,128]{1,0:T(8,128)(2,1)S(1)}, u32[]{:S(2)}, u32[]{:S(2)}) %collective-permute-start.9) | collective-permute-done | bytes 65568 | tf_op jit(solution)/shard_map/ppermute | solution.py:31
  44.9 3.5 %collective-permute-done.10 = bf16[256,128]{1,0:T(8,128)(2,1)S(1)} collective-permute-done((bf16[256,128]{1,0:T(8,128)(2,1)S(1)}, bf16[256,128]{1,0:T(8,128)(2,1)S(1)}, u32[]{:S(2)}, u32[]{:S(2)}) %collective-permute-start.10) | collective-permute-done | bytes 65568 | tf_op jit(solution)/shard_map/ppermute | solution.py:31
  48.5 3.1 %collective-permute-start.12 = (bf16[4,256,128]{2,1,0:T(8,128)(2,1)S(1)}, bf16[4,256,128]{2,1,0:T(8,128)(2,1)S(1)}, u32[]{:S(2)}, u32[]{:S(2)}) collective-permute-start(bf16[4,256,128]{2,1,0:T(8,128)(2,1)S(1)} %pad_maximum_fusion.3), channel_id=1, source_target_pairs={{0,32},{32,64},{64,96},{96,0},{1,33},{33,65},{65,97},{97,1},{2,34}... | collective-permute-start | bytes 786440 | tf_op jit(solution)/shard_map/ppermute | solution.py:31
  59.8 5.6 %collective-permute-done.13 = bf16[4,256,128]{2,1,0:T(8,128)(2,1)S(1)} collective-permute-done((bf16[4,256,128]{2,1,0:T(8,128)(2,1)S(1)}, bf16[4,256,128]{2,1,0:T(8,128)(2,1)S(1)}, u32[]{:S(2)}, u32[]{:S(2)}) %collective-permute-start.13) | collective-permute-done | bytes 262176 | tf_op jit(solution)/shard_map/ppermute | solution.py:31
  71.1 12.1 %collective-permute-done.refs_0_ = bf16[2048,256]{1,0:T(8,128)(2,1)S(1)} collective-permute-done((bf16[2048,256]{1,0:T(8,128)(2,1)}, bf16[2048,256]{1,0:T(8,128)(2,1)S(1)}, u32[]{:S(2)}, u32[]{:S(2)}) %collective-permute-start) | collective-permute-done | bytes 1048608 | tf_op jit(solution)/shard_map/ppermute | solution.py:31
  85.4 2.9 %collective-permute-start.3 = (bf16[1024,256]{1,0:T(8,128)(2,1)}, bf16[1024,256]{1,0:T(8,128)(2,1)S(1)}, u32[]{:S(2)}, u32[]{:S(2)}) collective-permute-start(bf16[1024,256]{1,0:T(8,128)(2,1)} %slice.95), channel_id=1, source_target_pairs={{0,3},{1,0},{2,1},{3,2},{4,7},{5,4},{6,5},{7,6},{8,11},{9,8},{10,9... | collective-permute-start | bytes 1572872 | tf_op jit(solution)/shard_map/ppermute | solution.py:31
  88.3 17.4 %collective-permute-done.16.refs_2_ = bf16[16,256,128]{2,1,0:T(8,128)(2,1)S(1)} collective-permute-done((bf16[16,256,128]{2,1,0:T(8,128)(2,1)S(1)}, bf16[16,256,128]{2,1,0:T(8,128)(2,1)S(1)}, u32[]{:S(2)}, u32[]{:S(2)}) %collective-permute-start.16) | collective-permute-done | bytes 1048608 | tf_op jit(solution)/shard_map/ppermute | solution.py:31
  107.8 3.6 %all-to-all-start = ((bf16[16,128,128]{2,1,0:T(8,128)(2,1)}), bf16[16,128,128]{2,1,0:T(8,128)(2,1)S(1)}, u32[]{:S(2)}, u32[]{:S(2)}) async-start(bf16[16,128,128]{2,1,0:T(8,128)(2,1)} %bitcast_bitcast_fusion), calls=%async_computation | async-start | bytes 1048576 | tf_op jit(solution)/shard_map/all_to_all | solution.py:302
  111.5 5.5 %collective-permute-done.1 = bf16[1024,256]{1,0:T(8,128)(2,1)} collective-permute-done((bf16[1024,256]{1,0:T(8,128)(2,1)}, bf16[1024,256]{1,0:T(8,128)(2,1)}, u32[]{:S(2)}, u32[]{:S(2)}) %collective-permute-start.1) | collective-permute-done | bytes 524320 | tf_op jit(solution)/shard_map/ppermute | solution.py:31
  126.8 6.9 %collective-permute-done.21 = bf16[8,256,128]{2,1,0:T(8,128)(2,1)} collective-permute-done((bf16[8,256,128]{2,1,0:T(8,128)(2,1)}, bf16[8,256,128]{2,1,0:T(8,128)(2,1)}, u32[]{:S(2)}, u32[]{:S(2)}) %collective-permute-start.21) | collective-permute-done | bytes 524320 | tf_op jit(solution)/shard_map/ppermute | solution.py:31
  136.1 12.5 %shard_map.104 = (f32[2048,128]{1,0:T(8,128)}, f32[2048,128]{1,0:T(8,128)}, f32[2048,128]{1,0:T(8,128)}) custom-call(s32[3]{0:T(128)S(1)} %pad_add_fusion.3.where_ref, bf16[2048,128]{1,0:T(8,128)(2,1)S(1)} %bitcast.72, bf16[2048,256]{1,0:T(8,128)(2,1)} %bitcast.13.refs_0_, bf16[2048,256]{1,0:T(8,128)(2,1)} %collective-permute-done.7.refs_1_), custom_call_target="tpu_custom_call" | custom-call | flops 2684354560 | bytes 2097152 | tf_op jit(solution)/shard_map/pallas_call | solution.py:155
  149.1 19.9 %shard_map.105 = (f32[2048,128]{1,0:T(8,128)}, f32[2048,128]{1,0:T(8,128)}, f32[2048,128]{1,0:T(8,128)}) custom-call(s32[4]{0:T(128)S(1)} %pad_add_fusion.2.where_ref, bf16[2048,128]{1,0:T(8,128)(2,1)S(1)} %bitcast.73, bf16[2048,256]{1,0:T(8,128)(2,1)S(1)} %copy-done.6, bf16[2048,256]{1,0:T(8,128)(2,1)} %collective-permute-done.5.refs_1_, ...), custom_call_target="tpu_custom_call" | custom-call | flops 5368709120 | bytes 4194304 | tf_op jit(solution)/shard_map/pallas_call | solution.py:155
  169.1 13.0 %shard_map.106 = bf16[2048,128]{1,0:T(8,128)(2,1)S(1)} custom-call(s32[3]{0:T(128)S(1)} %pad_add_fusion.where_ref, bf16[2048,128]{1,0:T(8,128)(2,1)S(1)} %bitcast.74, bf16[2048,256]{1,0:T(8,128)(2,1)} %constant_dynamic-update-slice_fusion.refs_0_, bf16[2048,256]{1,0:T(8,128)(2,1)} %collective-permute-done.4.refs_1_, f32[2048,128]{1,0:T(8,128)} %get-tuple-element.17.refs_2_, ...), custom_call_target="tpu_custom_call" | custom-call | flops 2684354560 | bytes 2097152 | tf_op jit(solution)/shard_map/pallas_call | solution.py:155
  182.9 3.6 %all-to-all-start.2 = ((bf16[16,128,128]{2,1,0:T(8,128)(2,1)}), bf16[16,128,128]{2,1,0:T(8,128)(2,1)S(1)}, u32[]{:S(2)}, u32[]{:S(2)}) async-start(bf16[16,128,128]{2,1,0:T(8,128)(2,1)} %bitcast.75), calls=%async_computation.2 | async-start | bytes 1048576 | tf_op jit(solution)/shard_map/all_to_all | solution.py:302
  186.6 12.1 %all-to-all-done.2.attn_ref = bf16[16,128,128]{2,1,0:T(8,128)(2,1)S(1)} async-done(((bf16[16,128,128]{2,1,0:T(8,128)(2,1)}), bf16[16,128,128]{2,1,0:T(8,128)(2,1)S(1)}, u32[]{:S(2)}, u32[]{:S(2)}) %all-to-all-start.2) | async-done | bytes 524320 | tf_op jit(solution)/shard_map/all_to_all | solution.py:302
  198.7 5.3 %shard_map.107 = (bf16[128,2048]{1,0:T(8,128)(2,1)}, bf16[128,2048]{1,0:T(8,128)(2,1)S(1)}) custom-call(s32[7]{0:T(128)S(1)} %stack.103.where_ref, bf16[16,128,128]{2,1,0:T(8,128)(2,1)S(1)} %all-to-all-done.2.attn_ref, bf16[128,2048]{1,0:T(8,128)(2,1)S(1)} %copy-done.3, bf16[1,2048]{1,0:T(2,128)(2,1)S(1)} %reshape.49.gain_ref, ...), custom_call_target="tpu_custom_call" | custom-call | flops 1073741824 | bytes 8388608 | tf_op jit(solution)/shard_map/pallas_call | solution.py:209
  204.4 2.9 %collective-permute-start.26 = (bf16[128,2048]{1,0:T(8,128)(2,1)S(1)}, bf16[128,2048]{1,0:T(8,128)(2,1)S(1)}, u32[]{:S(2)}, u32[]{:S(2)}) collective-permute-start(bf16[128,2048]{1,0:T(8,128)(2,1)S(1)} %get-tuple-element.23.refs_0_), channel_id=1, source_target_pairs={{0,3},{1,0},{2,1},{3,2},{4,7},{5,4},{6,5},{7,6},{8,11},{9,8},{10,9... | collective-permute-start | bytes 1572872 | tf_op jit(solution)/shard_map/ppermute | solution.py:31
  207.3 11.0 %collective-permute-done.25.refs_0_ = bf16[128,2048]{1,0:T(8,128)(2,1)S(1)} collective-permute-done((bf16[128,2048]{1,0:T(8,128)(2,1)S(1)}, bf16[128,2048]{1,0:T(8,128)(2,1)S(1)}, u32[]{:S(2)}, u32[]{:S(2)}) %collective-permute-start.25) | collective-permute-done | bytes 524320 | tf_op jit(solution)/shard_map/ppermute | solution.py:31
  218.4 3.3 %collective-permute-start.31 = (bf16[64,2048]{1,0:T(8,128)(2,1)S(1)}, bf16[64,2048]{1,0:T(8,128)(2,1)S(1)}, u32[]{:S(2)}, u32[]{:S(2)}) collective-permute-start(bf16[64,2048]{1,0:T(8,128)(2,1)S(1)} %slice.106), channel_id=1, source_target_pairs={{0,3},{1,0},{2,1},{3,2},{4,7},{5,4},{6,5},{7,6},{8,11},{9,8},{10,9... | collective-permute-start | bytes 786440 | tf_op jit(solution)/shard_map/ppermute | solution.py:31
  221.7 4.4 %collective-permute-done.30 = bf16[64,2048]{1,0:T(8,128)(2,1)S(1)} collective-permute-done((bf16[64,2048]{1,0:T(8,128)(2,1)S(1)}, bf16[64,2048]{1,0:T(8,128)(2,1)S(1)}, u32[]{:S(2)}, u32[]{:S(2)}) %collective-permute-start.30) | collective-permute-done | bytes 262176 | tf_op jit(solution)/shard_map/ppermute | solution.py:31
  228.1 3.8 %shard_map.110 = bf16[256,2048]{1,0:T(8,128)(2,1)S(1)} custom-call(bf16[16,3,2,224,256]{4,3,2,1,0:T(8,128)(2,1)S(1)} %bitcast.65, bf16[128,2048]{1,0:T(8,128)(2,1)S(1)} %constant_dynamic-update-slice_fusion.4.refs_0_, bf16[128,2048]{1,0:T(8,128)(2,1)S(1)} %collective-permute-done.32.refs_1_), custom_call_target="tpu_custom_call" | custom-call | flops 2818572288 | bytes 11010048 | tf_op jit(solution)/shard_map/pallas_call | solution.py:255
  232.4 7.6 %shard_map.109 = bf16[512,2048]{1,0:T(8,128)(2,1)S(1)} custom-call(bf16[16,3,2,224,256]{4,3,2,1,0:T(8,128)(2,1)S(1)} %bitcast.66, bf16[128,2048]{1,0:T(8,128)(2,1)S(1)} %collective-permute-done.25.refs_0_, bf16[128,2048]{1,0:T(8,128)(2,1)S(1)} %collective-permute-done.26.refs_1_, bf16[128,2048]{1,0:T(8,128)(2,1)S(1)} %collective-permute-done.27.refs_2_, ...), custom_call_target="tpu_custom_call" | custom-call | flops 5637144576 | bytes 11010048 | tf_op jit(solution)/shard_map/pallas_call | solution.py:255
  240.9 3.2 %collective-permute-start.35 = (bf16[64,2048]{1,0:T(8,128)(2,1)S(1)}, bf16[64,2048]{1,0:T(8,128)(2,1)S(1)}, u32[]{:S(2)}, u32[]{:S(2)}) collective-permute-start(bf16[64,2048]{1,0:T(8,128)(2,1)S(1)} %get-tuple-element.32), channel_id=1, source_target_pairs={{0,3},{1,0},{2,1},{3,2},{4,7},{5,4},{6,5},{7,6},{8,11},{9,8},{10,9... | collective-permute-start | bytes 786440 | tf_op jit(solution)/shard_map/ppermute | solution.py:31
  244.1 3.8 %shard_map.108 = bf16[256,2048]{1,0:T(8,128)(2,1)S(1)} custom-call(bf16[16,3,2,224,256]{4,3,2,1,0:T(8,128)(2,1)S(1)} %bitcast.67, bf16[128,2048]{1,0:T(8,128)(2,1)S(1)} %get-tuple-element.23.refs_0_, bf16[128,2048]{1,0:T(8,128)(2,1)S(1)} %collective-permute-done.23.refs_1_), custom_call_target="tpu_custom_call" | custom-call | flops 2818572288 | bytes 11010048 | tf_op jit(solution)/shard_map/pallas_call | solution.py:255
  248.0 2.6 collective-permute-done.34
  251.1 3.1 %collective-permute-start.39 = (bf16[64,2048]{1,0:T(8,128)(2,1)S(1)}, bf16[64,2048]{1,0:T(8,128)(2,1)S(1)}, u32[]{:S(2)}, u32[]{:S(2)}) collective-permute-start(bf16[64,2048]{1,0:T(8,128)(2,1)S(1)} %fusion.1), channel_id=1, source_target_pairs={{0,3},{1,0},{2,1},{3,2},{4,7},{5,4},{6,5},{7,6},{8,11},{9,8},{10,9... | collective-permute-start | bytes 786440 | tf_op jit(solution)/shard_map/ppermute | solution.py:31
  254.4 3.2 %collective-permute-start.37 = (bf16[64,2048]{1,0:T(8,128)(2,1)S(1)}, bf16[64,2048]{1,0:T(8,128)(2,1)S(1)}, u32[]{:S(2)}, u32[]{:S(2)}) collective-permute-start(bf16[64,2048]{1,0:T(8,128)(2,1)S(1)} %slice.134), channel_id=1, source_target_pairs={{0,3},{1,0},{2,1},{3,2},{4,7},{5,4},{6,5},{7,6},{8,11},{9,8},{10,9... | collective-permute-start | bytes 786440 | tf_op jit(solution)/shard_map/ppermute | solution.py:31
  257.7 3.1 %collective-permute-done.39 = bf16[64,2048]{1,0:T(8,128)(2,1)S(1)} collective-permute-done((bf16[64,2048]{1,0:T(8,128)(2,1)S(1)}, bf16[64,2048]{1,0:T(8,128)(2,1)S(1)}, u32[]{:S(2)}, u32[]{:S(2)}) %collective-permute-start.39) | collective-permute-done | bytes 262176 | tf_op jit(solution)/shard_map/ppermute | solution.py:31
  260.9 3.9 %collective-permute-done.36 = bf16[64,2048]{1,0:T(8,128)(2,1)S(1)} collective-permute-done((bf16[64,2048]{1,0:T(8,128)(2,1)S(1)}, bf16[64,2048]{1,0:T(8,128)(2,1)S(1)}, u32[]{:S(2)}, u32[]{:S(2)}) %collective-permute-start.36) | collective-permute-done | bytes 262176 | tf_op jit(solution)/shard_map/ppermute | solution.py:31
  264.8 3.6 %collective-permute-done.38 = bf16[64,2048]{1,0:T(8,128)(2,1)S(1)} collective-permute-done((bf16[64,2048]{1,0:T(8,128)(2,1)S(1)}, bf16[64,2048]{1,0:T(8,128)(2,1)S(1)}, u32[]{:S(2)}, u32[]{:S(2)}) %collective-permute-start.38) | collective-permute-done | bytes 262176 | tf_op jit(solution)/shard_map/ppermute | solution.py:31
  (136 shorter events, 46.8 us)
Async XLA Ops:
  7.2 191.5 %all-gather.2.cloned.1.call-start = ((), (), s32[]{:S(2)}) async-start(), calls=%async_computation.3 | async-start | bytes 11698176 | tf_op jit(solution)/shard_map/all_gather | solution.py:321
  12.8 42.9 %all-to-all-start.1 = ((bf16[16,128,256]{2,1,0:T(8,128)(2,1)}), bf16[16,128,256]{2,1,0:T(8,128)(2,1)}, u32[]{:S(2)}, u32[]{:S(2)}) async-start(bf16[16,128,256]{2,1,0:T(8,128)(2,1)} %maximum_bitcast_fusion), calls=%async_computation.1 | async-start | bytes 2097152 | tf_op jit(solution)/shard_map/all_to_all | solution.py:302
  20.9 24.0 %collective-permute-start.9 = (bf16[256,128]{1,0:T(8,128)(2,1)S(1)}, bf16[256,128]{1,0:T(8,128)(2,1)S(1)}, u32[]{:S(2)}, u32[]{:S(2)}) collective-permute-start(bf16[256,128]{1,0:T(8,128)(2,1)S(1)} %copy-done.13), channel_id=1, source_target_pairs={{0,4},{4,8},{8,12},{12,0},{1,5},{5,9},{9,13},{13,1},{2,6},{6,10},{... | collective-permute-start | bytes 196616 | tf_op jit(solution)/shard_map/ppermute | solution.py:31
  22.8 25.5 %collective-permute-start.10 = (bf16[256,128]{1,0:T(8,128)(2,1)S(1)}, bf16[256,128]{1,0:T(8,128)(2,1)S(1)}, u32[]{:S(2)}, u32[]{:S(2)}) collective-permute-start(bf16[256,128]{1,0:T(8,128)(2,1)S(1)} %copy-done.13), channel_id=1, source_target_pairs={{0,8},{4,12},{8,0},{12,4},{1,9},{5,13},{9,1},{13,5},{2,10},{6,14},... | collective-permute-start | bytes 196616 | tf_op jit(solution)/shard_map/ppermute | solution.py:31
  25.5 22.9 %collective-permute-start.11 = (bf16[256,128]{1,0:T(8,128)(2,1)S(1)}, bf16[256,128]{1,0:T(8,128)(2,1)S(1)}, u32[]{:S(2)}, u32[]{:S(2)}) collective-permute-start(bf16[256,128]{1,0:T(8,128)(2,1)S(1)} %copy-done.13), channel_id=1, source_target_pairs={{0,12},{4,0},{8,4},{12,8},{1,13},{5,1},{9,5},{13,9},{2,14},{6,2},{... | collective-permute-start | bytes 196616 | tf_op jit(solution)/shard_map/ppermute | solution.py:31
  48.5 11.3 %collective-permute-start.12 = (bf16[4,256,128]{2,1,0:T(8,128)(2,1)S(1)}, bf16[4,256,128]{2,1,0:T(8,128)(2,1)S(1)}, u32[]{:S(2)}, u32[]{:S(2)}) collective-permute-start(bf16[4,256,128]{2,1,0:T(8,128)(2,1)S(1)} %pad_maximum_fusion.3), channel_id=1, source_target_pairs={{0,32},{32,64},{64,96},{96,0},{1,33},{33,65},{65,97},{97,1},{2,34}... | collective-permute-start | bytes 786440 | tf_op jit(solution)/shard_map/ppermute | solution.py:31
  51.6 13.8 %collective-permute-start.13 = (bf16[4,256,128]{2,1,0:T(8,128)(2,1)S(1)}, bf16[4,256,128]{2,1,0:T(8,128)(2,1)S(1)}, u32[]{:S(2)}, u32[]{:S(2)}) collective-permute-start(bf16[4,256,128]{2,1,0:T(8,128)(2,1)S(1)} %pad_maximum_fusion.3), channel_id=1, source_target_pairs={{0,64},{32,96},{64,0},{96,32},{1,65},{33,97},{65,1},{97,33},{2,66}... | collective-permute-start | bytes 786440 | tf_op jit(solution)/shard_map/ppermute | solution.py:31
  54.1 12.7 %collective-permute-start.14 = (bf16[4,256,128]{2,1,0:T(8,128)(2,1)S(1)}, bf16[4,256,128]{2,1,0:T(8,128)(2,1)S(1)}, u32[]{:S(2)}, u32[]{:S(2)}) collective-permute-start(bf16[4,256,128]{2,1,0:T(8,128)(2,1)S(1)} %pad_maximum_fusion.3), channel_id=1, source_target_pairs={{0,96},{32,0},{64,32},{96,64},{1,97},{33,1},{65,33},{97,65},{2,98}... | collective-permute-start | bytes 786440 | tf_op jit(solution)/shard_map/ppermute | solution.py:31
  55.7 27.5 %collective-permute-start = (bf16[2048,256]{1,0:T(8,128)(2,1)}, bf16[2048,256]{1,0:T(8,128)(2,1)S(1)}, u32[]{:S(2)}, u32[]{:S(2)}) collective-permute-start(bf16[2048,256]{1,0:T(8,128)(2,1)} %bitcast.13.refs_0_), channel_id=1, source_target_pairs={{0,1},{1,2},{2,3},{3,0},{4,5},{5,6},{6,7},{7,4},{8,9},{9,10},{10,1... | collective-permute-start | bytes 3145736 | tf_op jit(solution)/shard_map/ppermute | solution.py:31
  57.3 27.2 %collective-permute-start.2 = (bf16[2048,256]{1,0:T(8,128)(2,1)}, bf16[2048,256]{1,0:T(8,128)(2,1)S(1)}, u32[]{:S(2)}, u32[]{:S(2)}) collective-permute-start(bf16[2048,256]{1,0:T(8,128)(2,1)} %bitcast.13.refs_0_), channel_id=1, source_target_pairs={{0,3},{1,0},{2,1},{3,2},{4,7},{5,4},{6,5},{7,6},{8,11},{9,8},{10,9... | collective-permute-start | bytes 3145736 | tf_op jit(solution)/shard_map/ppermute | solution.py:31
  66.9 38.7 %collective-permute-start.16 = (bf16[16,256,128]{2,1,0:T(8,128)(2,1)S(1)}, bf16[16,256,128]{2,1,0:T(8,128)(2,1)S(1)}, u32[]{:S(2)}, u32[]{:S(2)}) collective-permute-start(bf16[16,256,128]{2,1,0:T(8,128)(2,1)S(1)} %bitcast.68), channel_id=1, source_target_pairs={{0,1},{1,2},{2,3},{3,0},{4,5},{5,6},{6,7},{7,4},{8,9},{9,10},{10,1... | collective-permute-start | bytes 3145736 | tf_op jit(solution)/shard_map/ppermute | solution.py:31
  68.9 42.6 %collective-permute-start.18 = (bf16[16,256,128]{2,1,0:T(8,128)(2,1)S(1)}, bf16[16,256,128]{2,1,0:T(8,128)(2,1)}, u32[]{:S(2)}, u32[]{:S(2)}) collective-permute-start(bf16[16,256,128]{2,1,0:T(8,128)(2,1)S(1)} %bitcast.69), channel_id=1, source_target_pairs={{0,3},{1,0},{2,1},{3,2},{4,7},{5,4},{6,5},{7,6},{8,11},{9,8},{10,9... | collective-permute-start | bytes 3145736 | tf_op jit(solution)/shard_map/ppermute | solution.py:31
  84.1 32.9 %collective-permute-start.1 = (bf16[1024,256]{1,0:T(8,128)(2,1)}, bf16[1024,256]{1,0:T(8,128)(2,1)}, u32[]{:S(2)}, u32[]{:S(2)}) collective-permute-start(bf16[1024,256]{1,0:T(8,128)(2,1)} %slice.94), channel_id=1, source_target_pairs={{0,1},{1,2},{2,3},{3,0},{4,5},{5,6},{6,7},{7,4},{8,9},{9,10},{10,1... | collective-permute-start | bytes 1572872 | tf_op jit(solution)/shard_map/ppermute | solution.py:31
  85.4 33.6 %collective-permute-start.3 = (bf16[1024,256]{1,0:T(8,128)(2,1)}, bf16[1024,256]{1,0:T(8,128)(2,1)S(1)}, u32[]{:S(2)}, u32[]{:S(2)}) collective-permute-start(bf16[1024,256]{1,0:T(8,128)(2,1)} %slice.95), channel_id=1, source_target_pairs={{0,3},{1,0},{2,1},{3,2},{4,7},{5,4},{6,5},{7,6},{8,11},{9,8},{10,9... | collective-permute-start | bytes 1572872 | tf_op jit(solution)/shard_map/ppermute | solution.py:31
  88.3 47.3 %collective-permute-start.7 = (bf16[2048,256]{1,0:T(8,128)(2,1)}, bf16[2048,256]{1,0:T(8,128)(2,1)}, u32[]{:S(2)}, u32[]{:S(2)}) collective-permute-start(bf16[2048,256]{1,0:T(8,128)(2,1)} %bitcast.13.refs_0_), channel_id=1, source_target_pairs={{0,16},{16,0},{1,17},{17,1},{2,18},{18,2},{3,19},{19,3},{4,20},{20... | collective-permute-start | bytes 3145736 | tf_op jit(solution)/shard_map/ppermute | solution.py:39
  106.5 18.1 %collective-permute-start.20 = (bf16[8,256,128]{2,1,0:T(8,128)(2,1)}, bf16[8,256,128]{2,1,0:T(8,128)(2,1)}, u32[]{:S(2)}, u32[]{:S(2)}) collective-permute-start(bf16[8,256,128]{2,1,0:T(8,128)(2,1)} %slice.96), channel_id=1, source_target_pairs={{0,1},{1,2},{2,3},{3,0},{4,5},{5,6},{6,7},{7,4},{8,9},{9,10},{10,1... | collective-permute-start | bytes 1572872 | tf_op jit(solution)/shard_map/ppermute | solution.py:31
  107.8 28.2 %all-to-all-start = ((bf16[16,128,128]{2,1,0:T(8,128)(2,1)}), bf16[16,128,128]{2,1,0:T(8,128)(2,1)S(1)}, u32[]{:S(2)}, u32[]{:S(2)}) async-start(bf16[16,128,128]{2,1,0:T(8,128)(2,1)} %bitcast_bitcast_fusion), calls=%async_computation | async-start | bytes 1048576 | tf_op jit(solution)/shard_map/all_to_all | solution.py:302
  111.4 37.1 %collective-permute-start.5 = (bf16[2048,256]{1,0:T(8,128)(2,1)}, bf16[2048,256]{1,0:T(8,128)(2,1)}, u32[]{:S(2)}, u32[]{:S(2)}) collective-permute-start(bf16[2048,256]{1,0:T(8,128)(2,1)} %copy-done.5), channel_id=1, source_target_pairs={{0,16},{16,0},{1,17},{17,1},{2,18},{18,2},{3,19},{19,3},{4,20},{20... | collective-permute-start | bytes 3145736 | tf_op jit(solution)/shard_map/ppermute | solution.py:39
  117.0 31.6 %collective-permute-start.6 = (bf16[2048,256]{1,0:T(8,128)(2,1)}, bf16[2048,256]{1,0:T(8,128)(2,1)}, u32[]{:S(2)}, u32[]{:S(2)}) collective-permute-start(bf16[2048,256]{1,0:T(8,128)(2,1)} %copy-done.7), channel_id=1, source_target_pairs={{0,16},{16,0},{1,17},{17,1},{2,18},{18,2},{3,19},{19,3},{4,20},{20... | collective-permute-start | bytes 3145736 | tf_op jit(solution)/shard_map/ppermute | solution.py:39
  119.0 14.7 %collective-permute-start.21 = (bf16[8,256,128]{2,1,0:T(8,128)(2,1)}, bf16[8,256,128]{2,1,0:T(8,128)(2,1)}, u32[]{:S(2)}, u32[]{:S(2)}) collective-permute-start(bf16[8,256,128]{2,1,0:T(8,128)(2,1)} %slice.97), channel_id=1, source_target_pairs={{0,3},{1,0},{2,1},{3,2},{4,7},{5,4},{6,5},{7,6},{8,11},{9,8},{10,9... | collective-permute-start | bytes 1572872 | tf_op jit(solution)/shard_map/ppermute | solution.py:31
  124.6 44.5 %collective-permute-start.4 = (bf16[2048,256]{1,0:T(8,128)(2,1)}, bf16[2048,256]{1,0:T(8,128)(2,1)}, u32[]{:S(2)}, u32[]{:S(2)}) collective-permute-start(bf16[2048,256]{1,0:T(8,128)(2,1)} %constant_dynamic-update-slice_fusion.refs_0_), channel_id=1, source_target_pairs={{0,16},{16,0},{1,17},{17,1},{2,18},{18,2},{3,19},{19,3},{4,20},{20... | collective-permute-start | bytes 3145736 | tf_op jit(solution)/shard_map/ppermute | solution.py:39
  133.6 65.1 %collective-permute-start.15 = (bf16[16,256,128]{2,1,0:T(8,128)(2,1)S(1)}, bf16[16,256,128]{2,1,0:T(8,128)(2,1)}, u32[]{:S(2)}, u32[]{:S(2)}) collective-permute-start(bf16[16,256,128]{2,1,0:T(8,128)(2,1)S(1)} %bitcast.70), channel_id=1, source_target_pairs={{0,16},{16,0},{1,17},{17,1},{2,18},{18,2},{3,19},{19,3},{4,20},{20... | collective-permute-start | bytes 3145736 | tf_op jit(solution)/shard_map/ppermute | solution.py:39
  135.6 63.1 %collective-permute-start.17 = (bf16[16,256,128]{2,1,0:T(8,128)(2,1)S(1)}, bf16[16,256,128]{2,1,0:T(8,128)(2,1)}, u32[]{:S(2)}, u32[]{:S(2)}) collective-permute-start(bf16[16,256,128]{2,1,0:T(8,128)(2,1)S(1)} %collective-permute-done.16.refs_2_), channel_id=1, source_target_pairs={{0,16},{16,0},{1,17},{17,1},{2,18},{18,2},{3,19},{19,3},{4,20},{20... | collective-permute-start | bytes 3145736 | tf_op jit(solution)/shard_map/ppermute | solution.py:39
  148.5 50.2 %collective-permute-start.19 = (bf16[16,256,128]{2,1,0:T(8,128)(2,1)}, bf16[16,256,128]{2,1,0:T(8,128)(2,1)}, u32[]{:S(2)}, u32[]{:S(2)}) collective-permute-start(bf16[16,256,128]{2,1,0:T(8,128)(2,1)} %collective-permute-done.18.refs_4_), channel_id=1, source_target_pairs={{0,16},{16,0},{1,17},{17,1},{2,18},{18,2},{3,19},{19,3},{4,20},{20... | collective-permute-start | bytes 3145736 | tf_op jit(solution)/shard_map/ppermute | solution.py:39
  148.6 50.1 %collective-permute-start.22 = (bf16[16,256,128]{2,1,0:T(8,128)(2,1)}, bf16[16,256,128]{2,1,0:T(8,128)(2,1)}, u32[]{:S(2)}, u32[]{:S(2)}) collective-permute-start(bf16[16,256,128]{2,1,0:T(8,128)(2,1)} %constant_dynamic-update-slice_fusion.2.refs_6_), channel_id=1, source_target_pairs={{0,16},{16,0},{1,17},{17,1},{2,18},{18,2},{3,19},{19,3},{4,20},{20... | collective-permute-start | bytes 3145736 | tf_op jit(solution)/shard_map/ppermute | solution.py:39
  182.9 15.8 %all-to-all-start.2 = ((bf16[16,128,128]{2,1,0:T(8,128)(2,1)}), bf16[16,128,128]{2,1,0:T(8,128)(2,1)S(1)}, u32[]{:S(2)}, u32[]{:S(2)}) async-start(bf16[16,128,128]{2,1,0:T(8,128)(2,1)} %bitcast.75), calls=%async_computation.2 | async-start | bytes 1048576 | tf_op jit(solution)/shard_map/all_to_all | solution.py:302
  204.0 14.2 %collective-permute-start.25 = (bf16[128,2048]{1,0:T(8,128)(2,1)S(1)}, bf16[128,2048]{1,0:T(8,128)(2,1)S(1)}, u32[]{:S(2)}, u32[]{:S(2)}) collective-permute-start(bf16[128,2048]{1,0:T(8,128)(2,1)S(1)} %get-tuple-element.23.refs_0_), channel_id=1, source_target_pairs={{0,1},{1,2},{2,3},{3,0},{4,5},{5,6},{6,7},{7,4},{8,9},{9,10},{10,1... | collective-permute-start | bytes 1572872 | tf_op jit(solution)/shard_map/ppermute | solution.py:31
  204.4 14.0 %collective-permute-start.26 = (bf16[128,2048]{1,0:T(8,128)(2,1)S(1)}, bf16[128,2048]{1,0:T(8,128)(2,1)S(1)}, u32[]{:S(2)}, u32[]{:S(2)}) collective-permute-start(bf16[128,2048]{1,0:T(8,128)(2,1)S(1)} %get-tuple-element.23.refs_0_), channel_id=1, source_target_pairs={{0,3},{1,0},{2,1},{3,2},{4,7},{5,4},{6,5},{7,6},{8,11},{9,8},{10,9... | collective-permute-start | bytes 1572872 | tf_op jit(solution)/shard_map/ppermute | solution.py:31
  226.8 17.3 %collective-permute-start.23 = (bf16[128,2048]{1,0:T(8,128)(2,1)S(1)}, bf16[128,2048]{1,0:T(8,128)(2,1)S(1)}, u32[]{:S(2)}, u32[]{:S(2)}) collective-permute-start(bf16[128,2048]{1,0:T(8,128)(2,1)S(1)} %get-tuple-element.23.refs_0_), channel_id=1, source_target_pairs={{0,16},{16,0},{1,17},{17,1},{2,18},{18,2},{3,19},{19,3},{4,20},{20... | collective-permute-start | bytes 1572872 | tf_op jit(solution)/shard_map/ppermute | solution.py:39
  240.1 10.5 %collective-permute-start.29 = (bf16[256,2048]{1,0:T(8,128)(2,1)S(1)}, bf16[256,2048]{1,0:T(8,128)(2,1)S(1)}, u32[]{:S(2)}, u32[]{:S(2)}) collective-permute-start(bf16[256,2048]{1,0:T(8,128)(2,1)S(1)} %slice.102), channel_id=1, source_target_pairs={{0,16},{16,0},{1,17},{17,1},{2,18},{18,2},{3,19},{19,3},{4,20},{20... | collective-permute-start | bytes 3145736 | tf_op jit(solution)/shard_map/ppermute | solution.py:39
  254.3 10.5 %collective-permute-start.36 = (bf16[64,2048]{1,0:T(8,128)(2,1)S(1)}, bf16[64,2048]{1,0:T(8,128)(2,1)S(1)}, u32[]{:S(2)}, u32[]{:S(2)}) collective-permute-start(bf16[64,2048]{1,0:T(8,128)(2,1)S(1)} %fusion.2), channel_id=1, source_target_pairs={{0,1},{1,2},{2,3},{3,0},{4,5},{5,6},{6,7},{7,4},{8,9},{9,10},{10,1... | collective-permute-start | bytes 786440 | tf_op jit(solution)/shard_map/ppermute | solution.py:31
  257.6 10.8 %collective-permute-start.38 = (bf16[64,2048]{1,0:T(8,128)(2,1)S(1)}, bf16[64,2048]{1,0:T(8,128)(2,1)S(1)}, u32[]{:S(2)}, u32[]{:S(2)}) collective-permute-start(bf16[64,2048]{1,0:T(8,128)(2,1)S(1)} %slice.133), channel_id=1, source_target_pairs={{0,1},{1,2},{2,3},{3,0},{4,5},{5,6},{6,7},{7,4},{8,9},{9,10},{10,1... | collective-permute-start | bytes 786440 | tf_op jit(solution)/shard_map/ppermute | solution.py:31
  (27 other events, 376.0 us)
Sparse Core Ops, SparseCore 0:
  11.4 98.0 all-gather.1

commit v3 on v2

--- a/solution.py
+++ b/solution.py
@@ -37,6 +37,26 @@
 
 def other_core(array):
     return lax.ppermute(array, "c", [(0, 1), (1, 0)])
+
+
+def by_head_body(keys_ref, values_ref, o_ref):
+    n_kv = keys_ref.shape[1] // HEAD_DIM
+    for h in range(HEADS):
+        g = h * n_kv // HEADS
+        cols = slice(g * HEAD_DIM, (g + 1) * HEAD_DIM)
+        o_ref[h, :, :HEAD_DIM] = keys_ref[:, cols]
+        o_ref[h, :, HEAD_DIM:] = values_ref[:, cols]
+
+
+def by_head(keys, values):
+    vmem = pl.BlockSpec(memory_space=pltpu.VMEM)
+    return pl.pallas_call(
+        by_head_body,
+        out_shape=jax.ShapeDtypeStruct((HEADS, ROWS, 2 * HEAD_DIM), BF16),
+        in_specs=[vmem] * 2,
+        out_specs=vmem,
+        compiler_params=params(8),
+    )(keys, values)
 
 
 def attend_body(first, last, n_pairs, where_ref, q_ref, *refs):
@@ -291,18 +311,12 @@
     d = tokens.shape[1]
     core = lax.axis_index("c")
     y = lax.axis_index("y")
-    group = HEADS // (keys.shape[1] // HEAD_DIM)
-
-    def by_head(array, times):
-        out = array.reshape(ROWS, -1, 1, HEAD_DIM)
-        out = jnp.broadcast_to(out, (ROWS, out.shape[1], times, HEAD_DIM))
-        return out.reshape(ROWS, HEADS, HEAD_DIM)
 
     def regroup(array):
         return lax.all_to_all(array, ("z", "x"), split_axis=0, concat_axis=0, tiled=True)
 
-    kv = jnp.concatenate([by_head(keys, group), by_head(values, group)], axis=2)
-    kv = regroup(kv.transpose(1, 0, 2)).reshape(LOCAL, 2 * HEAD_DIM)
+    kv = by_head(keys, values)
+    kv = regroup(kv).reshape(LOCAL, 2 * HEAD_DIM)
     kv_c, before, after = gather_near(kv)
 
     wo = jnp.stack([out_weight] + [along(out_weight, "x", i) for i in range(1, X)])
@@ -310,7 +324,8 @@
     wo = jnp.stack([wo] + [along(wo, "z", i) for i in range(1, Z)])
     wo = wo.reshape(Z * X, *out_weight.shape)
 
-    q = regroup(by_head(queries, 1).transpose(1, 0, 2)).reshape(LOCAL, HEAD_DIM)
+    q = queries.reshape(ROWS, HEADS, HEAD_DIM).transpose(1, 0, 2)
+    q = regroup(q).reshape(LOCAL, HEAD_DIM)
 
     packed = jnp.stack([gate_weight.T, up_weight.T, down_weight])
     packed = packed.reshape(3, 2, packed.shape[1] // 2, packed.shape[2])

time: 277 us -> 277 us (level)
  transfers between devices with their start and end apart: 44 -> 44, of which waited for: 19 -> 19; matrix products, arithmetic and copies ran while one was open for 6% -> 5% of each run, Pallas kernels for 22% -> 22%
where the time goes in v3:
time: 277 us; the launch traced here: 276 us
  waiting for transfers between devices  115 us (42%)
  Pallas kernels  66.9 us (24%)
  starting transfers between devices  60.8 us (22%)
  between operations  14.5 us (5%)
  local copies, waits for them, and re-layouts  14.3 us (5%)
  other arithmetic  4.45 us (2%)
    ppermute x24, waiting for transfers between devices, along(): return lax.ppermute(array, axis, [(i, (i + step) % 4) for i in range(4)])  100 us
    pallas_call x3, Pallas kernels, attend(): pl.pallas_call(functools.partial(attend_body, first, last, n_pairs), out_...  45.4 us
    ppermute x24, starting transfers between devices, along(): return lax.ppermute(array, axis, [(i, (i + step) % 4) for i in range(4)])  42 us
    all_to_all x3, starting transfers between devices, regroup(): lax.all_to_all(array, ('z', 'x'), split_axis=0, concat_axis=0, tiled=True)  15.2 us
    pallas_call x3, Pallas kernels, ffn(): pl.pallas_call(functools.partial(ffn_body, n), out_shape=jax.ShapeDtypeSt...  15.1 us
    all_to_all x3, waiting for transfers between devices, regroup(): lax.all_to_all(array, ('z', 'x'), split_axis=0, concat_axis=0, tiled=True)  12.1 us
  transfers between devices with their start and end apart: 44, of which 19 were waited for; matrix products, arithmetic and copies ran while one was open for 5% of the time, Pallas kernels for 22%

profile of v3, /device:TPU:0, one launch (start us, length us, event | category | flops | bytes accessed | tf_op | source)
XLA Modules:
  0.0 275.9 jit_solution(886910883861180835)
XLA Ops:
  12.5 8.0 %all-to-all-start.1 = ((bf16[16,128,256]{2,1,0:T(8,128)(2,1)}), bf16[16,128,256]{2,1,0:T(8,128)(2,1)}, u32[]{:S(2)}, u32[]{:S(2)}) async-start(bf16[16,128,256]{2,1,0:T(8,128)(2,1)} %shard_map.104), calls=%async_computation.1 | async-start | bytes 2097152 | tf_op jit(solution)/shard_map/all_to_all | solution.py:316
  22.5 2.7 collective-permute-start.10
  26.6 17.9 %collective-permute-done.9 = bf16[256,128]{1,0:T(8,128)(2,1)S(1)} collective-permute-done((bf16[256,128]{1,0:T(8,128)(2,1)S(1)}, bf16[256,128]{1,0:T(8,128)(2,1)S(1)}, u32[]{:S(2)}, u32[]{:S(2)}) %collective-permute-start.9) | collective-permute-done | bytes 65568 | tf_op jit(solution)/shard_map/ppermute | solution.py:31
  44.6 3.2 %collective-permute-done.10 = bf16[256,128]{1,0:T(8,128)(2,1)S(1)} collective-permute-done((bf16[256,128]{1,0:T(8,128)(2,1)S(1)}, bf16[256,128]{1,0:T(8,128)(2,1)S(1)}, u32[]{:S(2)}, u32[]{:S(2)}) %collective-permute-start.10) | collective-permute-done | bytes 65568 | tf_op jit(solution)/shard_map/ppermute | solution.py:31
  48.0 3.2 %collective-permute-start.12 = (bf16[4,256,128]{2,1,0:T(8,128)(2,1)S(1)}, bf16[4,256,128]{2,1,0:T(8,128)(2,1)S(1)}, u32[]{:S(2)}, u32[]{:S(2)}) collective-permute-start(bf16[4,256,128]{2,1,0:T(8,128)(2,1)S(1)} %pad_maximum_fusion.3), channel_id=1, source_target_pairs={{0,32},{32,64},{64,96},{96,0},{1,33},{33,65},{65,97},{97,1},{2,34}... | collective-permute-start | bytes 786440 | tf_op jit(solution)/shard_map/ppermute | solution.py:31
  59.4 5.0 %collective-permute-done.13 = bf16[4,256,128]{2,1,0:T(8,128)(2,1)S(1)} collective-permute-done((bf16[4,256,128]{2,1,0:T(8,128)(2,1)S(1)}, bf16[4,256,128]{2,1,0:T(8,128)(2,1)S(1)}, u32[]{:S(2)}, u32[]{:S(2)}) %collective-permute-start.13) | collective-permute-done | bytes 262176 | tf_op jit(solution)/shard_map/ppermute | solution.py:31
  69.9 12.9 %collective-permute-done.refs_0_ = bf16[2048,256]{1,0:T(8,128)(2,1)S(1)} collective-permute-done((bf16[2048,256]{1,0:T(8,128)(2,1)}, bf16[2048,256]{1,0:T(8,128)(2,1)S(1)}, u32[]{:S(2)}, u32[]{:S(2)}) %collective-permute-start) | collective-permute-done | bytes 1048608 | tf_op jit(solution)/shard_map/ppermute | solution.py:31
  85.0 2.9 %collective-permute-start.3 = (bf16[1024,256]{1,0:T(8,128)(2,1)}, bf16[1024,256]{1,0:T(8,128)(2,1)S(1)}, u32[]{:S(2)}, u32[]{:S(2)}) collective-permute-start(bf16[1024,256]{1,0:T(8,128)(2,1)} %slice.95), channel_id=1, source_target_pairs={{0,3},{1,0},{2,1},{3,2},{4,7},{5,4},{6,5},{7,6},{8,11},{9,8},{10,9... | collective-permute-start | bytes 1572872 | tf_op jit(solution)/shard_map/ppermute | solution.py:31
  87.9 17.4 %collective-permute-done.16.refs_2_ = bf16[16,256,128]{2,1,0:T(8,128)(2,1)S(1)} collective-permute-done((bf16[16,256,128]{2,1,0:T(8,128)(2,1)S(1)}, bf16[16,256,128]{2,1,0:T(8,128)(2,1)S(1)}, u32[]{:S(2)}, u32[]{:S(2)}) %collective-permute-start.16) | collective-permute-done | bytes 1048608 | tf_op jit(solution)/shard_map/ppermute | solution.py:31
  107.5 3.6 %all-to-all-start = ((bf16[16,128,128]{2,1,0:T(8,128)(2,1)}), bf16[16,128,128]{2,1,0:T(8,128)(2,1)S(1)}, u32[]{:S(2)}, u32[]{:S(2)}) async-start(bf16[16,128,128]{2,1,0:T(8,128)(2,1)} %bitcast_bitcast_fusion), calls=%async_computation | async-start | bytes 1048576 | tf_op jit(solution)/shard_map/all_to_all | solution.py:316
  111.2 5.5 %collective-permute-done.1 = bf16[1024,256]{1,0:T(8,128)(2,1)} collective-permute-done((bf16[1024,256]{1,0:T(8,128)(2,1)}, bf16[1024,256]{1,0:T(8,128)(2,1)}, u32[]{:S(2)}, u32[]{:S(2)}) %collective-permute-start.1) | collective-permute-done | bytes 524320 | tf_op jit(solution)/shard_map/ppermute | solution.py:31
  126.4 6.9 %collective-permute-done.21 = bf16[8,256,128]{2,1,0:T(8,128)(2,1)} collective-permute-done((bf16[8,256,128]{2,1,0:T(8,128)(2,1)}, bf16[8,256,128]{2,1,0:T(8,128)(2,1)}, u32[]{:S(2)}, u32[]{:S(2)}) %collective-permute-start.21) | collective-permute-done | bytes 524320 | tf_op jit(solution)/shard_map/ppermute | solution.py:31
  135.7 12.5 %shard_map.105 = (f32[2048,128]{1,0:T(8,128)}, f32[2048,128]{1,0:T(8,128)}, f32[2048,128]{1,0:T(8,128)}) custom-call(s32[3]{0:T(128)S(1)} %pad_add_fusion.3.where_ref, bf16[2048,128]{1,0:T(8,128)(2,1)S(1)} %bitcast.58, bf16[2048,256]{1,0:T(8,128)(2,1)} %bitcast.10.refs_0_, bf16[2048,256]{1,0:T(8,128)(2,1)} %collective-permute-done.7.refs_1_), custom_call_target="tpu_custom_call" | custom-call | flops 2684354560 | bytes 2097152 | tf_op jit(solution)/shard_map/pallas_call | solution.py:175
  148.8 19.9 %shard_map.106 = (f32[2048,128]{1,0:T(8,128)}, f32[2048,128]{1,0:T(8,128)}, f32[2048,128]{1,0:T(8,128)}) custom-call(s32[4]{0:T(128)S(1)} %pad_add_fusion.2.where_ref, bf16[2048,128]{1,0:T(8,128)(2,1)S(1)} %bitcast.59, bf16[2048,256]{1,0:T(8,128)(2,1)S(1)} %copy-done.6, bf16[2048,256]{1,0:T(8,128)(2,1)} %collective-permute-done.5.refs_1_, ...), custom_call_target="tpu_custom_call" | custom-call | flops 5368709120 | bytes 4194304 | tf_op jit(solution)/shard_map/pallas_call | solution.py:175
  168.8 13.0 %shard_map.107 = bf16[2048,128]{1,0:T(8,128)(2,1)S(1)} custom-call(s32[3]{0:T(128)S(1)} %pad_add_fusion.where_ref, bf16[2048,128]{1,0:T(8,128)(2,1)S(1)} %bitcast.60, bf16[2048,256]{1,0:T(8,128)(2,1)} %constant_dynamic-update-slice_fusion.refs_0_, bf16[2048,256]{1,0:T(8,128)(2,1)} %collective-permute-done.4.refs_1_, f32[2048,128]{1,0:T(8,128)} %get-tuple-element.17.refs_2_, ...), custom_call_target="tpu_custom_call" | custom-call | flops 2684354560 | bytes 2097152 | tf_op jit(solution)/shard_map/pallas_call | solution.py:175
  182.5 3.6 %all-to-all-start.2 = ((bf16[16,128,128]{2,1,0:T(8,128)(2,1)}), bf16[16,128,128]{2,1,0:T(8,128)(2,1)S(1)}, u32[]{:S(2)}, u32[]{:S(2)}) async-start(bf16[16,128,128]{2,1,0:T(8,128)(2,1)} %bitcast.61), calls=%async_computation.2 | async-start | bytes 1048576 | tf_op jit(solution)/shard_map/all_to_all | solution.py:316
  186.2 12.1 %all-to-all-done.2.attn_ref = bf16[16,128,128]{2,1,0:T(8,128)(2,1)S(1)} async-done(((bf16[16,128,128]{2,1,0:T(8,128)(2,1)}), bf16[16,128,128]{2,1,0:T(8,128)(2,1)S(1)}, u32[]{:S(2)}, u32[]{:S(2)}) %all-to-all-start.2) | async-done | bytes 524320 | tf_op jit(solution)/shard_map/all_to_all | solution.py:316
  198.4 5.3 %shard_map.108 = (bf16[128,2048]{1,0:T(8,128)(2,1)}, bf16[128,2048]{1,0:T(8,128)(2,1)S(1)}) custom-call(s32[7]{0:T(128)S(1)} %stack.103.where_ref, bf16[16,128,128]{2,1,0:T(8,128)(2,1)S(1)} %all-to-all-done.2.attn_ref, bf16[128,2048]{1,0:T(8,128)(2,1)S(1)} %copy-done.3, bf16[1,2048]{1,0:T(2,128)(2,1)S(1)} %reshape.41.gain_ref, ...), custom_call_target="tpu_custom_call" | custom-call | flops 1073741824 | bytes 8388608 | tf_op jit(solution)/shard_map/pallas_call | solution.py:229
  204.0 2.9 %collective-permute-start.26 = (bf16[128,2048]{1,0:T(8,128)(2,1)S(1)}, bf16[128,2048]{1,0:T(8,128)(2,1)S(1)}, u32[]{:S(2)}, u32[]{:S(2)}) collective-permute-start(bf16[128,2048]{1,0:T(8,128)(2,1)S(1)} %get-tuple-element.23.refs_0_), channel_id=1, source_target_pairs={{0,3},{1,0},{2,1},{3,2},{4,7},{5,4},{6,5},{7,6},{8,11},{9,8},{10,9... | collective-permute-start | bytes 1572872 | tf_op jit(solution)/shard_map/ppermute | solution.py:31
  206.9 11.0 %collective-permute-done.25.refs_0_ = bf16[128,2048]{1,0:T(8,128)(2,1)S(1)} collective-permute-done((bf16[128,2048]{1,0:T(8,128)(2,1)S(1)}, bf16[128,2048]{1,0:T(8,128)(2,1)S(1)}, u32[]{:S(2)}, u32[]{:S(2)}) %collective-permute-start.25) | collective-permute-done | bytes 524320 | tf_op jit(solution)/shard_map/ppermute | solution.py:31
  218.1 3.3 %collective-permute-start.31 = (bf16[64,2048]{1,0:T(8,128)(2,1)S(1)}, bf16[64,2048]{1,0:T(8,128)(2,1)S(1)}, u32[]{:S(2)}, u32[]{:S(2)}) collective-permute-start(bf16[64,2048]{1,0:T(8,128)(2,1)S(1)} %slice.106), channel_id=1, source_target_pairs={{0,3},{1,0},{2,1},{3,2},{4,7},{5,4},{6,5},{7,6},{8,11},{9,8},{10,9... | collective-permute-start | bytes 786440 | tf_op jit(solution)/shard_map/ppermute | solution.py:31
  221.3 4.4 %collective-permute-done.30 = bf16[64,2048]{1,0:T(8,128)(2,1)S(1)} collective-permute-done((bf16[64,2048]{1,0:T(8,128)(2,1)S(1)}, bf16[64,2048]{1,0:T(8,128)(2,1)S(1)}, u32[]{:S(2)}, u32[]{:S(2)}) %collective-permute-start.30) | collective-permute-done | bytes 262176 | tf_op jit(solution)/shard_map/ppermute | solution.py:31
  227.8 3.8 %shard_map.111 = bf16[256,2048]{1,0:T(8,128)(2,1)S(1)} custom-call(bf16[16,3,2,224,256]{4,3,2,1,0:T(8,128)(2,1)S(1)} %bitcast.51, bf16[128,2048]{1,0:T(8,128)(2,1)S(1)} %constant_dynamic-update-slice_fusion.4.refs_0_, bf16[128,2048]{1,0:T(8,128)(2,1)S(1)} %collective-permute-done.32.refs_1_), custom_call_target="tpu_custom_call" | custom-call | flops 2818572288 | bytes 11010048 | tf_op jit(solution)/shard_map/pallas_call | solution.py:275
  232.1 7.6 %shard_map.110 = bf16[512,2048]{1,0:T(8,128)(2,1)S(1)} custom-call(bf16[16,3,2,224,256]{4,3,2,1,0:T(8,128)(2,1)S(1)} %bitcast.52, bf16[128,2048]{1,0:T(8,128)(2,1)S(1)} %collective-permute-done.25.refs_0_, bf16[128,2048]{1,0:T(8,128)(2,1)S(1)} %collective-permute-done.26.refs_1_, bf16[128,2048]{1,0:T(8,128)(2,1)S(1)} %collective-permute-done.27.refs_2_, ...), custom_call_target="tpu_custom_call" | custom-call | flops 5637144576 | bytes 11010048 | tf_op jit(solution)/shard_map/pallas_call | solution.py:275
  240.5 3.2 %collective-permute-start.35 = (bf16[64,2048]{1,0:T(8,128)(2,1)S(1)}, bf16[64,2048]{1,0:T(8,128)(2,1)S(1)}, u32[]{:S(2)}, u32[]{:S(2)}) collective-permute-start(bf16[64,2048]{1,0:T(8,128)(2,1)S(1)} %get-tuple-element.32), channel_id=1, source_target_pairs={{0,3},{1,0},{2,1},{3,2},{4,7},{5,4},{6,5},{7,6},{8,11},{9,8},{10,9... | collective-permute-start | bytes 786440 | tf_op jit(solution)/shard_map/ppermute | solution.py:31
  243.8 3.8 %shard_map.109 = bf16[256,2048]{1,0:T(8,128)(2,1)S(1)} custom-call(bf16[16,3,2,224,256]{4,3,2,1,0:T(8,128)(2,1)S(1)} %bitcast.53, bf16[128,2048]{1,0:T(8,128)(2,1)S(1)} %get-tuple-element.23.refs_0_, bf16[128,2048]{1,0:T(8,128)(2,1)S(1)} %collective-permute-done.23.refs_1_), custom_call_target="tpu_custom_call" | custom-call | flops 2818572288 | bytes 11010048 | tf_op jit(solution)/shard_map/pallas_call | solution.py:275
  247.7 2.6 collective-permute-done.34
  250.7 3.1 %collective-permute-start.39 = (bf16[64,2048]{1,0:T(8,128)(2,1)S(1)}, bf16[64,2048]{1,0:T(8,128)(2,1)S(1)}, u32[]{:S(2)}, u32[]{:S(2)}) collective-permute-start(bf16[64,2048]{1,0:T(8,128)(2,1)S(1)} %fusion.1), channel_id=1, source_target_pairs={{0,3},{1,0},{2,1},{3,2},{4,7},{5,4},{6,5},{7,6},{8,11},{9,8},{10,9... | collective-permute-start | bytes 786440 | tf_op jit(solution)/shard_map/ppermute | solution.py:31
  254.0 3.2 %collective-permute-start.37 = (bf16[64,2048]{1,0:T(8,128)(2,1)S(1)}, bf16[64,2048]{1,0:T(8,128)(2,1)S(1)}, u32[]{:S(2)}, u32[]{:S(2)}) collective-permute-start(bf16[64,2048]{1,0:T(8,128)(2,1)S(1)} %slice.134), channel_id=1, source_target_pairs={{0,3},{1,0},{2,1},{3,2},{4,7},{5,4},{6,5},{7,6},{8,11},{9,8},{10,9... | collective-permute-start | bytes 786440 | tf_op jit(solution)/shard_map/ppermute | solution.py:31
  257.4 3.1 %collective-permute-done.39 = bf16[64,2048]{1,0:T(8,128)(2,1)S(1)} collective-permute-done((bf16[64,2048]{1,0:T(8,128)(2,1)S(1)}, bf16[64,2048]{1,0:T(8,128)(2,1)S(1)}, u32[]{:S(2)}, u32[]{:S(2)}) %collective-permute-start.39) | collective-permute-done | bytes 262176 | tf_op jit(solution)/shard_map/ppermute | solution.py:31
  260.5 3.9 %collective-permute-done.36 = bf16[64,2048]{1,0:T(8,128)(2,1)S(1)} collective-permute-done((bf16[64,2048]{1,0:T(8,128)(2,1)S(1)}, bf16[64,2048]{1,0:T(8,128)(2,1)S(1)}, u32[]{:S(2)}, u32[]{:S(2)}) %collective-permute-start.36) | collective-permute-done | bytes 262176 | tf_op jit(solution)/shard_map/ppermute | solution.py:31
  264.4 3.6 %collective-permute-done.38 = bf16[64,2048]{1,0:T(8,128)(2,1)S(1)} collective-permute-done((bf16[64,2048]{1,0:T(8,128)(2,1)S(1)}, bf16[64,2048]{1,0:T(8,128)(2,1)S(1)}, u32[]{:S(2)}, u32[]{:S(2)}) %collective-permute-start.38) | collective-permute-done | bytes 262176 | tf_op jit(solution)/shard_map/ppermute | solution.py:31
  (132 shorter events, 46.4 us)
Async XLA Ops:
  7.2 191.2 %all-gather.2.cloned.1.call-start = ((), (), s32[]{:S(2)}) async-start(), calls=%async_computation.3 | async-start | bytes 11698176 | tf_op jit(solution)/shard_map/all_gather | solution.py:336
  12.5 42.9 %all-to-all-start.1 = ((bf16[16,128,256]{2,1,0:T(8,128)(2,1)}), bf16[16,128,256]{2,1,0:T(8,128)(2,1)}, u32[]{:S(2)}, u32[]{:S(2)}) async-start(bf16[16,128,256]{2,1,0:T(8,128)(2,1)} %shard_map.104), calls=%async_computation.1 | async-start | bytes 2097152 | tf_op jit(solution)/shard_map/all_to_all | solution.py:316
  20.5 24.0 %collective-permute-start.9 = (bf16[256,128]{1,0:T(8,128)(2,1)S(1)}, bf16[256,128]{1,0:T(8,128)(2,1)S(1)}, u32[]{:S(2)}, u32[]{:S(2)}) collective-permute-start(bf16[256,128]{1,0:T(8,128)(2,1)S(1)} %copy-done.13), channel_id=1, source_target_pairs={{0,4},{4,8},{8,12},{12,0},{1,5},{5,9},{9,13},{13,1},{2,6},{6,10},{... | collective-permute-start | bytes 196616 | tf_op jit(solution)/shard_map/ppermute | solution.py:31
  22.5 25.3 %collective-permute-start.10 = (bf16[256,128]{1,0:T(8,128)(2,1)S(1)}, bf16[256,128]{1,0:T(8,128)(2,1)S(1)}, u32[]{:S(2)}, u32[]{:S(2)}) collective-permute-start(bf16[256,128]{1,0:T(8,128)(2,1)S(1)} %copy-done.13), channel_id=1, source_target_pairs={{0,8},{4,12},{8,0},{12,4},{1,9},{5,13},{9,1},{13,5},{2,10},{6,14},... | collective-permute-start | bytes 196616 | tf_op jit(solution)/shard_map/ppermute | solution.py:31
  25.2 22.8 %collective-permute-start.11 = (bf16[256,128]{1,0:T(8,128)(2,1)S(1)}, bf16[256,128]{1,0:T(8,128)(2,1)S(1)}, u32[]{:S(2)}, u32[]{:S(2)}) collective-permute-start(bf16[256,128]{1,0:T(8,128)(2,1)S(1)} %copy-done.13), channel_id=1, source_target_pairs={{0,12},{4,0},{8,4},{12,8},{1,13},{5,1},{9,5},{13,9},{2,14},{6,2},{... | collective-permute-start | bytes 196616 | tf_op jit(solution)/shard_map/ppermute | solution.py:31
  48.0 11.4 %collective-permute-start.12 = (bf16[4,256,128]{2,1,0:T(8,128)(2,1)S(1)}, bf16[4,256,128]{2,1,0:T(8,128)(2,1)S(1)}, u32[]{:S(2)}, u32[]{:S(2)}) collective-permute-start(bf16[4,256,128]{2,1,0:T(8,128)(2,1)S(1)} %pad_maximum_fusion.3), channel_id=1, source_target_pairs={{0,32},{32,64},{64,96},{96,0},{1,33},{33,65},{65,97},{97,1},{2,34}... | collective-permute-start | bytes 786440 | tf_op jit(solution)/shard_map/ppermute | solution.py:31
  51.3 13.2 %collective-permute-start.13 = (bf16[4,256,128]{2,1,0:T(8,128)(2,1)S(1)}, bf16[4,256,128]{2,1,0:T(8,128)(2,1)S(1)}, u32[]{:S(2)}, u32[]{:S(2)}) collective-permute-start(bf16[4,256,128]{2,1,0:T(8,128)(2,1)S(1)} %pad_maximum_fusion.3), channel_id=1, source_target_pairs={{0,64},{32,96},{64,0},{96,32},{1,65},{33,97},{65,1},{97,33},{2,66}... | collective-permute-start | bytes 786440 | tf_op jit(solution)/shard_map/ppermute | solution.py:31
  53.8 12.4 %collective-permute-start.14 = (bf16[4,256,128]{2,1,0:T(8,128)(2,1)S(1)}, bf16[4,256,128]{2,1,0:T(8,128)(2,1)S(1)}, u32[]{:S(2)}, u32[]{:S(2)}) collective-permute-start(bf16[4,256,128]{2,1,0:T(8,128)(2,1)S(1)} %pad_maximum_fusion.3), channel_id=1, source_target_pairs={{0,96},{32,0},{64,32},{96,64},{1,97},{33,1},{65,33},{97,65},{2,98}... | collective-permute-start | bytes 786440 | tf_op jit(solution)/shard_map/ppermute | solution.py:31
  55.4 27.5 %collective-permute-start = (bf16[2048,256]{1,0:T(8,128)(2,1)}, bf16[2048,256]{1,0:T(8,128)(2,1)S(1)}, u32[]{:S(2)}, u32[]{:S(2)}) collective-permute-start(bf16[2048,256]{1,0:T(8,128)(2,1)} %bitcast.10.refs_0_), channel_id=1, source_target_pairs={{0,1},{1,2},{2,3},{3,0},{4,5},{5,6},{6,7},{7,4},{8,9},{9,10},{10,1... | collective-permute-start | bytes 3145736 | tf_op jit(solution)/shard_map/ppermute | solution.py:31
  57.0 27.2 %collective-permute-start.2 = (bf16[2048,256]{1,0:T(8,128)(2,1)}, bf16[2048,256]{1,0:T(8,128)(2,1)S(1)}, u32[]{:S(2)}, u32[]{:S(2)}) collective-permute-start(bf16[2048,256]{1,0:T(8,128)(2,1)} %bitcast.10.refs_0_), channel_id=1, source_target_pairs={{0,3},{1,0},{2,1},{3,2},{4,7},{5,4},{6,5},{7,6},{8,11},{9,8},{10,9... | collective-permute-start | bytes 3145736 | tf_op jit(solution)/shard_map/ppermute | solution.py:31
  66.3 39.0 %collective-permute-start.16 = (bf16[16,256,128]{2,1,0:T(8,128)(2,1)S(1)}, bf16[16,256,128]{2,1,0:T(8,128)(2,1)S(1)}, u32[]{:S(2)}, u32[]{:S(2)}) collective-permute-start(bf16[16,256,128]{2,1,0:T(8,128)(2,1)S(1)} %bitcast.54), channel_id=1, source_target_pairs={{0,1},{1,2},{2,3},{3,0},{4,5},{5,6},{6,7},{7,4},{8,9},{9,10},{10,1... | collective-permute-start | bytes 3145736 | tf_op jit(solution)/shard_map/ppermute | solution.py:31
  68.0 43.0 %collective-permute-start.18 = (bf16[16,256,128]{2,1,0:T(8,128)(2,1)S(1)}, bf16[16,256,128]{2,1,0:T(8,128)(2,1)}, u32[]{:S(2)}, u32[]{:S(2)}) collective-permute-start(bf16[16,256,128]{2,1,0:T(8,128)(2,1)S(1)} %bitcast.55), channel_id=1, source_target_pairs={{0,3},{1,0},{2,1},{3,2},{4,7},{5,4},{6,5},{7,6},{8,11},{9,8},{10,9... | collective-permute-start | bytes 3145736 | tf_op jit(solution)/shard_map/ppermute | solution.py:31
  83.8 32.9 %collective-permute-start.1 = (bf16[1024,256]{1,0:T(8,128)(2,1)}, bf16[1024,256]{1,0:T(8,128)(2,1)}, u32[]{:S(2)}, u32[]{:S(2)}) collective-permute-start(bf16[1024,256]{1,0:T(8,128)(2,1)} %slice.94), channel_id=1, source_target_pairs={{0,1},{1,2},{2,3},{3,0},{4,5},{5,6},{6,7},{7,4},{8,9},{9,10},{10,1... | collective-permute-start | bytes 1572872 | tf_op jit(solution)/shard_map/ppermute | solution.py:31
  85.0 33.6 %collective-permute-start.3 = (bf16[1024,256]{1,0:T(8,128)(2,1)}, bf16[1024,256]{1,0:T(8,128)(2,1)S(1)}, u32[]{:S(2)}, u32[]{:S(2)}) collective-permute-start(bf16[1024,256]{1,0:T(8,128)(2,1)} %slice.95), channel_id=1, source_target_pairs={{0,3},{1,0},{2,1},{3,2},{4,7},{5,4},{6,5},{7,6},{8,11},{9,8},{10,9... | collective-permute-start | bytes 1572872 | tf_op jit(solution)/shard_map/ppermute | solution.py:31
  87.9 47.3 %collective-permute-start.7 = (bf16[2048,256]{1,0:T(8,128)(2,1)}, bf16[2048,256]{1,0:T(8,128)(2,1)}, u32[]{:S(2)}, u32[]{:S(2)}) collective-permute-start(bf16[2048,256]{1,0:T(8,128)(2,1)} %bitcast.10.refs_0_), channel_id=1, source_target_pairs={{0,16},{16,0},{1,17},{17,1},{2,18},{18,2},{3,19},{19,3},{4,20},{20... | collective-permute-start | bytes 3145736 | tf_op jit(solution)/shard_map/ppermute | solution.py:39
  106.2 18.1 %collective-permute-start.20 = (bf16[8,256,128]{2,1,0:T(8,128)(2,1)}, bf16[8,256,128]{2,1,0:T(8,128)(2,1)}, u32[]{:S(2)}, u32[]{:S(2)}) collective-permute-start(bf16[8,256,128]{2,1,0:T(8,128)(2,1)} %slice.96), channel_id=1, source_target_pairs={{0,1},{1,2},{2,3},{3,0},{4,5},{5,6},{6,7},{7,4},{8,9},{9,10},{10,1... | collective-permute-start | bytes 1572872 | tf_op jit(solution)/shard_map/ppermute | solution.py:31
  107.5 28.2 %all-to-all-start = ((bf16[16,128,128]{2,1,0:T(8,128)(2,1)}), bf16[16,128,128]{2,1,0:T(8,128)(2,1)S(1)}, u32[]{:S(2)}, u32[]{:S(2)}) async-start(bf16[16,128,128]{2,1,0:T(8,128)(2,1)} %bitcast_bitcast_fusion), calls=%async_computation | async-start | bytes 1048576 | tf_op jit(solution)/shard_map/all_to_all | solution.py:316
  111.1 37.1 %collective-permute-start.5 = (bf16[2048,256]{1,0:T(8,128)(2,1)}, bf16[2048,256]{1,0:T(8,128)(2,1)}, u32[]{:S(2)}, u32[]{:S(2)}) collective-permute-start(bf16[2048,256]{1,0:T(8,128)(2,1)} %copy-done.5), channel_id=1, source_target_pairs={{0,16},{16,0},{1,17},{17,1},{2,18},{18,2},{3,19},{19,3},{4,20},{20... | collective-permute-start | bytes 3145736 | tf_op jit(solution)/shard_map/ppermute | solution.py:39
  116.7 31.6 %collective-permute-start.6 = (bf16[2048,256]{1,0:T(8,128)(2,1)}, bf16[2048,256]{1,0:T(8,128)(2,1)}, u32[]{:S(2)}, u32[]{:S(2)}) collective-permute-start(bf16[2048,256]{1,0:T(8,128)(2,1)} %copy-done.7), channel_id=1, source_target_pairs={{0,16},{16,0},{1,17},{17,1},{2,18},{18,2},{3,19},{19,3},{4,20},{20... | collective-permute-start | bytes 3145736 | tf_op jit(solution)/shard_map/ppermute | solution.py:39
  118.6 14.7 %collective-permute-start.21 = (bf16[8,256,128]{2,1,0:T(8,128)(2,1)}, bf16[8,256,128]{2,1,0:T(8,128)(2,1)}, u32[]{:S(2)}, u32[]{:S(2)}) collective-permute-start(bf16[8,256,128]{2,1,0:T(8,128)(2,1)} %slice.97), channel_id=1, source_target_pairs={{0,3},{1,0},{2,1},{3,2},{4,7},{5,4},{6,5},{7,6},{8,11},{9,8},{10,9... | collective-permute-start | bytes 1572872 | tf_op jit(solution)/shard_map/ppermute | solution.py:31
  124.3 44.5 %collective-permute-start.4 = (bf16[2048,256]{1,0:T(8,128)(2,1)}, bf16[2048,256]{1,0:T(8,128)(2,1)}, u32[]{:S(2)}, u32[]{:S(2)}) collective-permute-start(bf16[2048,256]{1,0:T(8,128)(2,1)} %constant_dynamic-update-slice_fusion.refs_0_), channel_id=1, source_target_pairs={{0,16},{16,0},{1,17},{17,1},{2,18},{18,2},{3,19},{19,3},{4,20},{20... | collective-permute-start | bytes 3145736 | tf_op jit(solution)/shard_map/ppermute | solution.py:39
  133.3 65.1 %collective-permute-start.15 = (bf16[16,256,128]{2,1,0:T(8,128)(2,1)S(1)}, bf16[16,256,128]{2,1,0:T(8,128)(2,1)}, u32[]{:S(2)}, u32[]{:S(2)}) collective-permute-start(bf16[16,256,128]{2,1,0:T(8,128)(2,1)S(1)} %bitcast.56), channel_id=1, source_target_pairs={{0,16},{16,0},{1,17},{17,1},{2,18},{18,2},{3,19},{19,3},{4,20},{20... | collective-permute-start | bytes 3145736 | tf_op jit(solution)/shard_map/ppermute | solution.py:39
  135.2 63.1 %collective-permute-start.17 = (bf16[16,256,128]{2,1,0:T(8,128)(2,1)S(1)}, bf16[16,256,128]{2,1,0:T(8,128)(2,1)}, u32[]{:S(2)}, u32[]{:S(2)}) collective-permute-start(bf16[16,256,128]{2,1,0:T(8,128)(2,1)S(1)} %collective-permute-done.16.refs_2_), channel_id=1, source_target_pairs={{0,16},{16,0},{1,17},{17,1},{2,18},{18,2},{3,19},{19,3},{4,20},{20... | collective-permute-start | bytes 3145736 | tf_op jit(solution)/shard_map/ppermute | solution.py:39
  148.2 50.2 %collective-permute-start.19 = (bf16[16,256,128]{2,1,0:T(8,128)(2,1)}, bf16[16,256,128]{2,1,0:T(8,128)(2,1)}, u32[]{:S(2)}, u32[]{:S(2)}) collective-permute-start(bf16[16,256,128]{2,1,0:T(8,128)(2,1)} %collective-permute-done.18.refs_4_), channel_id=1, source_target_pairs={{0,16},{16,0},{1,17},{17,1},{2,18},{18,2},{3,19},{19,3},{4,20},{20... | collective-permute-start | bytes 3145736 | tf_op jit(solution)/shard_map/ppermute | solution.py:39
  148.3 50.1 %collective-permute-start.22 = (bf16[16,256,128]{2,1,0:T(8,128)(2,1)}, bf16[16,256,128]{2,1,0:T(8,128)(2,1)}, u32[]{:S(2)}, u32[]{:S(2)}) collective-permute-start(bf16[16,256,128]{2,1,0:T(8,128)(2,1)} %constant_dynamic-update-slice_fusion.2.refs_6_), channel_id=1, source_target_pairs={{0,16},{16,0},{1,17},{17,1},{2,18},{18,2},{3,19},{19,3},{4,20},{20... | collective-permute-start | bytes 3145736 | tf_op jit(solution)/shard_map/ppermute | solution.py:39
  182.5 15.8 %all-to-all-start.2 = ((bf16[16,128,128]{2,1,0:T(8,128)(2,1)}), bf16[16,128,128]{2,1,0:T(8,128)(2,1)S(1)}, u32[]{:S(2)}, u32[]{:S(2)}) async-start(bf16[16,128,128]{2,1,0:T(8,128)(2,1)} %bitcast.61), calls=%async_computation.2 | async-start | bytes 1048576 | tf_op jit(solution)/shard_map/all_to_all | solution.py:316
  203.7 14.2 %collective-permute-start.25 = (bf16[128,2048]{1,0:T(8,128)(2,1)S(1)}, bf16[128,2048]{1,0:T(8,128)(2,1)S(1)}, u32[]{:S(2)}, u32[]{:S(2)}) collective-permute-start(bf16[128,2048]{1,0:T(8,128)(2,1)S(1)} %get-tuple-element.23.refs_0_), channel_id=1, source_target_pairs={{0,1},{1,2},{2,3},{3,0},{4,5},{5,6},{6,7},{7,4},{8,9},{9,10},{10,1... | collective-permute-start | bytes 1572872 | tf_op jit(solution)/shard_map/ppermute | solution.py:31
  204.0 14.0 %collective-permute-start.26 = (bf16[128,2048]{1,0:T(8,128)(2,1)S(1)}, bf16[128,2048]{1,0:T(8,128)(2,1)S(1)}, u32[]{:S(2)}, u32[]{:S(2)}) collective-permute-start(bf16[128,2048]{1,0:T(8,128)(2,1)S(1)} %get-tuple-element.23.refs_0_), channel_id=1, source_target_pairs={{0,3},{1,0},{2,1},{3,2},{4,7},{5,4},{6,5},{7,6},{8,11},{9,8},{10,9... | collective-permute-start | bytes 1572872 | tf_op jit(solution)/shard_map/ppermute | solution.py:31
  226.5 17.3 %collective-permute-start.23 = (bf16[128,2048]{1,0:T(8,128)(2,1)S(1)}, bf16[128,2048]{1,0:T(8,128)(2,1)S(1)}, u32[]{:S(2)}, u32[]{:S(2)}) collective-permute-start(bf16[128,2048]{1,0:T(8,128)(2,1)S(1)} %get-tuple-element.23.refs_0_), channel_id=1, source_target_pairs={{0,16},{16,0},{1,17},{17,1},{2,18},{18,2},{3,19},{19,3},{4,20},{20... | collective-permute-start | bytes 1572872 | tf_op jit(solution)/shard_map/ppermute | solution.py:39
  239.8 10.4 %collective-permute-start.29 = (bf16[256,2048]{1,0:T(8,128)(2,1)S(1)}, bf16[256,2048]{1,0:T(8,128)(2,1)S(1)}, u32[]{:S(2)}, u32[]{:S(2)}) collective-permute-start(bf16[256,2048]{1,0:T(8,128)(2,1)S(1)} %slice.102), channel_id=1, source_target_pairs={{0,16},{16,0},{1,17},{17,1},{2,18},{18,2},{3,19},{19,3},{4,20},{20... | collective-permute-start | bytes 3145736 | tf_op jit(solution)/shard_map/ppermute | solution.py:39
  253.9 10.5 %collective-permute-start.36 = (bf16[64,2048]{1,0:T(8,128)(2,1)S(1)}, bf16[64,2048]{1,0:T(8,128)(2,1)S(1)}, u32[]{:S(2)}, u32[]{:S(2)}) collective-permute-start(bf16[64,2048]{1,0:T(8,128)(2,1)S(1)} %fusion.2), channel_id=1, source_target_pairs={{0,1},{1,2},{2,3},{3,0},{4,5},{5,6},{6,7},{7,4},{8,9},{9,10},{10,1... | collective-permute-start | bytes 786440 | tf_op jit(solution)/shard_map/ppermute | solution.py:31
  257.2 10.8 %collective-permute-start.38 = (bf16[64,2048]{1,0:T(8,128)(2,1)S(1)}, bf16[64,2048]{1,0:T(8,128)(2,1)S(1)}, u32[]{:S(2)}, u32[]{:S(2)}) collective-permute-start(bf16[64,2048]{1,0:T(8,128)(2,1)S(1)} %slice.133), channel_id=1, source_target_pairs={{0,1},{1,2},{2,3},{3,0},{4,5},{5,6},{6,7},{7,4},{8,9},{9,10},{10,1... | collective-permute-start | bytes 786440 | tf_op jit(solution)/shard_map/ppermute | solution.py:31
  (27 other events, 375.7 us)
Sparse Core Ops, SparseCore 0:
  11.4 97.7 all-gather.1

commit v4 on v3

--- a/solution.py
+++ b/solution.py
@@ -59,7 +59,7 @@
     )(keys, values)
 
 
-def attend_body(first, last, n_pairs, where_ref, q_ref, *refs):
+def attend_body(first, last, n_pairs, zs, where_ref, q_ref, *refs):
     kv_refs = refs[: 2 * n_pairs]
     refs = refs[2 * n_pairs :]
     given = () if first else refs[:3]
@@ -84,7 +84,7 @@
         rows = rows_of(zq)
         return pltpu.make_async_copy(held[i].at[rows], kept[i].at[rows], left.at[i, zq])
 
-    for zq in range(Z):
+    for zq in range(*zs):
         for i in range(len(given)):
             arriving(i, zq).start()
     c_q = where_ref[0]
@@ -150,18 +150,18 @@
         lax.fori_loop(0, zq + 1, per_key, 0)
         if last:
             total = jnp.sum(l_s[rows, :], axis=1, keepdims=True)
-            o_ref[rows, :] = (a_s[rows, :] / total).astype(BF16)
+            o_ref[rows_of(zq - zs[0]), :] = (a_s[rows, :] / total).astype(BF16)
         for i in range(len(kept)):
             leaving(i, zq).start()
         return 0
 
-    lax.fori_loop(0, Z, per_z, 0)
-    for zq in range(Z):
+    lax.fori_loop(*zs, per_z, 0)
+    for zq in range(*zs):
         for i in range(len(kept)):
             leaving(i, zq).wait()
 
 
-def attend(where, q, chunks, state, last):
+def attend(where, q, chunks, state, last, zs=(0, Z)):
     n_pairs = len(chunks) // 2
     first = state is None
     wide = pltpu.HBM((LOCAL, 128), F32)
@@ -171,10 +171,11 @@
     if not first:
         args += [pltpu.with_memory_space_constraint(a, pltpu.HBM) for a in state]
     n_vmem = 1 + len(chunks)
-    pairs = LOCAL * LOCAL * n_pairs * 5 // 4
+    n_rows = (zs[1] - zs[0]) * BLOCK
+    pairs = sum(range(1 + zs[0], 1 + zs[1])) * BLOCK * BLOCK * 2 * n_pairs
     return pl.pallas_call(
-        functools.partial(attend_body, first, last, n_pairs),
-        out_shape=jax.ShapeDtypeStruct((LOCAL, HEAD_DIM), BF16) if last else [wide] * 3,
+        functools.partial(attend_body, first, last, n_pairs, zs),
+        out_shape=jax.ShapeDtypeStruct((n_rows, HEAD_DIM), BF16) if last else [wide] * 3,
         in_specs=[pl.BlockSpec(memory_space=pltpu.SMEM)]
         + [vmem] * n_vmem
         + [hbm] * (len(args) - 1 - n_vmem),
@@ -342,7 +343,9 @@
     state = attend(where(0), q, [kv, kv_c], None, False)
     far = gather_far(before[0], after[0])
     state = attend(where(-1, 1), q, [*before, *after], state, False)
-    attn = attend(where(2), q, far, state, True)
+    low = attend(where(2), q, far, state, True, (0, Z - 1))
+    high = attend(where(2), q, far, state, True, (Z - 1, Z))
+    attn = jnp.concatenate([low, high], axis=0)
 
     wo_c, wo_before, wo_after = gather_near(wo)
     wo_far = gather_far(wo_before[0], wo_after[0])

time: 277 us -> 278 us (level)
    unnamed x33 -> x25, local copies, waits for them, and re-layouts: 4.61 us -> 0.99 us
    pallas_call x3 -> x4, Pallas kernels: 45.4 us -> 46.5 us  [attend(): pl.pallas_call(functools.partial(attend_body, first, last, n_pairs, zs),...]
  transfers between devices with their start and end apart: 44 -> 44, of which waited for: 19 -> 21; matrix products, arithmetic and copies ran while one was open for 5% -> 5% of each run, Pallas kernels for 22% -> 23%
where the time goes in v4:
time: 278 us; the launch traced here: 277 us
  waiting for transfers between devices  117 us (42%)
  Pallas kernels  68.3 us (25%)
  starting transfers between devices  60.5 us (22%)
  between operations  14.6 us (5%)
  local copies, waits for them, and re-layouts  11.8 us (4%)
  other arithmetic  5.23 us (2%)
    ppermute x24, waiting for transfers between devices, along(): return lax.ppermute(array, axis, [(i, (i + step) % 4) for i in range(4)])  102 us
    pallas_call x4, Pallas kernels, attend(): pl.pallas_call(functools.partial(attend_body, first, last, n_pairs, zs),...  46.5 us
    ppermute x24, starting transfers between devices, along(): return lax.ppermute(array, axis, [(i, (i + step) % 4) for i in range(4)])  42 us
    all_to_all x3, starting transfers between devices, regroup(): lax.all_to_all(array, ('z', 'x'), split_axis=0, concat_axis=0, tiled=True)  15.2 us
    pallas_call x3, Pallas kernels, ffn(): pl.pallas_call(functools.partial(ffn_body, n), out_shape=jax.ShapeDtypeSt...  15.1 us
    all_to_all x3, waiting for transfers between devices, regroup(): lax.all_to_all(array, ('z', 'x'), split_axis=0, concat_axis=0, tiled=True)  12.1 us
    pallas_call x1, Pallas kernels, project(): pl.pallas_call(project_body, out_shape=[out, out], in_specs=[pl.BlockSpec...  5.59 us
  transfers between devices with their start and end apart: 44, of which 21 were waited for; matrix products, arithmetic and copies ran while one was open for 5% of the time, Pallas kernels for 23%

profile of v4, /device:TPU:0, one launch (start us, length us, event | category | flops | bytes accessed | tf_op | source)
XLA Modules:
  0.0 277.2 jit_solution(9843122746494736685)
XLA Ops:
  12.4 8.0 %all-to-all-start.1 = ((bf16[16,128,256]{2,1,0:T(8,128)(2,1)}), bf16[16,128,256]{2,1,0:T(8,128)(2,1)}, u32[]{:S(2)}, u32[]{:S(2)}) async-start(bf16[16,128,256]{2,1,0:T(8,128)(2,1)} %shard_map.104), calls=%async_computation.1 | async-start | bytes 2097152 | tf_op jit(solution)/shard_map/all_to_all | solution.py:317
  22.4 2.7 collective-permute-start.10
  26.6 17.9 %collective-permute-done.9 = bf16[256,128]{1,0:T(8,128)(2,1)S(1)} collective-permute-done((bf16[256,128]{1,0:T(8,128)(2,1)S(1)}, bf16[256,128]{1,0:T(8,128)(2,1)S(1)}, u32[]{:S(2)}, u32[]{:S(2)}) %collective-permute-start.9) | collective-permute-done | bytes 65568 | tf_op jit(solution)/shard_map/ppermute | solution.py:31
  44.5 3.2 %collective-permute-done.10 = bf16[256,128]{1,0:T(8,128)(2,1)S(1)} collective-permute-done((bf16[256,128]{1,0:T(8,128)(2,1)S(1)}, bf16[256,128]{1,0:T(8,128)(2,1)S(1)}, u32[]{:S(2)}, u32[]{:S(2)}) %collective-permute-start.10) | collective-permute-done | bytes 65568 | tf_op jit(solution)/shard_map/ppermute | solution.py:31
  48.0 3.2 %collective-permute-start.12 = (bf16[4,256,128]{2,1,0:T(8,128)(2,1)S(1)}, bf16[4,256,128]{2,1,0:T(8,128)(2,1)S(1)}, u32[]{:S(2)}, u32[]{:S(2)}) collective-permute-start(bf16[4,256,128]{2,1,0:T(8,128)(2,1)S(1)} %pad_maximum_fusion.4), channel_id=1, source_target_pairs={{0,32},{32,64},{64,96},{96,0},{1,33},{33,65},{65,97},{97,1},{2,34}... | collective-permute-start | bytes 786440 | tf_op jit(solution)/shard_map/ppermute | solution.py:31
  59.4 4.9 %collective-permute-done.13 = bf16[4,256,128]{2,1,0:T(8,128)(2,1)S(1)} collective-permute-done((bf16[4,256,128]{2,1,0:T(8,128)(2,1)S(1)}, bf16[4,256,128]{2,1,0:T(8,128)(2,1)S(1)}, u32[]{:S(2)}, u32[]{:S(2)}) %collective-permute-start.13) | collective-permute-done | bytes 262176 | tf_op jit(solution)/shard_map/ppermute | solution.py:31
  69.8 13.2 %collective-permute-done.refs_0_ = bf16[2048,256]{1,0:T(8,128)(2,1)} collective-permute-done((bf16[2048,256]{1,0:T(8,128)(2,1)}, bf16[2048,256]{1,0:T(8,128)(2,1)}, u32[]{:S(2)}, u32[]{:S(2)}) %collective-permute-start) | collective-permute-done | bytes 1048608 | tf_op jit(solution)/shard_map/ppermute | solution.py:31
  87.1 2.8 %collective-permute-start.3 = (bf16[1024,256]{1,0:T(8,128)(2,1)}, bf16[1024,256]{1,0:T(8,128)(2,1)S(1)}, u32[]{:S(2)}, u32[]{:S(2)}) collective-permute-start(bf16[1024,256]{1,0:T(8,128)(2,1)} %slice.95), channel_id=1, source_target_pairs={{0,3},{1,0},{2,1},{3,2},{4,7},{5,4},{6,5},{7,6},{8,11},{9,8},{10,9... | collective-permute-start | bytes 1572872 | tf_op jit(solution)/shard_map/ppermute | solution.py:31
  89.9 15.5 %collective-permute-done.16.refs_2_ = bf16[16,256,128]{2,1,0:T(8,128)(2,1)} collective-permute-done((bf16[16,256,128]{2,1,0:T(8,128)(2,1)S(1)}, bf16[16,256,128]{2,1,0:T(8,128)(2,1)}, u32[]{:S(2)}, u32[]{:S(2)}) %collective-permute-start.16) | collective-permute-done | bytes 1048608 | tf_op jit(solution)/shard_map/ppermute | solution.py:31
  108.6 3.6 %all-to-all-start = ((bf16[16,128,128]{2,1,0:T(8,128)(2,1)}), bf16[16,128,128]{2,1,0:T(8,128)(2,1)S(1)}, u32[]{:S(2)}, u32[]{:S(2)}) async-start(bf16[16,128,128]{2,1,0:T(8,128)(2,1)} %bitcast_bitcast_fusion), calls=%async_computation | async-start | bytes 1048576 | tf_op jit(solution)/shard_map/all_to_all | solution.py:317
  112.3 4.2 %collective-permute-done.1 = bf16[1024,256]{1,0:T(8,128)(2,1)S(1)} collective-permute-done((bf16[1024,256]{1,0:T(8,128)(2,1)}, bf16[1024,256]{1,0:T(8,128)(2,1)S(1)}, u32[]{:S(2)}, u32[]{:S(2)}) %collective-permute-start.1) | collective-permute-done | bytes 524320 | tf_op jit(solution)/shard_map/ppermute | solution.py:31
  123.8 9.3 %collective-permute-done.21 = bf16[8,256,128]{2,1,0:T(8,128)(2,1)} collective-permute-done((bf16[8,256,128]{2,1,0:T(8,128)(2,1)}, bf16[8,256,128]{2,1,0:T(8,128)(2,1)}, u32[]{:S(2)}, u32[]{:S(2)}) %collective-permute-start.21) | collective-permute-done | bytes 524320 | tf_op jit(solution)/shard_map/ppermute | solution.py:31
  135.5 12.3 %shard_map.105 = (f32[2048,128]{1,0:T(8,128)}, f32[2048,128]{1,0:T(8,128)}, f32[2048,128]{1,0:T(8,128)}) custom-call(s32[3]{0:T(128)S(1)} %pad_add_fusion.3.where_ref, bf16[2048,128]{1,0:T(8,128)(2,1)S(1)} %bitcast.54, bf16[2048,256]{1,0:T(8,128)(2,1)} %bitcast.10.refs_0_, bf16[2048,256]{1,0:T(8,128)(2,1)} %collective-permute-done.7.refs_1_), custom_call_target="tpu_custom_call" | custom-call | flops 2684354560 | bytes 2097152 | tf_op jit(solution)/shard_map/pallas_call | solution.py:176
  148.4 20.4 %shard_map.106 = (f32[2048,128]{1,0:T(8,128)}, f32[2048,128]{1,0:T(8,128)}, f32[2048,128]{1,0:T(8,128)}) custom-call(s32[4]{0:T(128)S(1)} %pad_add_fusion.2.where_ref, bf16[2048,128]{1,0:T(8,128)(2,1)S(1)} %bitcast.55, bf16[2048,256]{1,0:T(8,128)(2,1)} %collective-permute-done.refs_0_, bf16[2048,256]{1,0:T(8,128)(2,1)} %collective-permute-done.5.refs_1_, ...), custom_call_target="tpu_custom_call" | custom-call | flops 5368709120 | bytes 4194304 | tf_op jit(solution)/shard_map/pallas_call | solution.py:176
  168.9 5.8 %shard_map.108 = bf16[512,128]{1,0:T(8,128)(2,1)S(1)} custom-call(s32[3]{0:T(128)S(1)} %pad_add_fusion.where_ref, bf16[2048,128]{1,0:T(8,128)(2,1)S(1)} %bitcast.56, bf16[2048,256]{1,0:T(8,128)(2,1)S(1)} %constant_dynamic-update-slice_fusion.refs_0_, bf16[2048,256]{1,0:T(8,128)(2,1)S(1)} %collective-permute-done.4.refs_1_, ...), custom_call_target="tpu_custom_call" | custom-call | flops 1073741824 | bytes 2097152 | tf_op jit(solution)/shard_map/pallas_call | solution.py:176
  174.6 8.0 %shard_map.107 = bf16[1536,128]{1,0:T(8,128)(2,1)S(1)} custom-call(s32[3]{0:T(128)S(1)} %pad_add_fusion.where_ref, bf16[2048,128]{1,0:T(8,128)(2,1)S(1)} %bitcast.57, bf16[2048,256]{1,0:T(8,128)(2,1)S(1)} %constant_dynamic-update-slice_fusion.refs_0_, bf16[2048,256]{1,0:T(8,128)(2,1)S(1)} %collective-permute-done.4.refs_1_, ...), custom_call_target="tpu_custom_call" | custom-call | flops 1610612736 | bytes 2097152 | tf_op jit(solution)/shard_map/pallas_call | solution.py:176
  183.5 3.6 %all-to-all-start.2 = ((bf16[16,128,128]{2,1,0:T(8,128)(2,1)}), bf16[16,128,128]{2,1,0:T(8,128)(2,1)S(1)}, u32[]{:S(2)}, u32[]{:S(2)}) async-start(bf16[16,128,128]{2,1,0:T(8,128)(2,1)} %bitcast.11), calls=%async_computation.2 | async-start | bytes 1048576 | tf_op jit(solution)/shard_map/all_to_all | solution.py:317
  187.2 12.1 %all-to-all-done.2.attn_ref = bf16[16,128,128]{2,1,0:T(8,128)(2,1)S(1)} async-done(((bf16[16,128,128]{2,1,0:T(8,128)(2,1)}), bf16[16,128,128]{2,1,0:T(8,128)(2,1)S(1)}, u32[]{:S(2)}, u32[]{:S(2)}) %all-to-all-start.2) | async-done | bytes 524320 | tf_op jit(solution)/shard_map/all_to_all | solution.py:317
  199.3 5.6 %shard_map.109 = (bf16[128,2048]{1,0:T(8,128)(2,1)}, bf16[128,2048]{1,0:T(8,128)(2,1)S(1)}) custom-call(s32[7]{0:T(128)S(1)} %stack.107.where_ref, bf16[16,128,128]{2,1,0:T(8,128)(2,1)S(1)} %all-to-all-done.2.attn_ref, bf16[128,2048]{1,0:T(8,128)(2,1)S(1)} %copy-done.5, bf16[1,2048]{1,0:T(2,128)(2,1)S(1)} %reshape.41.gain_ref, ...), custom_call_target="tpu_custom_call" | custom-call | flops 1073741824 | bytes 8388608 | tf_op jit(solution)/shard_map/pallas_call | solution.py:230
  208.2 10.9 %collective-permute-done.25.refs_0_ = bf16[128,2048]{1,0:T(8,128)(2,1)S(1)} collective-permute-done((bf16[128,2048]{1,0:T(8,128)(2,1)S(1)}, bf16[128,2048]{1,0:T(8,128)(2,1)S(1)}, u32[]{:S(2)}, u32[]{:S(2)}) %collective-permute-start.25) | collective-permute-done | bytes 524320 | tf_op jit(solution)/shard_map/ppermute | solution.py:31
  219.3 3.3 %collective-permute-start.31 = (bf16[64,2048]{1,0:T(8,128)(2,1)S(1)}, bf16[64,2048]{1,0:T(8,128)(2,1)S(1)}, u32[]{:S(2)}, u32[]{:S(2)}) collective-permute-start(bf16[64,2048]{1,0:T(8,128)(2,1)S(1)} %slice.106), channel_id=1, source_target_pairs={{0,3},{1,0},{2,1},{3,2},{4,7},{5,4},{6,5},{7,6},{8,11},{9,8},{10,9... | collective-permute-start | bytes 786440 | tf_op jit(solution)/shard_map/ppermute | solution.py:31
  222.6 4.4 %collective-permute-done.30 = bf16[64,2048]{1,0:T(8,128)(2,1)S(1)} collective-permute-done((bf16[64,2048]{1,0:T(8,128)(2,1)S(1)}, bf16[64,2048]{1,0:T(8,128)(2,1)S(1)}, u32[]{:S(2)}, u32[]{:S(2)}) %collective-permute-start.30) | collective-permute-done | bytes 262176 | tf_op jit(solution)/shard_map/ppermute | solution.py:31
  229.0 3.7 %shard_map.112 = bf16[256,2048]{1,0:T(8,128)(2,1)S(1)} custom-call(bf16[16,3,2,224,256]{4,3,2,1,0:T(8,128)(2,1)S(1)} %bitcast.51, bf16[128,2048]{1,0:T(8,128)(2,1)S(1)} %constant_dynamic-update-slice_fusion.4.refs_0_, bf16[128,2048]{1,0:T(8,128)(2,1)S(1)} %collective-permute-done.32.refs_1_), custom_call_target="tpu_custom_call" | custom-call | flops 2818572288 | bytes 11010048 | tf_op jit(solution)/shard_map/pallas_call | solution.py:276
  233.2 7.6 %shard_map.111 = bf16[512,2048]{1,0:T(8,128)(2,1)S(1)} custom-call(bf16[16,3,2,224,256]{4,3,2,1,0:T(8,128)(2,1)S(1)} %bitcast.52, bf16[128,2048]{1,0:T(8,128)(2,1)S(1)} %collective-permute-done.25.refs_0_, bf16[128,2048]{1,0:T(8,128)(2,1)S(1)} %collective-permute-done.26.refs_1_, bf16[128,2048]{1,0:T(8,128)(2,1)S(1)} %collective-permute-done.27.refs_2_, ...), custom_call_target="tpu_custom_call" | custom-call | flops 5637144576 | bytes 11010048 | tf_op jit(solution)/shard_map/pallas_call | solution.py:276
  241.7 3.2 %collective-permute-start.35 = (bf16[64,2048]{1,0:T(8,128)(2,1)S(1)}, bf16[64,2048]{1,0:T(8,128)(2,1)S(1)}, u32[]{:S(2)}, u32[]{:S(2)}) collective-permute-start(bf16[64,2048]{1,0:T(8,128)(2,1)S(1)} %get-tuple-element.32), channel_id=1, source_target_pairs={{0,3},{1,0},{2,1},{3,2},{4,7},{5,4},{6,5},{7,6},{8,11},{9,8},{10,9... | collective-permute-start | bytes 786440 | tf_op jit(solution)/shard_map/ppermute | solution.py:31
  245.0 3.8 %shard_map.110 = bf16[256,2048]{1,0:T(8,128)(2,1)S(1)} custom-call(bf16[16,3,2,224,256]{4,3,2,1,0:T(8,128)(2,1)S(1)} %bitcast.53, bf16[128,2048]{1,0:T(8,128)(2,1)S(1)} %get-tuple-element.23.refs_0_, bf16[128,2048]{1,0:T(8,128)(2,1)S(1)} %collective-permute-done.23.refs_1_), custom_call_target="tpu_custom_call" | custom-call | flops 2818572288 | bytes 11010048 | tf_op jit(solution)/shard_map/pallas_call | solution.py:276
  248.9 2.6 collective-permute-done.34
  252.0 3.1 %collective-permute-start.39 = (bf16[64,2048]{1,0:T(8,128)(2,1)S(1)}, bf16[64,2048]{1,0:T(8,128)(2,1)S(1)}, u32[]{:S(2)}, u32[]{:S(2)}) collective-permute-start(bf16[64,2048]{1,0:T(8,128)(2,1)S(1)} %fusion.1), channel_id=1, source_target_pairs={{0,3},{1,0},{2,1},{3,2},{4,7},{5,4},{6,5},{7,6},{8,11},{9,8},{10,9... | collective-permute-start | bytes 786440 | tf_op jit(solution)/shard_map/ppermute | solution.py:31
  255.3 3.2 %collective-permute-start.37 = (bf16[64,2048]{1,0:T(8,128)(2,1)S(1)}, bf16[64,2048]{1,0:T(8,128)(2,1)S(1)}, u32[]{:S(2)}, u32[]{:S(2)}) collective-permute-start(bf16[64,2048]{1,0:T(8,128)(2,1)S(1)} %slice.134), channel_id=1, source_target_pairs={{0,3},{1,0},{2,1},{3,2},{4,7},{5,4},{6,5},{7,6},{8,11},{9,8},{10,9... | collective-permute-start | bytes 786440 | tf_op jit(solution)/shard_map/ppermute | solution.py:31
  258.6 3.1 %collective-permute-done.39 = bf16[64,2048]{1,0:T(8,128)(2,1)S(1)} collective-permute-done((bf16[64,2048]{1,0:T(8,128)(2,1)S(1)}, bf16[64,2048]{1,0:T(8,128)(2,1)S(1)}, u32[]{:S(2)}, u32[]{:S(2)}) %collective-permute-start.39) | collective-permute-done | bytes 262176 | tf_op jit(solution)/shard_map/ppermute | solution.py:31
  261.8 3.9 %collective-permute-done.36 = bf16[64,2048]{1,0:T(8,128)(2,1)S(1)} collective-permute-done((bf16[64,2048]{1,0:T(8,128)(2,1)S(1)}, bf16[64,2048]{1,0:T(8,128)(2,1)S(1)}, u32[]{:S(2)}, u32[]{:S(2)}) %collective-permute-start.36) | collective-permute-done | bytes 262176 | tf_op jit(solution)/shard_map/ppermute | solution.py:31
  265.7 3.6 %collective-permute-done.38 = bf16[64,2048]{1,0:T(8,128)(2,1)S(1)} collective-permute-done((bf16[64,2048]{1,0:T(8,128)(2,1)S(1)}, bf16[64,2048]{1,0:T(8,128)(2,1)S(1)}, u32[]{:S(2)}, u32[]{:S(2)}) %collective-permute-start.38) | collective-permute-done | bytes 262176 | tf_op jit(solution)/shard_map/ppermute | solution.py:31
  (126 shorter events, 49.8 us)
Async XLA Ops:
  7.2 192.1 %all-gather.2.cloned.1.call-start = ((), (), s32[]{:S(2)}) async-start(), calls=%async_computation.3 | async-start | bytes 11698176 | tf_op jit(solution)/shard_map/all_gather | solution.py:337
  12.4 42.9 %all-to-all-start.1 = ((bf16[16,128,256]{2,1,0:T(8,128)(2,1)}), bf16[16,128,256]{2,1,0:T(8,128)(2,1)}, u32[]{:S(2)}, u32[]{:S(2)}) async-start(bf16[16,128,256]{2,1,0:T(8,128)(2,1)} %shard_map.104), calls=%async_computation.1 | async-start | bytes 2097152 | tf_op jit(solution)/shard_map/all_to_all | solution.py:317
  20.5 24.0 %collective-permute-start.9 = (bf16[256,128]{1,0:T(8,128)(2,1)S(1)}, bf16[256,128]{1,0:T(8,128)(2,1)S(1)}, u32[]{:S(2)}, u32[]{:S(2)}) collective-permute-start(bf16[256,128]{1,0:T(8,128)(2,1)S(1)} %copy-done.9), channel_id=1, source_target_pairs={{0,4},{4,8},{8,12},{12,0},{1,5},{5,9},{9,13},{13,1},{2,6},{6,10},{... | collective-permute-start | bytes 196616 | tf_op jit(solution)/shard_map/ppermute | solution.py:31
  22.4 25.3 %collective-permute-start.10 = (bf16[256,128]{1,0:T(8,128)(2,1)S(1)}, bf16[256,128]{1,0:T(8,128)(2,1)S(1)}, u32[]{:S(2)}, u32[]{:S(2)}) collective-permute-start(bf16[256,128]{1,0:T(8,128)(2,1)S(1)} %copy-done.9), channel_id=1, source_target_pairs={{0,8},{4,12},{8,0},{12,4},{1,9},{5,13},{9,1},{13,5},{2,10},{6,14},... | collective-permute-start | bytes 196616 | tf_op jit(solution)/shard_map/ppermute | solution.py:31
  25.1 22.8 %collective-permute-start.11 = (bf16[256,128]{1,0:T(8,128)(2,1)S(1)}, bf16[256,128]{1,0:T(8,128)(2,1)S(1)}, u32[]{:S(2)}, u32[]{:S(2)}) collective-permute-start(bf16[256,128]{1,0:T(8,128)(2,1)S(1)} %copy-done.9), channel_id=1, source_target_pairs={{0,12},{4,0},{8,4},{12,8},{1,13},{5,1},{9,5},{13,9},{2,14},{6,2},{... | collective-permute-start | bytes 196616 | tf_op jit(solution)/shard_map/ppermute | solution.py:31
  48.0 11.4 %collective-permute-start.12 = (bf16[4,256,128]{2,1,0:T(8,128)(2,1)S(1)}, bf16[4,256,128]{2,1,0:T(8,128)(2,1)S(1)}, u32[]{:S(2)}, u32[]{:S(2)}) collective-permute-start(bf16[4,256,128]{2,1,0:T(8,128)(2,1)S(1)} %pad_maximum_fusion.4), channel_id=1, source_target_pairs={{0,32},{32,64},{64,96},{96,0},{1,33},{33,65},{65,97},{97,1},{2,34}... | collective-permute-start | bytes 786440 | tf_op jit(solution)/shard_map/ppermute | solution.py:31
  51.2 13.0 %collective-permute-start.13 = (bf16[4,256,128]{2,1,0:T(8,128)(2,1)S(1)}, bf16[4,256,128]{2,1,0:T(8,128)(2,1)S(1)}, u32[]{:S(2)}, u32[]{:S(2)}) collective-permute-start(bf16[4,256,128]{2,1,0:T(8,128)(2,1)S(1)} %pad_maximum_fusion.4), channel_id=1, source_target_pairs={{0,64},{32,96},{64,0},{96,32},{1,65},{33,97},{65,1},{97,33},{2,66}... | collective-permute-start | bytes 786440 | tf_op jit(solution)/shard_map/ppermute | solution.py:31
  53.7 12.4 %collective-permute-start.14 = (bf16[4,256,128]{2,1,0:T(8,128)(2,1)S(1)}, bf16[4,256,128]{2,1,0:T(8,128)(2,1)S(1)}, u32[]{:S(2)}, u32[]{:S(2)}) collective-permute-start(bf16[4,256,128]{2,1,0:T(8,128)(2,1)S(1)} %pad_maximum_fusion.4), channel_id=1, source_target_pairs={{0,96},{32,0},{64,32},{96,64},{1,97},{33,1},{65,33},{97,65},{2,98}... | collective-permute-start | bytes 786440 | tf_op jit(solution)/shard_map/ppermute | solution.py:31
  55.4 27.6 %collective-permute-start = (bf16[2048,256]{1,0:T(8,128)(2,1)}, bf16[2048,256]{1,0:T(8,128)(2,1)}, u32[]{:S(2)}, u32[]{:S(2)}) collective-permute-start(bf16[2048,256]{1,0:T(8,128)(2,1)} %bitcast.10.refs_0_), channel_id=1, source_target_pairs={{0,1},{1,2},{2,3},{3,0},{4,5},{5,6},{6,7},{7,4},{8,9},{9,10},{10,1... | collective-permute-start | bytes 3145736 | tf_op jit(solution)/shard_map/ppermute | solution.py:31
  56.9 28.2 %collective-permute-start.2 = (bf16[2048,256]{1,0:T(8,128)(2,1)}, bf16[2048,256]{1,0:T(8,128)(2,1)}, u32[]{:S(2)}, u32[]{:S(2)}) collective-permute-start(bf16[2048,256]{1,0:T(8,128)(2,1)} %bitcast.10.refs_0_), channel_id=1, source_target_pairs={{0,3},{1,0},{2,1},{3,2},{4,7},{5,4},{6,5},{7,6},{8,11},{9,8},{10,9... | collective-permute-start | bytes 3145736 | tf_op jit(solution)/shard_map/ppermute | solution.py:31
  66.2 39.1 %collective-permute-start.16 = (bf16[16,256,128]{2,1,0:T(8,128)(2,1)S(1)}, bf16[16,256,128]{2,1,0:T(8,128)(2,1)}, u32[]{:S(2)}, u32[]{:S(2)}) collective-permute-start(bf16[16,256,128]{2,1,0:T(8,128)(2,1)S(1)} %bitcast.58), channel_id=1, source_target_pairs={{0,1},{1,2},{2,3},{3,0},{4,5},{5,6},{6,7},{7,4},{8,9},{9,10},{10,1... | collective-permute-start | bytes 3145736 | tf_op jit(solution)/shard_map/ppermute | solution.py:31
  67.9 44.3 %collective-permute-start.18 = (bf16[16,256,128]{2,1,0:T(8,128)(2,1)S(1)}, bf16[16,256,128]{2,1,0:T(8,128)(2,1)}, u32[]{:S(2)}, u32[]{:S(2)}) collective-permute-start(bf16[16,256,128]{2,1,0:T(8,128)(2,1)S(1)} %bitcast.59), channel_id=1, source_target_pairs={{0,3},{1,0},{2,1},{3,2},{4,7},{5,4},{6,5},{7,6},{8,11},{9,8},{10,9... | collective-permute-start | bytes 3145736 | tf_op jit(solution)/shard_map/ppermute | solution.py:31
  84.8 31.7 %collective-permute-start.1 = (bf16[1024,256]{1,0:T(8,128)(2,1)}, bf16[1024,256]{1,0:T(8,128)(2,1)S(1)}, u32[]{:S(2)}, u32[]{:S(2)}) collective-permute-start(bf16[1024,256]{1,0:T(8,128)(2,1)} %slice.94), channel_id=1, source_target_pairs={{0,1},{1,2},{2,3},{3,0},{4,5},{5,6},{6,7},{7,4},{8,9},{9,10},{10,1... | collective-permute-start | bytes 1572872 | tf_op jit(solution)/shard_map/ppermute | solution.py:31
  87.1 31.4 %collective-permute-start.3 = (bf16[1024,256]{1,0:T(8,128)(2,1)}, bf16[1024,256]{1,0:T(8,128)(2,1)S(1)}, u32[]{:S(2)}, u32[]{:S(2)}) collective-permute-start(bf16[1024,256]{1,0:T(8,128)(2,1)} %slice.95), channel_id=1, source_target_pairs={{0,3},{1,0},{2,1},{3,2},{4,7},{5,4},{6,5},{7,6},{8,11},{9,8},{10,9... | collective-permute-start | bytes 1572872 | tf_op jit(solution)/shard_map/ppermute | solution.py:31
  89.9 45.1 %collective-permute-start.7 = (bf16[2048,256]{1,0:T(8,128)(2,1)}, bf16[2048,256]{1,0:T(8,128)(2,1)}, u32[]{:S(2)}, u32[]{:S(2)}) collective-permute-start(bf16[2048,256]{1,0:T(8,128)(2,1)} %bitcast.10.refs_0_), channel_id=1, source_target_pairs={{0,16},{16,0},{1,17},{17,1},{2,18},{18,2},{3,19},{19,3},{4,20},{20... | collective-permute-start | bytes 3145736 | tf_op jit(solution)/shard_map/ppermute | solution.py:39
  107.3 15.5 %collective-permute-start.20 = (bf16[8,256,128]{2,1,0:T(8,128)(2,1)}, bf16[8,256,128]{2,1,0:T(8,128)(2,1)S(1)}, u32[]{:S(2)}, u32[]{:S(2)}) collective-permute-start(bf16[8,256,128]{2,1,0:T(8,128)(2,1)} %slice.96), channel_id=1, source_target_pairs={{0,1},{1,2},{2,3},{3,0},{4,5},{5,6},{6,7},{7,4},{8,9},{9,10},{10,1... | collective-permute-start | bytes 1572872 | tf_op jit(solution)/shard_map/ppermute | solution.py:31
  108.6 26.9 %all-to-all-start = ((bf16[16,128,128]{2,1,0:T(8,128)(2,1)}), bf16[16,128,128]{2,1,0:T(8,128)(2,1)S(1)}, u32[]{:S(2)}, u32[]{:S(2)}) async-start(bf16[16,128,128]{2,1,0:T(8,128)(2,1)} %bitcast_bitcast_fusion), calls=%async_computation | async-start | bytes 1048576 | tf_op jit(solution)/shard_map/all_to_all | solution.py:317
  112.2 35.6 %collective-permute-start.5 = (bf16[2048,256]{1,0:T(8,128)(2,1)}, bf16[2048,256]{1,0:T(8,128)(2,1)}, u32[]{:S(2)}, u32[]{:S(2)}) collective-permute-start(bf16[2048,256]{1,0:T(8,128)(2,1)} %collective-permute-done.refs_0_), channel_id=1, source_target_pairs={{0,16},{16,0},{1,17},{17,1},{2,18},{18,2},{3,19},{19,3},{4,20},{20... | collective-permute-start | bytes 3145736 | tf_op jit(solution)/shard_map/ppermute | solution.py:39
  116.5 31.4 %collective-permute-start.6 = (bf16[2048,256]{1,0:T(8,128)(2,1)}, bf16[2048,256]{1,0:T(8,128)(2,1)}, u32[]{:S(2)}, u32[]{:S(2)}) collective-permute-start(bf16[2048,256]{1,0:T(8,128)(2,1)} %collective-permute-done.2.refs_2_), channel_id=1, source_target_pairs={{0,16},{16,0},{1,17},{17,1},{2,18},{18,2},{3,19},{19,3},{4,20},{20... | collective-permute-start | bytes 3145736 | tf_op jit(solution)/shard_map/ppermute | solution.py:39
  118.5 14.7 %collective-permute-start.21 = (bf16[8,256,128]{2,1,0:T(8,128)(2,1)}, bf16[8,256,128]{2,1,0:T(8,128)(2,1)}, u32[]{:S(2)}, u32[]{:S(2)}) collective-permute-start(bf16[8,256,128]{2,1,0:T(8,128)(2,1)} %slice.97), channel_id=1, source_target_pairs={{0,3},{1,0},{2,1},{3,2},{4,7},{5,4},{6,5},{7,6},{8,11},{9,8},{10,9... | collective-permute-start | bytes 1572872 | tf_op jit(solution)/shard_map/ppermute | solution.py:31
  122.8 46.0 %collective-permute-start.4 = (bf16[2048,256]{1,0:T(8,128)(2,1)S(1)}, bf16[2048,256]{1,0:T(8,128)(2,1)S(1)}, u32[]{:S(2)}, u32[]{:S(2)}) collective-permute-start(bf16[2048,256]{1,0:T(8,128)(2,1)S(1)} %constant_dynamic-update-slice_fusion.refs_0_), channel_id=1, source_target_pairs={{0,16},{16,0},{1,17},{17,1},{2,18},{18,2},{3,19},{19,3},{4,20},{20... | collective-permute-start | bytes 3145736 | tf_op jit(solution)/shard_map/ppermute | solution.py:39
  133.1 66.2 %collective-permute-start.15 = (bf16[16,256,128]{2,1,0:T(8,128)(2,1)}, bf16[16,256,128]{2,1,0:T(8,128)(2,1)}, u32[]{:S(2)}, u32[]{:S(2)}) collective-permute-start(bf16[16,256,128]{2,1,0:T(8,128)(2,1)} %bitcast.60), channel_id=1, source_target_pairs={{0,16},{16,0},{1,17},{17,1},{2,18},{18,2},{3,19},{19,3},{4,20},{20... | collective-permute-start | bytes 3145736 | tf_op jit(solution)/shard_map/ppermute | solution.py:39
  135.0 64.3 %collective-permute-start.17 = (bf16[16,256,128]{2,1,0:T(8,128)(2,1)}, bf16[16,256,128]{2,1,0:T(8,128)(2,1)}, u32[]{:S(2)}, u32[]{:S(2)}) collective-permute-start(bf16[16,256,128]{2,1,0:T(8,128)(2,1)} %collective-permute-done.16.refs_2_), channel_id=1, source_target_pairs={{0,16},{16,0},{1,17},{17,1},{2,18},{18,2},{3,19},{19,3},{4,20},{20... | collective-permute-start | bytes 3145736 | tf_op jit(solution)/shard_map/ppermute | solution.py:39
  147.8 51.4 %collective-permute-start.19 = (bf16[16,256,128]{2,1,0:T(8,128)(2,1)}, bf16[16,256,128]{2,1,0:T(8,128)(2,1)}, u32[]{:S(2)}, u32[]{:S(2)}) collective-permute-start(bf16[16,256,128]{2,1,0:T(8,128)(2,1)} %collective-permute-done.18.refs_4_), channel_id=1, source_target_pairs={{0,16},{16,0},{1,17},{17,1},{2,18},{18,2},{3,19},{19,3},{4,20},{20... | collective-permute-start | bytes 3145736 | tf_op jit(solution)/shard_map/ppermute | solution.py:39
  147.9 51.4 %collective-permute-start.22 = (bf16[16,256,128]{2,1,0:T(8,128)(2,1)}, bf16[16,256,128]{2,1,0:T(8,128)(2,1)}, u32[]{:S(2)}, u32[]{:S(2)}) collective-permute-start(bf16[16,256,128]{2,1,0:T(8,128)(2,1)} %constant_dynamic-update-slice_fusion.2.refs_6_), channel_id=1, source_target_pairs={{0,16},{16,0},{1,17},{17,1},{2,18},{18,2},{3,19},{19,3},{4,20},{20... | collective-permute-start | bytes 3145736 | tf_op jit(solution)/shard_map/ppermute | solution.py:39
  183.5 15.8 %all-to-all-start.2 = ((bf16[16,128,128]{2,1,0:T(8,128)(2,1)}), bf16[16,128,128]{2,1,0:T(8,128)(2,1)S(1)}, u32[]{:S(2)}, u32[]{:S(2)}) async-start(bf16[16,128,128]{2,1,0:T(8,128)(2,1)} %bitcast.11), calls=%async_computation.2 | async-start | bytes 1048576 | tf_op jit(solution)/shard_map/all_to_all | solution.py:317
  204.9 14.2 %collective-permute-start.25 = (bf16[128,2048]{1,0:T(8,128)(2,1)S(1)}, bf16[128,2048]{1,0:T(8,128)(2,1)S(1)}, u32[]{:S(2)}, u32[]{:S(2)}) collective-permute-start(bf16[128,2048]{1,0:T(8,128)(2,1)S(1)} %get-tuple-element.23.refs_0_), channel_id=1, source_target_pairs={{0,1},{1,2},{2,3},{3,0},{4,5},{5,6},{6,7},{7,4},{8,9},{9,10},{10,1... | collective-permute-start | bytes 1572872 | tf_op jit(solution)/shard_map/ppermute | solution.py:31
  205.7 13.6 %collective-permute-start.26 = (bf16[128,2048]{1,0:T(8,128)(2,1)S(1)}, bf16[128,2048]{1,0:T(8,128)(2,1)S(1)}, u32[]{:S(2)}, u32[]{:S(2)}) collective-permute-start(bf16[128,2048]{1,0:T(8,128)(2,1)S(1)} %get-tuple-element.23.refs_0_), channel_id=1, source_target_pairs={{0,3},{1,0},{2,1},{3,2},{4,7},{5,4},{6,5},{7,6},{8,11},{9,8},{10,9... | collective-permute-start | bytes 1572872 | tf_op jit(solution)/shard_map/ppermute | solution.py:31
  227.7 17.3 %collective-permute-start.23 = (bf16[128,2048]{1,0:T(8,128)(2,1)S(1)}, bf16[128,2048]{1,0:T(8,128)(2,1)S(1)}, u32[]{:S(2)}, u32[]{:S(2)}) collective-permute-start(bf16[128,2048]{1,0:T(8,128)(2,1)S(1)} %get-tuple-element.23.refs_0_), channel_id=1, source_target_pairs={{0,16},{16,0},{1,17},{17,1},{2,18},{18,2},{3,19},{19,3},{4,20},{20... | collective-permute-start | bytes 1572872 | tf_op jit(solution)/shard_map/ppermute | solution.py:39
  241.0 10.5 %collective-permute-start.29 = (bf16[256,2048]{1,0:T(8,128)(2,1)S(1)}, bf16[256,2048]{1,0:T(8,128)(2,1)S(1)}, u32[]{:S(2)}, u32[]{:S(2)}) collective-permute-start(bf16[256,2048]{1,0:T(8,128)(2,1)S(1)} %slice.102), channel_id=1, source_target_pairs={{0,16},{16,0},{1,17},{17,1},{2,18},{18,2},{3,19},{19,3},{4,20},{20... | collective-permute-start | bytes 3145736 | tf_op jit(solution)/shard_map/ppermute | solution.py:39
  255.3 10.5 %collective-permute-start.37 = (bf16[64,2048]{1,0:T(8,128)(2,1)S(1)}, bf16[64,2048]{1,0:T(8,128)(2,1)S(1)}, u32[]{:S(2)}, u32[]{:S(2)}) collective-permute-start(bf16[64,2048]{1,0:T(8,128)(2,1)S(1)} %slice.134), channel_id=1, source_target_pairs={{0,3},{1,0},{2,1},{3,2},{4,7},{5,4},{6,5},{7,6},{8,11},{9,8},{10,9... | collective-permute-start | bytes 786440 | tf_op jit(solution)/shard_map/ppermute | solution.py:31
  258.5 10.8 %collective-permute-start.38 = (bf16[64,2048]{1,0:T(8,128)(2,1)S(1)}, bf16[64,2048]{1,0:T(8,128)(2,1)S(1)}, u32[]{:S(2)}, u32[]{:S(2)}) collective-permute-start(bf16[64,2048]{1,0:T(8,128)(2,1)S(1)} %slice.133), channel_id=1, source_target_pairs={{0,1},{1,2},{2,3},{3,0},{4,5},{5,6},{6,7},{7,4},{8,9},{9,10},{10,1... | collective-permute-start | bytes 786440 | tf_op jit(solution)/shard_map/ppermute | solution.py:31
  (23 other events, 337.2 us)
Sparse Core Ops, SparseCore 0:
  11.4 95.6 all-gather.1

commit v5 on v4

--- a/solution.py
+++ b/solution.py
@@ -31,8 +31,9 @@
     return lax.ppermute(array, axis, [(i, (i + step) % 4) for i in range(4)])
 
 
-def along_y(array, step):
-    return along(array, "y", step)
+def around(array, way):
+    pairs = [(c * Y + i, c * Y + (i + (way if c == 0 else -way)) % Y) for c in range(C) for i in range(Y)]
+    return lax.ppermute(array, ("c", "y"), pairs)
 
 
 def other_core(array):
@@ -289,16 +290,13 @@
 
 
 def gather_near(own):
-    before = along_y(own, 1)
-    after = along_y(own, -1)
-    return other_core(own), (before, other_core(before)), (after, other_core(after))
-
-
-def gather_far(before, after):
-    half = before.shape[0] // 2
-    top = along_y(before[:half], 1)
-    bottom = along_y(after[half:], -1)
-    far = jnp.concatenate([top, bottom], axis=0)
+    before = around(own, 1)
+    after = around(own, -1)
+    return other_core(own), (before, other_core(after)), (after, other_core(before))
+
+
+def gather_far(before):
+    far = around(before, 1)
     return far, other_core(far)
 
 
@@ -337,24 +335,26 @@
     w = lax.all_gather(both.reshape(-1, both.shape[-1]), ("z", "x"), axis=0, tiled=True)
     w = w.reshape(Z * X, *both.shape)
 
+    side = 2 * core - 1
+
     def where(*steps):
         return jnp.stack([core, y] + [(y + s) % Y for s in steps]).astype(jnp.int32)
 
     state = attend(where(0), q, [kv, kv_c], None, False)
-    far = gather_far(before[0], after[0])
-    state = attend(where(-1, 1), q, [*before, *after], state, False)
+    far = gather_far(before[0])
+    state = attend(where(side, -side), q, [*before, *after], state, False)
     low = attend(where(2), q, far, state, True, (0, Z - 1))
     high = attend(where(2), q, far, state, True, (Z - 1, Z))
     attn = jnp.concatenate([low, high], axis=0)
 
     wo_c, wo_before, wo_after = gather_near(wo)
-    wo_far = gather_far(wo_before[0], wo_after[0])
+    wo_far = gather_far(wo_before[0])
     attn = regroup(attn.reshape(HEADS, ROWS, HEAD_DIM))
     attn, w = lax.optimization_barrier((attn, w))
     attended, normed = project(
         jnp.stack(
             [core, lax.axis_index("z"), lax.axis_index("x")]
-            + [(y + s) % Y for s in (0, -1, 1, 2)]
+            + [(y + s) % Y for s in (0, side, -side, 2)]
         ).astype(jnp.int32),
         attn,
         [wo, wo_c, *wo_before, *wo_after, *wo_far],
@@ -364,31 +364,21 @@
 
     normed_c, before, after = gather_near(normed)
     own_part = ffn(w, [normed, normed_c])
-    far = gather_far(before[0], after[0])
+    far = gather_far(before[0])
     near_part = ffn(w, [before[0], after[0], before[1], after[1]])
     far_part = ffn(w, far)
 
-    half = ROWS // 2
     got_own = other_core(own_part[ROWS:])
     got_near = other_core(near_part[2 * ROWS :])
-    before = wide_add(near_part[:ROWS], got_near[:ROWS])
-    after = wide_add(near_part[ROWS : 2 * ROWS], got_near[ROWS:])
-    early_after = along_y(after[half:].astype(BF16), 1)
-    early_before = along_y(before[:half].astype(BF16), -1)
+    before = wide_add(near_part[:ROWS], got_near[ROWS:])
+    after = wide_add(near_part[ROWS : 2 * ROWS], got_near[:ROWS])
     far = wide_add(far_part[:ROWS], other_core(far_part[ROWS:])).astype(BF16)
-    far_top = along_y(far[:half], 1)
-    far_bottom = along_y(far[half:], -1)
-    far_top, far_bottom = lax.optimization_barrier((far_top, far_bottom))
-    late_after = along_y(wide_add(after[:half], far_top).astype(BF16), 1)
-    late_before = along_y(wide_add(before[half:], far_bottom).astype(BF16), -1)
+    far = around(far, 1)
+    before, after = lax.optimization_barrier((before.astype(BF16), after))
+    before = around(before, -1)
+    after = around(wide_add(after, far).astype(BF16), 1)
     own = wide_add(own_part[:ROWS], got_own)
-    total = jnp.concatenate(
-        [
-            own[:half] + wide_add(late_after, early_before),
-            own[half:] + wide_add(early_after, late_before),
-        ],
-        axis=0,
-    )
+    total = own + wide_add(before, after)
     return attended, (attended.astype(F32) + total).astype(BF16)
 
 

time: 278 us -> 274 us (0.986)
  blocking collectives: 0 us -> 32.4 us
  starting transfers between devices: 60.5 us -> 30 us
  local copies, waits for them, and re-layouts: 11.8 us -> 8.87 us
    ppermute x24 -> x6, waiting for transfers between devices: 102 us -> 24.8 us  [along(): return lax.ppermute(array, axis, [(i, (i + step) % 4) for i in range(4)])]
    ppermute x0 -> x12, waiting for transfers between devices: none -> 71.9 us  [around(): return lax.ppermute(array, ('c', 'y'), pairs)]
    ppermute x24 -> x6, starting transfers between devices: 42 us -> 6.96 us  [along(): return lax.ppermute(array, axis, [(i, (i + step) % 4) for i in range(4)])]
    all_to_all x0 -> x1, blocking collectives: none -> 32.4 us  [regroup(): lax.all_to_all(array, ('z', 'x'), split_axis=0, concat_axis=0, tiled=True)]
    ppermute x0 -> x12, starting transfers between devices: none -> 11.9 us  [around(): return lax.ppermute(array, ('c', 'y'), pairs)]
    all_to_all x3 -> x2, starting transfers between devices: 15.2 us -> 7.15 us  [regroup(): lax.all_to_all(array, ('z', 'x'), split_axis=0, concat_axis=0, tiled=True)]
    slice x9 -> x0, local copies, waits for them, and re-layouts: 7.66 us -> none  [the longest x3 3.79 us: gather_far(): top = along_y(before[:half], 1)]
    unnamed x25 -> x30, local copies, waits for them, and re-layouts: 0.99 us -> 7.63 us
  transfers between devices with their start and end apart: 44 -> 37, of which waited for: 21 -> 16; matrix products, arithmetic and copies ran while one was open for 5% -> 1% of each run, Pallas kernels for 23% -> 22%
where the time goes in v5:
time: 274 us; the launch traced here: 273 us
  waiting for transfers between devices  115 us (42%)
  Pallas kernels  66.6 us (24%)
  blocking collectives  32.4 us (12%)
  starting transfers between devices  30 us (11%)
  between operations  14.5 us (5%)
  local copies, waits for them, and re-layouts  8.87 us (3%)
  other arithmetic  6.26 us (2%)
    ppermute x12, waiting for transfers between devices, around(): return lax.ppermute(array, ('c', 'y'), pairs)  71.9 us
    pallas_call x4, Pallas kernels, attend(): pl.pallas_call(functools.partial(attend_body, first, last, n_pairs, zs),...  45.5 us
    all_to_all x1, blocking collectives, regroup(): lax.all_to_all(array, ('z', 'x'), split_axis=0, concat_axis=0, tiled=True)  32.4 us
    ppermute x6, waiting for transfers between devices, along(): return lax.ppermute(array, axis, [(i, (i + step) % 4) for i in range(4)])  24.8 us
    pallas_call x3, Pallas kernels, ffn(): pl.pallas_call(functools.partial(ffn_body, n), out_shape=jax.ShapeDtypeSt...  15.2 us
    all_to_all x2, waiting for transfers between devices, regroup(): lax.all_to_all(array, ('z', 'x'), split_axis=0, concat_axis=0, tiled=True)  12.1 us
    ppermute x12, starting transfers between devices, around(): return lax.ppermute(array, ('c', 'y'), pairs)  11.9 us
    unnamed x30, local copies, waits for them, and re-layouts  7.63 us
  transfers between devices with their start and end apart: 37, of which 16 were waited for; matrix products, arithmetic and copies ran while one was open for 1% of the time, Pallas kernels for 22%

profile of v5, /device:TPU:0, one launch (start us, length us, event | category | flops | bytes accessed | tf_op | source)
XLA Modules:
  0.0 273.1 jit_solution(15757770425082712069)
XLA Ops:
  8.7 1.6 collective-permute-done.7
  11.5 32.4 %all_to_all.15 = bf16[16,128,256]{2,1,0:T(8,128)(2,1)S(1)} all-to-all(bf16[16,128,256]{2,1,0:T(8,128)(2,1)S(1)} %shard_map.104), channel_id=1, replica_groups=mesh['z'=4,'c'=2,'x'=4,'y'=4] {'z','x'}, dimensions={0} | all-to-all | bytes 2097152 | tf_op jit(solution)/shard_map/all_to_all | solution.py:315
  43.8 1.7 collective-permute-start
  46.1 2.8 %collective-permute-start.10 = (bf16[256,128]{1,0:T(8,128)(2,1)S(1)}, bf16[256,128]{1,0:T(8,128)(2,1)S(1)}, u32[]{:S(2)}, u32[]{:S(2)}) collective-permute-start(bf16[256,128]{1,0:T(8,128)(2,1)S(1)} %copy-done.10), channel_id=1, source_target_pairs={{0,12},{4,0},{8,4},{12,8},{1,13},{5,1},{9,5},{13,9},{2,14},{6,2},{... | collective-permute-start | bytes 196616 | tf_op jit(solution)/shard_map/ppermute | solution.py:31
  48.8 2.9 %collective-permute-done.8 = bf16[256,128]{1,0:T(8,128)(2,1)S(1)} collective-permute-done((bf16[256,128]{1,0:T(8,128)(2,1)S(1)}, bf16[256,128]{1,0:T(8,128)(2,1)S(1)}, u32[]{:S(2)}, u32[]{:S(2)}) %collective-permute-start.8) | collective-permute-done | bytes 65568 | tf_op jit(solution)/shard_map/ppermute | solution.py:31
  52.8 2.4 collective-permute-start.12
  56.4 11.8 %collective-permute-done.11 = bf16[4,256,128]{2,1,0:T(8,128)(2,1)S(1)} collective-permute-done((bf16[4,256,128]{2,1,0:T(8,128)(2,1)S(1)}, bf16[4,256,128]{2,1,0:T(8,128)(2,1)S(1)}, u32[]{:S(2)}, u32[]{:S(2)}) %collective-permute-start.11) | collective-permute-done | bytes 262176 | tf_op jit(solution)/shard_map/ppermute | solution.py:31
  68.2 5.0 %collective-permute-done.12 = bf16[4,256,128]{2,1,0:T(8,128)(2,1)S(1)} collective-permute-done((bf16[4,256,128]{2,1,0:T(8,128)(2,1)S(1)}, bf16[4,256,128]{2,1,0:T(8,128)(2,1)S(1)}, u32[]{:S(2)}, u32[]{:S(2)}) %collective-permute-start.12) | collective-permute-done | bytes 262176 | tf_op jit(solution)/shard_map/ppermute | solution.py:31
  73.2 4.2 %collective-permute-done.13 = bf16[4,256,128]{2,1,0:T(8,128)(2,1)S(1)} collective-permute-done((bf16[4,256,128]{2,1,0:T(8,128)(2,1)S(1)}, bf16[4,256,128]{2,1,0:T(8,128)(2,1)S(1)}, u32[]{:S(2)}, u32[]{:S(2)}) %collective-permute-start.13) | collective-permute-done | bytes 262176 | tf_op jit(solution)/shard_map/ppermute | solution.py:31
  78.6 3.2 %collective-permute-start.3 = (bf16[2048,256]{1,0:T(8,128)(2,1)S(1)}, bf16[2048,256]{1,0:T(8,128)(2,1)}, u32[]{:S(2)}, u32[]{:S(2)}) collective-permute-start(bf16[2048,256]{1,0:T(8,128)(2,1)S(1)} %bitcast.62), channel_id=1, source_target_pairs={{0,3},{1,0},{2,1},{3,2},{16,17},{17,18},{18,19},{19,16},{4,7},{5,4... | collective-permute-start | bytes 3145736 | tf_op jit(solution)/shard_map/ppermute | solution.py:36
  81.8 3.2 %collective-permute-start.16 = (bf16[16,256,128]{2,1,0:T(8,128)(2,1)}, bf16[16,256,128]{2,1,0:T(8,128)(2,1)}, u32[]{:S(2)}, u32[]{:S(2)}) collective-permute-start(bf16[16,256,128]{2,1,0:T(8,128)(2,1)} %bitcast.32.refs_0_), channel_id=1, source_target_pairs={{0,3},{1,0},{2,1},{3,2},{16,17},{17,18},{18,19},{19,16},{4,7},{5,4... | collective-permute-start | bytes 3145736 | tf_op jit(solution)/shard_map/ppermute | solution.py:36
  85.0 21.1 %collective-permute-done.15.refs_2_ = bf16[16,256,128]{2,1,0:T(8,128)(2,1)} collective-permute-done((bf16[16,256,128]{2,1,0:T(8,128)(2,1)}, bf16[16,256,128]{2,1,0:T(8,128)(2,1)}, u32[]{:S(2)}, u32[]{:S(2)}) %collective-permute-start.15) | collective-permute-done | bytes 1048608 | tf_op jit(solution)/shard_map/ppermute | solution.py:36
  108.5 3.6 %all-to-all-start = ((bf16[16,128,128]{2,1,0:T(8,128)(2,1)}), bf16[16,128,128]{2,1,0:T(8,128)(2,1)S(1)}, u32[]{:S(2)}, u32[]{:S(2)}) async-start(bf16[16,128,128]{2,1,0:T(8,128)(2,1)} %bitcast_bitcast_fusion), calls=%async_computation | async-start | bytes 1048576 | tf_op jit(solution)/shard_map/all_to_all | solution.py:315
  112.2 15.9 %collective-permute-done.1.refs_0_ = bf16[2048,256]{1,0:T(8,128)(2,1)S(1)} collective-permute-done((bf16[2048,256]{1,0:T(8,128)(2,1)}, bf16[2048,256]{1,0:T(8,128)(2,1)S(1)}, u32[]{:S(2)}, u32[]{:S(2)}) %collective-permute-start.1) | collective-permute-done | bytes 1048608 | tf_op jit(solution)/shard_map/ppermute | solution.py:36
  130.8 11.4 %shard_map.105 = (f32[2048,128]{1,0:T(8,128)}, f32[2048,128]{1,0:T(8,128)}, f32[2048,128]{1,0:T(8,128)}) custom-call(s32[3]{0:T(128)S(1)} %pad_add_fusion.3.where_ref, bf16[2048,128]{1,0:T(8,128)(2,1)S(1)} %bitcast.56, bf16[2048,256]{1,0:T(8,128)(2,1)S(1)} %bitcast.63, bf16[2048,256]{1,0:T(8,128)(2,1)S(1)} %copy-done.8), custom_call_target="tpu_custom_call" | custom-call | flops 2684354560 | bytes 2097152 | tf_op jit(solution)/shard_map/pallas_call | solution.py:177
  143.6 20.4 %shard_map.106 = (f32[2048,128]{1,0:T(8,128)}, f32[2048,128]{1,0:T(8,128)}, f32[2048,128]{1,0:T(8,128)}) custom-call(s32[4]{0:T(128)S(1)} %pad_add_fusion.2.where_ref, bf16[2048,128]{1,0:T(8,128)(2,1)S(1)} %bitcast.57, bf16[2048,256]{1,0:T(8,128)(2,1)} %collective-permute-done.refs_0_, bf16[2048,256]{1,0:T(8,128)(2,1)} %collective-permute-done.4.refs_1_, ...), custom_call_target="tpu_custom_call" | custom-call | flops 5368709120 | bytes 4194304 | tf_op jit(solution)/shard_map/pallas_call | solution.py:177
  164.0 5.8 %shard_map.108 = bf16[512,128]{1,0:T(8,128)(2,1)S(1)} custom-call(s32[3]{0:T(128)S(1)} %pad_add_fusion.where_ref, bf16[2048,128]{1,0:T(8,128)(2,1)S(1)} %bitcast.58, bf16[2048,256]{1,0:T(8,128)(2,1)S(1)} %collective-permute-done.1.refs_0_, bf16[2048,256]{1,0:T(8,128)(2,1)S(1)} %collective-permute-done.2.refs_1_, f32[2048,128]{1,0:T(8,128)} %get-tuple-element.17.refs_2_, ...), custom_call_target="tpu_custom_call" | custom-call | flops 1073741824 | bytes 2097152 | tf_op jit(solution)/shard_map/pallas_call | solution.py:177
  169.7 8.0 %shard_map.107 = bf16[1536,128]{1,0:T(8,128)(2,1)S(1)} custom-call(s32[3]{0:T(128)S(1)} %pad_add_fusion.where_ref, bf16[2048,128]{1,0:T(8,128)(2,1)S(1)} %bitcast.59, bf16[2048,256]{1,0:T(8,128)(2,1)S(1)} %collective-permute-done.1.refs_0_, bf16[2048,256]{1,0:T(8,128)(2,1)S(1)} %collective-permute-done.2.refs_1_, f32[2048,128]{1,0:T(8,128)} %get-tuple-element.17.refs_2_, ...), custom_call_target="tpu_custom_call" | custom-call | flops 1610612736 | bytes 2097152 | tf_op jit(solution)/shard_map/pallas_call | solution.py:177
  178.6 3.6 %all-to-all-start.2 = ((bf16[16,128,128]{2,1,0:T(8,128)(2,1)}), bf16[16,128,128]{2,1,0:T(8,128)(2,1)S(1)}, u32[]{:S(2)}, u32[]{:S(2)}) async-start(bf16[16,128,128]{2,1,0:T(8,128)(2,1)} %bitcast.11), calls=%async_computation.2 | async-start | bytes 1048576 | tf_op jit(solution)/shard_map/all_to_all | solution.py:315
  182.3 12.1 %all-to-all-done.2.attn_ref = bf16[16,128,128]{2,1,0:T(8,128)(2,1)S(1)} async-done(((bf16[16,128,128]{2,1,0:T(8,128)(2,1)}), bf16[16,128,128]{2,1,0:T(8,128)(2,1)S(1)}, u32[]{:S(2)}, u32[]{:S(2)}) %all-to-all-start.2) | async-done | bytes 524320 | tf_op jit(solution)/shard_map/all_to_all | solution.py:315
  194.4 5.7 %shard_map.109 = (bf16[128,2048]{1,0:T(8,128)(2,1)}, bf16[128,2048]{1,0:T(8,128)(2,1)S(1)}) custom-call(s32[7]{0:T(128)S(1)} %stack.107.where_ref, bf16[16,128,128]{2,1,0:T(8,128)(2,1)S(1)} %all-to-all-done.2.attn_ref, bf16[128,2048]{1,0:T(8,128)(2,1)S(1)} %copy-done.4, bf16[1,2048]{1,0:T(2,128)(2,1)S(1)} %reshape.41.gain_ref, ...), custom_call_target="tpu_custom_call" | custom-call | flops 1073741824 | bytes 8388608 | tf_op jit(solution)/shard_map/pallas_call | solution.py:231
  200.1 10.4 %collective-permute-done.23.refs_0_ = bf16[128,2048]{1,0:T(8,128)(2,1)S(1)} collective-permute-done((bf16[128,2048]{1,0:T(8,128)(2,1)S(1)}, bf16[128,2048]{1,0:T(8,128)(2,1)S(1)}, u32[]{:S(2)}, u32[]{:S(2)}) %collective-permute-start.23) | collective-permute-done | bytes 524320 | tf_op jit(solution)/shard_map/ppermute | solution.py:36
  210.5 3.2 %collective-permute-start.24 = (bf16[128,2048]{1,0:T(8,128)(2,1)S(1)}, bf16[128,2048]{1,0:T(8,128)(2,1)S(1)}, u32[]{:S(2)}, u32[]{:S(2)}) collective-permute-start(bf16[128,2048]{1,0:T(8,128)(2,1)S(1)} %get-tuple-element.23.refs_0_), channel_id=1, source_target_pairs={{0,3},{1,0},{2,1},{3,2},{16,17},{17,18},{18,19},{19,16},{4,7},{5,4... | collective-permute-start | bytes 1572872 | tf_op jit(solution)/shard_map/ppermute | solution.py:36
  213.8 9.8 %collective-permute-done.29.refs_0_ = bf16[128,2048]{1,0:T(8,128)(2,1)S(1)} collective-permute-done((bf16[128,2048]{1,0:T(8,128)(2,1)S(1)}, bf16[128,2048]{1,0:T(8,128)(2,1)S(1)}, u32[]{:S(2)}, u32[]{:S(2)}) %collective-permute-start.29) | collective-permute-done | bytes 524320 | tf_op jit(solution)/shard_map/ppermute | solution.py:36
  224.0 1.4 collective-permute-done.30.refs_1_
  225.4 4.1 %copy-done.1 = bf16[21504,256]{1,0:T(8,128)(2,1)S(1)} copy-done((bf16[21504,256]{1,0:T(8,128)(2,1)S(1)}, bf16[21504,256]{1,0:T(8,128)(2,1)}, u32[]{:S(2)}) %copy-start.1) | copy-done | bytes 11010072
  229.6 3.7 %shard_map.112 = bf16[256,2048]{1,0:T(8,128)(2,1)S(1)} custom-call(bf16[16,3,2,224,256]{4,3,2,1,0:T(8,128)(2,1)S(1)} %bitcast.51, bf16[128,2048]{1,0:T(8,128)(2,1)S(1)} %collective-permute-done.29.refs_0_, bf16[128,2048]{1,0:T(8,128)(2,1)S(1)} %collective-permute-done.30.refs_1_), custom_call_target="tpu_custom_call" | custom-call | flops 2818572288 | bytes 11010048 | tf_op jit(solution)/shard_map/pallas_call | solution.py:277
  233.8 7.7 %shard_map.111 = bf16[512,2048]{1,0:T(8,128)(2,1)S(1)} custom-call(bf16[16,3,2,224,256]{4,3,2,1,0:T(8,128)(2,1)S(1)} %bitcast.52, bf16[128,2048]{1,0:T(8,128)(2,1)S(1)} %collective-permute-done.23.refs_0_, bf16[128,2048]{1,0:T(8,128)(2,1)S(1)} %collective-permute-done.24.refs_1_, bf16[128,2048]{1,0:T(8,128)(2,1)S(1)} %collective-permute-done.25.refs_2_, ...), custom_call_target="tpu_custom_call" | custom-call | flops 5637144576 | bytes 11010048 | tf_op jit(solution)/shard_map/pallas_call | solution.py:277
  242.4 2.7 collective-permute-done.21.refs_1_
  245.1 3.8 %shard_map.110 = bf16[256,2048]{1,0:T(8,128)(2,1)S(1)} custom-call(bf16[16,3,2,224,256]{4,3,2,1,0:T(8,128)(2,1)S(1)} %bitcast.55, bf16[128,2048]{1,0:T(8,128)(2,1)S(1)} %get-tuple-element.23.refs_0_, bf16[128,2048]{1,0:T(8,128)(2,1)S(1)} %collective-permute-done.21.refs_1_), custom_call_target="tpu_custom_call" | custom-call | flops 2818572288 | bytes 11010048 | tf_op jit(solution)/shard_map/pallas_call | solution.py:277
  250.0 2.8 %collective-permute-done.32 = bf16[128,2048]{1,0:T(8,128)(2,1)S(1)} collective-permute-done((bf16[128,2048]{1,0:T(8,128)(2,1)S(1)}, bf16[128,2048]{1,0:T(8,128)(2,1)S(1)}, u32[]{:S(2)}, u32[]{:S(2)}) %collective-permute-start.32) | collective-permute-done | bytes 524320 | tf_op jit(solution)/shard_map/ppermute | solution.py:36
  253.0 11.1 %collective-permute-done.28 = bf16[128,2048]{1,0:T(8,128)(2,1)S(1)} collective-permute-done((bf16[128,2048]{1,0:T(8,128)(2,1)S(1)}, bf16[128,2048]{1,0:T(8,128)(2,1)S(1)}, u32[]{:S(2)}, u32[]{:S(2)}) %collective-permute-start.28) | collective-permute-done | bytes 524320 | tf_op jit(solution)/shard_map/ppermute | solution.py:36
  (104 shorter events, 19.2 us)
Async XLA Ops:
  7.2 187.2 %all-gather.2.cloned.1.call-start = ((), (), s32[]{:S(2)}) async-start(), calls=%async_computation.3 | async-start | bytes 11698176 | tf_op jit(solution)/shard_map/all_gather | solution.py:335
  43.8 37.9 %collective-permute-start = (bf16[2048,256]{1,0:T(8,128)(2,1)S(1)}, bf16[2048,256]{1,0:T(8,128)(2,1)}, u32[]{:S(2)}, u32[]{:S(2)}) collective-permute-start(bf16[2048,256]{1,0:T(8,128)(2,1)S(1)} %bitcast.60), channel_id=1, source_target_pairs={{0,1},{1,2},{2,3},{3,0},{16,19},{17,16},{18,17},{19,18},{4,5},{5,6... | collective-permute-start | bytes 3145736 | tf_op jit(solution)/shard_map/ppermute | solution.py:36
  45.6 6.2 %collective-permute-start.8 = (bf16[256,128]{1,0:T(8,128)(2,1)S(1)}, bf16[256,128]{1,0:T(8,128)(2,1)S(1)}, u32[]{:S(2)}, u32[]{:S(2)}) collective-permute-start(bf16[256,128]{1,0:T(8,128)(2,1)S(1)} %copy-done.10), channel_id=1, source_target_pairs={{0,4},{4,8},{8,12},{12,0},{1,5},{5,9},{9,13},{13,1},{2,6},{6,10},{... | collective-permute-start | bytes 196616 | tf_op jit(solution)/shard_map/ppermute | solution.py:31
  46.1 6.6 %collective-permute-start.10 = (bf16[256,128]{1,0:T(8,128)(2,1)S(1)}, bf16[256,128]{1,0:T(8,128)(2,1)S(1)}, u32[]{:S(2)}, u32[]{:S(2)}) collective-permute-start(bf16[256,128]{1,0:T(8,128)(2,1)S(1)} %copy-done.10), channel_id=1, source_target_pairs={{0,12},{4,0},{8,4},{12,8},{1,13},{5,1},{9,5},{13,9},{2,14},{6,2},{... | collective-permute-start | bytes 196616 | tf_op jit(solution)/shard_map/ppermute | solution.py:31
  52.7 15.5 %collective-permute-start.11 = (bf16[4,256,128]{2,1,0:T(8,128)(2,1)S(1)}, bf16[4,256,128]{2,1,0:T(8,128)(2,1)S(1)}, u32[]{:S(2)}, u32[]{:S(2)}) collective-permute-start(bf16[4,256,128]{2,1,0:T(8,128)(2,1)S(1)} %pad_maximum_fusion.4), channel_id=1, source_target_pairs={{0,32},{32,64},{64,96},{96,0},{1,33},{33,65},{65,97},{97,1},{2,34}... | collective-permute-start | bytes 786440 | tf_op jit(solution)/shard_map/ppermute | solution.py:31
  52.8 20.4 %collective-permute-start.12 = (bf16[4,256,128]{2,1,0:T(8,128)(2,1)S(1)}, bf16[4,256,128]{2,1,0:T(8,128)(2,1)S(1)}, u32[]{:S(2)}, u32[]{:S(2)}) collective-permute-start(bf16[4,256,128]{2,1,0:T(8,128)(2,1)S(1)} %pad_maximum_fusion.4), channel_id=1, source_target_pairs={{0,64},{32,96},{64,0},{96,32},{1,65},{33,97},{65,1},{97,33},{2,66}... | collective-permute-start | bytes 786440 | tf_op jit(solution)/shard_map/ppermute | solution.py:31
  55.1 22.3 %collective-permute-start.13 = (bf16[4,256,128]{2,1,0:T(8,128)(2,1)S(1)}, bf16[4,256,128]{2,1,0:T(8,128)(2,1)S(1)}, u32[]{:S(2)}, u32[]{:S(2)}) collective-permute-start(bf16[4,256,128]{2,1,0:T(8,128)(2,1)S(1)} %pad_maximum_fusion.4), channel_id=1, source_target_pairs={{0,96},{32,0},{64,32},{96,64},{1,97},{33,1},{65,33},{97,65},{2,98}... | collective-permute-start | bytes 786440 | tf_op jit(solution)/shard_map/ppermute | solution.py:31
  78.5 27.6 %collective-permute-start.15 = (bf16[16,256,128]{2,1,0:T(8,128)(2,1)}, bf16[16,256,128]{2,1,0:T(8,128)(2,1)}, u32[]{:S(2)}, u32[]{:S(2)}) collective-permute-start(bf16[16,256,128]{2,1,0:T(8,128)(2,1)} %bitcast.32.refs_0_), channel_id=1, source_target_pairs={{0,1},{1,2},{2,3},{3,0},{16,19},{17,16},{18,17},{19,18},{4,5},{5,6... | collective-permute-start | bytes 3145736 | tf_op jit(solution)/shard_map/ppermute | solution.py:36
  78.5 27.6 %collective-permute-start.6 = (bf16[2048,256]{1,0:T(8,128)(2,1)S(1)}, bf16[2048,256]{1,0:T(8,128)(2,1)S(1)}, u32[]{:S(2)}, u32[]{:S(2)}) collective-permute-start(bf16[2048,256]{1,0:T(8,128)(2,1)S(1)} %bitcast.61), channel_id=1, source_target_pairs={{0,16},{16,0},{1,17},{17,1},{2,18},{18,2},{3,19},{19,3},{4,20},{20... | collective-permute-start | bytes 3145736 | tf_op jit(solution)/shard_map/ppermute | solution.py:40
  78.6 28.5 %collective-permute-start.3 = (bf16[2048,256]{1,0:T(8,128)(2,1)S(1)}, bf16[2048,256]{1,0:T(8,128)(2,1)}, u32[]{:S(2)}, u32[]{:S(2)}) collective-permute-start(bf16[2048,256]{1,0:T(8,128)(2,1)S(1)} %bitcast.62), channel_id=1, source_target_pairs={{0,3},{1,0},{2,1},{3,2},{16,17},{17,18},{18,19},{19,16},{4,7},{5,4... | collective-permute-start | bytes 3145736 | tf_op jit(solution)/shard_map/ppermute | solution.py:36
  81.8 46.3 %collective-permute-start.1 = (bf16[2048,256]{1,0:T(8,128)(2,1)}, bf16[2048,256]{1,0:T(8,128)(2,1)S(1)}, u32[]{:S(2)}, u32[]{:S(2)}) collective-permute-start(bf16[2048,256]{1,0:T(8,128)(2,1)} %collective-permute-done.refs_0_), channel_id=1, source_target_pairs={{0,1},{1,2},{2,3},{3,0},{16,19},{17,16},{18,17},{19,18},{4,5},{5,6... | collective-permute-start | bytes 3145736 | tf_op jit(solution)/shard_map/ppermute | solution.py:36
  81.8 60.4 %collective-permute-start.16 = (bf16[16,256,128]{2,1,0:T(8,128)(2,1)}, bf16[16,256,128]{2,1,0:T(8,128)(2,1)}, u32[]{:S(2)}, u32[]{:S(2)}) collective-permute-start(bf16[16,256,128]{2,1,0:T(8,128)(2,1)} %bitcast.32.refs_0_), channel_id=1, source_target_pairs={{0,3},{1,0},{2,1},{3,2},{16,17},{17,18},{18,19},{19,16},{4,7},{5,4... | collective-permute-start | bytes 3145736 | tf_op jit(solution)/shard_map/ppermute | solution.py:36
  106.1 36.7 %collective-permute-start.19 = (bf16[16,256,128]{2,1,0:T(8,128)(2,1)}, bf16[16,256,128]{2,1,0:T(8,128)(2,1)}, u32[]{:S(2)}, u32[]{:S(2)}) collective-permute-start(bf16[16,256,128]{2,1,0:T(8,128)(2,1)} %collective-permute-done.15.refs_2_), channel_id=1, source_target_pairs={{0,1},{1,2},{2,3},{3,0},{16,19},{17,16},{18,17},{19,18},{4,5},{5,6... | collective-permute-start | bytes 3145736 | tf_op jit(solution)/shard_map/ppermute | solution.py:36
  107.1 35.8 %collective-permute-start.5 = (bf16[2048,256]{1,0:T(8,128)(2,1)}, bf16[2048,256]{1,0:T(8,128)(2,1)}, u32[]{:S(2)}, u32[]{:S(2)}) collective-permute-start(bf16[2048,256]{1,0:T(8,128)(2,1)} %collective-permute-done.refs_0_), channel_id=1, source_target_pairs={{0,16},{16,0},{1,17},{17,1},{2,18},{18,2},{3,19},{19,3},{4,20},{20... | collective-permute-start | bytes 3145736 | tf_op jit(solution)/shard_map/ppermute | solution.py:40
  107.1 36.2 %collective-permute-start.4 = (bf16[2048,256]{1,0:T(8,128)(2,1)}, bf16[2048,256]{1,0:T(8,128)(2,1)}, u32[]{:S(2)}, u32[]{:S(2)}) collective-permute-start(bf16[2048,256]{1,0:T(8,128)(2,1)} %collective-permute-done.3.refs_2_), channel_id=1, source_target_pairs={{0,16},{16,0},{1,17},{17,1},{2,18},{18,2},{3,19},{19,3},{4,20},{20... | collective-permute-start | bytes 3145736 | tf_op jit(solution)/shard_map/ppermute | solution.py:40
  108.5 19.8 %all-to-all-start = ((bf16[16,128,128]{2,1,0:T(8,128)(2,1)}), bf16[16,128,128]{2,1,0:T(8,128)(2,1)S(1)}, u32[]{:S(2)}, u32[]{:S(2)}) async-start(bf16[16,128,128]{2,1,0:T(8,128)(2,1)} %bitcast_bitcast_fusion), calls=%async_computation | async-start | bytes 1048576 | tf_op jit(solution)/shard_map/all_to_all | solution.py:315
  128.1 35.9 %collective-permute-start.2 = (bf16[2048,256]{1,0:T(8,128)(2,1)S(1)}, bf16[2048,256]{1,0:T(8,128)(2,1)S(1)}, u32[]{:S(2)}, u32[]{:S(2)}) collective-permute-start(bf16[2048,256]{1,0:T(8,128)(2,1)S(1)} %collective-permute-done.1.refs_0_), channel_id=1, source_target_pairs={{0,16},{16,0},{1,17},{17,1},{2,18},{18,2},{3,19},{19,3},{4,20},{20... | collective-permute-start | bytes 3145736 | tf_op jit(solution)/shard_map/ppermute | solution.py:40
  142.2 52.1 %collective-permute-start.14 = (bf16[16,256,128]{2,1,0:T(8,128)(2,1)}, bf16[16,256,128]{2,1,0:T(8,128)(2,1)}, u32[]{:S(2)}, u32[]{:S(2)}) collective-permute-start(bf16[16,256,128]{2,1,0:T(8,128)(2,1)} %bitcast.32.refs_0_), channel_id=1, source_target_pairs={{0,16},{16,0},{1,17},{17,1},{2,18},{18,2},{3,19},{19,3},{4,20},{20... | collective-permute-start | bytes 3145736 | tf_op jit(solution)/shard_map/ppermute | solution.py:40
  142.8 51.6 %collective-permute-start.18 = (bf16[16,256,128]{2,1,0:T(8,128)(2,1)}, bf16[16,256,128]{2,1,0:T(8,128)(2,1)}, u32[]{:S(2)}, u32[]{:S(2)}) collective-permute-start(bf16[16,256,128]{2,1,0:T(8,128)(2,1)} %collective-permute-done.15.refs_2_), channel_id=1, source_target_pairs={{0,16},{16,0},{1,17},{17,1},{2,18},{18,2},{3,19},{19,3},{4,20},{20... | collective-permute-start | bytes 3145736 | tf_op jit(solution)/shard_map/ppermute | solution.py:40
  142.9 51.5 %collective-permute-start.17 = (bf16[16,256,128]{2,1,0:T(8,128)(2,1)}, bf16[16,256,128]{2,1,0:T(8,128)(2,1)}, u32[]{:S(2)}, u32[]{:S(2)}) collective-permute-start(bf16[16,256,128]{2,1,0:T(8,128)(2,1)} %collective-permute-done.16.refs_4_), channel_id=1, source_target_pairs={{0,16},{16,0},{1,17},{17,1},{2,18},{18,2},{3,19},{19,3},{4,20},{20... | collective-permute-start | bytes 3145736 | tf_op jit(solution)/shard_map/ppermute | solution.py:40
  143.3 51.1 %collective-permute-start.20 = (bf16[16,256,128]{2,1,0:T(8,128)(2,1)}, bf16[16,256,128]{2,1,0:T(8,128)(2,1)}, u32[]{:S(2)}, u32[]{:S(2)}) collective-permute-start(bf16[16,256,128]{2,1,0:T(8,128)(2,1)} %collective-permute-done.19.refs_6_), channel_id=1, source_target_pairs={{0,16},{16,0},{1,17},{17,1},{2,18},{18,2},{3,19},{19,3},{4,20},{20... | collective-permute-start | bytes 3145736 | tf_op jit(solution)/shard_map/ppermute | solution.py:40
  178.6 15.8 %all-to-all-start.2 = ((bf16[16,128,128]{2,1,0:T(8,128)(2,1)}), bf16[16,128,128]{2,1,0:T(8,128)(2,1)S(1)}, u32[]{:S(2)}, u32[]{:S(2)}) async-start(bf16[16,128,128]{2,1,0:T(8,128)(2,1)} %bitcast.11), calls=%async_computation.2 | async-start | bytes 1048576 | tf_op jit(solution)/shard_map/all_to_all | solution.py:315
  200.1 10.4 %collective-permute-start.23 = (bf16[128,2048]{1,0:T(8,128)(2,1)S(1)}, bf16[128,2048]{1,0:T(8,128)(2,1)S(1)}, u32[]{:S(2)}, u32[]{:S(2)}) collective-permute-start(bf16[128,2048]{1,0:T(8,128)(2,1)S(1)} %get-tuple-element.23.refs_0_), channel_id=1, source_target_pairs={{0,1},{1,2},{2,3},{3,0},{16,19},{17,16},{18,17},{19,18},{4,5},{5,6... | collective-permute-start | bytes 1572872 | tf_op jit(solution)/shard_map/ppermute | solution.py:36
  210.5 13.0 %collective-permute-start.29 = (bf16[128,2048]{1,0:T(8,128)(2,1)S(1)}, bf16[128,2048]{1,0:T(8,128)(2,1)S(1)}, u32[]{:S(2)}, u32[]{:S(2)}) collective-permute-start(bf16[128,2048]{1,0:T(8,128)(2,1)S(1)} %collective-permute-done.23.refs_0_), channel_id=1, source_target_pairs={{0,1},{1,2},{2,3},{3,0},{16,19},{17,16},{18,17},{19,18},{4,5},{5,6... | collective-permute-start | bytes 1572872 | tf_op jit(solution)/shard_map/ppermute | solution.py:36
  210.5 13.0 %collective-permute-start.24 = (bf16[128,2048]{1,0:T(8,128)(2,1)S(1)}, bf16[128,2048]{1,0:T(8,128)(2,1)S(1)}, u32[]{:S(2)}, u32[]{:S(2)}) collective-permute-start(bf16[128,2048]{1,0:T(8,128)(2,1)S(1)} %get-tuple-element.23.refs_0_), channel_id=1, source_target_pairs={{0,3},{1,0},{2,1},{3,2},{16,17},{17,18},{18,19},{19,16},{4,7},{5,4... | collective-permute-start | bytes 1572872 | tf_op jit(solution)/shard_map/ppermute | solution.py:36
  223.5 10.3 %collective-permute-start.25 = (bf16[128,2048]{1,0:T(8,128)(2,1)S(1)}, bf16[128,2048]{1,0:T(8,128)(2,1)S(1)}, u32[]{:S(2)}, u32[]{:S(2)}) collective-permute-start(bf16[128,2048]{1,0:T(8,128)(2,1)S(1)} %collective-permute-done.24.refs_1_), channel_id=1, source_target_pairs={{0,16},{16,0},{1,17},{17,1},{2,18},{18,2},{3,19},{19,3},{4,20},{20... | collective-permute-start | bytes 1572872 | tf_op jit(solution)/shard_map/ppermute | solution.py:40
  224.0 9.8 %collective-permute-start.26 = (bf16[128,2048]{1,0:T(8,128)(2,1)S(1)}, bf16[128,2048]{1,0:T(8,128)(2,1)S(1)}, u32[]{:S(2)}, u32[]{:S(2)}) collective-permute-start(bf16[128,2048]{1,0:T(8,128)(2,1)S(1)} %collective-permute-done.23.refs_0_), channel_id=1, source_target_pairs={{0,16},{16,0},{1,17},{17,1},{2,18},{18,2},{3,19},{19,3},{4,20},{20... | collective-permute-start | bytes 1572872 | tf_op jit(solution)/shard_map/ppermute | solution.py:40
  233.4 8.8 %collective-permute-start.31 = (bf16[128,2048]{1,0:T(8,128)(2,1)S(1)}, bf16[128,2048]{1,0:T(8,128)(2,1)S(1)}, u32[]{:S(2)}, u32[]{:S(2)}) collective-permute-start(bf16[128,2048]{1,0:T(8,128)(2,1)S(1)} %slice.44), channel_id=1, source_target_pairs={{0,16},{16,0},{1,17},{17,1},{2,18},{18,2},{3,19},{19,3},{4,20},{20... | collective-permute-start | bytes 1572872 | tf_op jit(solution)/shard_map/ppermute | solution.py:40
  241.6 7.8 %collective-permute-start.27 = (bf16[256,2048]{1,0:T(8,128)(2,1)S(1)}, bf16[256,2048]{1,0:T(8,128)(2,1)S(1)}, u32[]{:S(2)}, u32[]{:S(2)}) collective-permute-start(bf16[256,2048]{1,0:T(8,128)(2,1)S(1)} %slice.39), channel_id=1, source_target_pairs={{0,16},{16,0},{1,17},{17,1},{2,18},{18,2},{3,19},{19,3},{4,20},{20... | collective-permute-start | bytes 3145736 | tf_op jit(solution)/shard_map/ppermute | solution.py:40
  242.3 10.5 %collective-permute-start.32 = (bf16[128,2048]{1,0:T(8,128)(2,1)S(1)}, bf16[128,2048]{1,0:T(8,128)(2,1)S(1)}, u32[]{:S(2)}, u32[]{:S(2)}) collective-permute-start(bf16[128,2048]{1,0:T(8,128)(2,1)S(1)} %add_convert_fusion.2), channel_id=1, source_target_pairs={{0,1},{1,2},{2,3},{3,0},{16,19},{17,16},{18,17},{19,18},{4,5},{5,6... | collective-permute-start | bytes 1572872 | tf_op jit(solution)/shard_map/ppermute | solution.py:36
  249.8 14.4 %collective-permute-start.28 = (bf16[128,2048]{1,0:T(8,128)(2,1)S(1)}, bf16[128,2048]{1,0:T(8,128)(2,1)S(1)}, u32[]{:S(2)}, u32[]{:S(2)}) collective-permute-start(bf16[128,2048]{1,0:T(8,128)(2,1)S(1)} %get-tuple-element.24), channel_id=1, source_target_pairs={{0,3},{1,0},{2,1},{3,2},{16,17},{17,18},{18,19},{19,16},{4,7},{5,4... | collective-permute-start | bytes 1572872 | tf_op jit(solution)/shard_map/ppermute | solution.py:36
  252.9 12.1 %collective-permute-start.33 = (bf16[128,2048]{1,0:T(8,128)(2,1)S(1)}, bf16[128,2048]{1,0:T(8,128)(2,1)S(1)}, u32[]{:S(2)}, u32[]{:S(2)}) collective-permute-start(bf16[128,2048]{1,0:T(8,128)(2,1)S(1)} %add_convert_fusion.1), channel_id=1, source_target_pairs={{0,1},{1,2},{2,3},{3,0},{16,19},{17,16},{18,17},{19,18},{4,5},{5,6... | collective-permute-start | bytes 1572872 | tf_op jit(solution)/shard_map/ppermute | solution.py:36
  (20 other events, 274.9 us)
Sparse Core Ops, SparseCore 0:
  11.4 98.4 all-gather.1

commit v6 on v5

--- a/solution.py
+++ b/solution.py
@@ -373,12 +373,22 @@
     before = wide_add(near_part[:ROWS], got_near[ROWS:])
     after = wide_add(near_part[ROWS : 2 * ROWS], got_near[:ROWS])
     far = wide_add(far_part[:ROWS], other_core(far_part[ROWS:])).astype(BF16)
-    far = around(far, 1)
-    before, after = lax.optimization_barrier((before.astype(BF16), after))
-    before = around(before, -1)
-    after = around(wide_add(after, far).astype(BF16), 1)
+    half = ROWS // 2
+    far_top = around(far[:half], 1)
+    far_bottom = around(far[half:], -1)
+    early_after = around(after[half:].astype(BF16), 1)
+    early_before = around(before[:half].astype(BF16), -1)
+    far_top, far_bottom = lax.optimization_barrier((far_top, far_bottom))
+    late_after = around(wide_add(after[:half], far_top).astype(BF16), 1)
+    late_before = around(wide_add(before[half:], far_bottom).astype(BF16), -1)
     own = wide_add(own_part[:ROWS], got_own)
-    total = own + wide_add(before, after)
+    total = jnp.concatenate(
+        [
+            own[:half] + wide_add(late_after, early_before),
+            own[half:] + wide_add(early_after, late_before),
+        ],
+        axis=0,
+    )
     return attended, (attended.astype(F32) + total).astype(BF16)
 
 

time: 274 us -> 276 us (level)
  starting transfers between devices: 30 us -> 37.3 us
  waiting for transfers between devices: 115 us -> 109 us
    ppermute x12 -> x15, starting transfers between devices: 11.9 us -> 19.1 us  [around(): return lax.ppermute(array, ('c', 'y'), pairs)]
    ppermute x16, waiting for transfers between devices: 5.74 us -> 2.56 us  [other_core(): return lax.ppermute(array, 'c', [(0, 1), (1, 0)])]
    ppermute x12 -> x15, waiting for transfers between devices: 71.9 us -> 69.9 us  [around(): return lax.ppermute(array, ('c', 'y'), pairs)]
  transfers between devices with their start and end apart: 37 -> 40, of which waited for: 16 -> 17; matrix products, arithmetic and copies ran while one was open for 1% -> 2% of each run, Pallas kernels for 22% -> 22%
where the time goes in v6:
time: 276 us; the launch traced here: 275 us
  waiting for transfers between devices  109 us (39%)
  Pallas kernels  66.6 us (24%)
  starting transfers between devices  37.3 us (14%)
  blocking collectives  32.4 us (12%)
  between operations  14.6 us (5%)
  local copies, waits for them, and re-layouts  8.96 us (3%)
  other arithmetic  6.26 us (2%)
    ppermute x15, waiting for transfers between devices, around(): return lax.ppermute(array, ('c', 'y'), pairs)  69.9 us
    pallas_call x4, Pallas kernels, attend(): pl.pallas_call(functools.partial(attend_body, first, last, n_pairs, zs),...  45.5 us
    all_to_all x1, blocking collectives, regroup(): lax.all_to_all(array, ('z', 'x'), split_axis=0, concat_axis=0, tiled=True)  32.4 us
    ppermute x6, waiting for transfers between devices, along(): return lax.ppermute(array, axis, [(i, (i + step) % 4) for i in range(4)])  24.8 us
    ppermute x15, starting transfers between devices, around(): return lax.ppermute(array, ('c', 'y'), pairs)  19.1 us
    pallas_call x3, Pallas kernels, ffn(): pl.pallas_call(functools.partial(ffn_body, n), out_shape=jax.ShapeDtypeSt...  15.2 us
    all_to_all x2, waiting for transfers between devices, regroup(): lax.all_to_all(array, ('z', 'x'), split_axis=0, concat_axis=0, tiled=True)  12 us
    unnamed x30, local copies, waits for them, and re-layouts  7.62 us
  transfers between devices with their start and end apart: 40, of which 17 were waited for; matrix products, arithmetic and copies ran while one was open for 2% of the time, Pallas kernels for 22%

profile of v6, /device:TPU:0, one launch (start us, length us, event | category | flops | bytes accessed | tf_op | source)
XLA Modules:
  0.0 275.4 jit_solution(12585786345508280406)
XLA Ops:
  11.5 32.4 %all_to_all.15 = bf16[16,128,256]{2,1,0:T(8,128)(2,1)S(1)} all-to-all(bf16[16,128,256]{2,1,0:T(8,128)(2,1)S(1)} %shard_map.104), channel_id=1, replica_groups=mesh['z'=4,'c'=2,'x'=4,'y'=4] {'z','x'}, dimensions={0} | all-to-all | bytes 2097152 | tf_op jit(solution)/shard_map/all_to_all | solution.py:315
  46.1 2.8 %collective-permute-start.10 = (bf16[256,128]{1,0:T(8,128)(2,1)S(1)}, bf16[256,128]{1,0:T(8,128)(2,1)S(1)}, u32[]{:S(2)}, u32[]{:S(2)}) collective-permute-start(bf16[256,128]{1,0:T(8,128)(2,1)S(1)} %copy-done.10), channel_id=1, source_target_pairs={{0,12},{4,0},{8,4},{12,8},{1,13},{5,1},{9,5},{13,9},{2,14},{6,2},{... | collective-permute-start | bytes 196616 | tf_op jit(solution)/shard_map/ppermute | solution.py:31
  48.8 2.9 %collective-permute-done.8 = bf16[256,128]{1,0:T(8,128)(2,1)S(1)} collective-permute-done((bf16[256,128]{1,0:T(8,128)(2,1)S(1)}, bf16[256,128]{1,0:T(8,128)(2,1)S(1)}, u32[]{:S(2)}, u32[]{:S(2)}) %collective-permute-start.8) | collective-permute-done | bytes 65568 | tf_op jit(solution)/shard_map/ppermute | solution.py:31
  52.8 2.4 collective-permute-start.12
  56.4 11.8 %collective-permute-done.11 = bf16[4,256,128]{2,1,0:T(8,128)(2,1)S(1)} collective-permute-done((bf16[4,256,128]{2,1,0:T(8,128)(2,1)S(1)}, bf16[4,256,128]{2,1,0:T(8,128)(2,1)S(1)}, u32[]{:S(2)}, u32[]{:S(2)}) %collective-permute-start.11) | collective-permute-done | bytes 262176 | tf_op jit(solution)/shard_map/ppermute | solution.py:31
  68.2 5.0 %collective-permute-done.12 = bf16[4,256,128]{2,1,0:T(8,128)(2,1)S(1)} collective-permute-done((bf16[4,256,128]{2,1,0:T(8,128)(2,1)S(1)}, bf16[4,256,128]{2,1,0:T(8,128)(2,1)S(1)}, u32[]{:S(2)}, u32[]{:S(2)}) %collective-permute-start.12) | collective-permute-done | bytes 262176 | tf_op jit(solution)/shard_map/ppermute | solution.py:31
  73.2 4.2 %collective-permute-done.13 = bf16[4,256,128]{2,1,0:T(8,128)(2,1)S(1)} collective-permute-done((bf16[4,256,128]{2,1,0:T(8,128)(2,1)S(1)}, bf16[4,256,128]{2,1,0:T(8,128)(2,1)S(1)}, u32[]{:S(2)}, u32[]{:S(2)}) %collective-permute-start.13) | collective-permute-done | bytes 262176 | tf_op jit(solution)/shard_map/ppermute | solution.py:31
  78.6 3.2 %collective-permute-start.3 = (bf16[2048,256]{1,0:T(8,128)(2,1)S(1)}, bf16[2048,256]{1,0:T(8,128)(2,1)}, u32[]{:S(2)}, u32[]{:S(2)}) collective-permute-start(bf16[2048,256]{1,0:T(8,128)(2,1)S(1)} %bitcast.62), channel_id=1, source_target_pairs={{0,3},{1,0},{2,1},{3,2},{16,17},{17,18},{18,19},{19,16},{4,7},{5,4... | collective-permute-start | bytes 3145736 | tf_op jit(solution)/shard_map/ppermute | solution.py:36
  81.8 3.2 %collective-permute-start.16 = (bf16[16,256,128]{2,1,0:T(8,128)(2,1)}, bf16[16,256,128]{2,1,0:T(8,128)(2,1)}, u32[]{:S(2)}, u32[]{:S(2)}) collective-permute-start(bf16[16,256,128]{2,1,0:T(8,128)(2,1)} %bitcast.32.refs_0_), channel_id=1, source_target_pairs={{0,3},{1,0},{2,1},{3,2},{16,17},{17,18},{18,19},{19,16},{4,7},{5,4... | collective-permute-start | bytes 3145736 | tf_op jit(solution)/shard_map/ppermute | solution.py:36
  85.0 21.1 %collective-permute-done.15.refs_2_ = bf16[16,256,128]{2,1,0:T(8,128)(2,1)} collective-permute-done((bf16[16,256,128]{2,1,0:T(8,128)(2,1)}, bf16[16,256,128]{2,1,0:T(8,128)(2,1)}, u32[]{:S(2)}, u32[]{:S(2)}) %collective-permute-start.15) | collective-permute-done | bytes 1048608 | tf_op jit(solution)/shard_map/ppermute | solution.py:36
  108.5 3.6 %all-to-all-start = ((bf16[16,128,128]{2,1,0:T(8,128)(2,1)}), bf16[16,128,128]{2,1,0:T(8,128)(2,1)S(1)}, u32[]{:S(2)}, u32[]{:S(2)}) async-start(bf16[16,128,128]{2,1,0:T(8,128)(2,1)} %bitcast_bitcast_fusion), calls=%async_computation | async-start | bytes 1048576 | tf_op jit(solution)/shard_map/all_to_all | solution.py:315
  112.2 15.9 %collective-permute-done.1.refs_0_ = bf16[2048,256]{1,0:T(8,128)(2,1)S(1)} collective-permute-done((bf16[2048,256]{1,0:T(8,128)(2,1)}, bf16[2048,256]{1,0:T(8,128)(2,1)S(1)}, u32[]{:S(2)}, u32[]{:S(2)}) %collective-permute-start.1) | collective-permute-done | bytes 1048608 | tf_op jit(solution)/shard_map/ppermute | solution.py:36
  130.8 11.4 %shard_map.105 = (f32[2048,128]{1,0:T(8,128)}, f32[2048,128]{1,0:T(8,128)}, f32[2048,128]{1,0:T(8,128)}) custom-call(s32[3]{0:T(128)S(1)} %pad_add_fusion.3.where_ref, bf16[2048,128]{1,0:T(8,128)(2,1)S(1)} %bitcast.56, bf16[2048,256]{1,0:T(8,128)(2,1)S(1)} %bitcast.63, bf16[2048,256]{1,0:T(8,128)(2,1)S(1)} %copy-done.8), custom_call_target="tpu_custom_call" | custom-call | flops 2684354560 | bytes 2097152 | tf_op jit(solution)/shard_map/pallas_call | solution.py:177
  143.6 20.4 %shard_map.106 = (f32[2048,128]{1,0:T(8,128)}, f32[2048,128]{1,0:T(8,128)}, f32[2048,128]{1,0:T(8,128)}) custom-call(s32[4]{0:T(128)S(1)} %pad_add_fusion.2.where_ref, bf16[2048,128]{1,0:T(8,128)(2,1)S(1)} %bitcast.57, bf16[2048,256]{1,0:T(8,128)(2,1)} %collective-permute-done.refs_0_, bf16[2048,256]{1,0:T(8,128)(2,1)} %collective-permute-done.4.refs_1_, ...), custom_call_target="tpu_custom_call" | custom-call | flops 5368709120 | bytes 4194304 | tf_op jit(solution)/shard_map/pallas_call | solution.py:177
  164.0 5.8 %shard_map.108 = bf16[512,128]{1,0:T(8,128)(2,1)S(1)} custom-call(s32[3]{0:T(128)S(1)} %pad_add_fusion.where_ref, bf16[2048,128]{1,0:T(8,128)(2,1)S(1)} %bitcast.58, bf16[2048,256]{1,0:T(8,128)(2,1)S(1)} %collective-permute-done.1.refs_0_, bf16[2048,256]{1,0:T(8,128)(2,1)S(1)} %collective-permute-done.2.refs_1_, f32[2048,128]{1,0:T(8,128)} %get-tuple-element.17.refs_2_, ...), custom_call_target="tpu_custom_call" | custom-call | flops 1073741824 | bytes 2097152 | tf_op jit(solution)/shard_map/pallas_call | solution.py:177
  169.8 8.0 %shard_map.107 = bf16[1536,128]{1,0:T(8,128)(2,1)S(1)} custom-call(s32[3]{0:T(128)S(1)} %pad_add_fusion.where_ref, bf16[2048,128]{1,0:T(8,128)(2,1)S(1)} %bitcast.59, bf16[2048,256]{1,0:T(8,128)(2,1)S(1)} %collective-permute-done.1.refs_0_, bf16[2048,256]{1,0:T(8,128)(2,1)S(1)} %collective-permute-done.2.refs_1_, f32[2048,128]{1,0:T(8,128)} %get-tuple-element.17.refs_2_, ...), custom_call_target="tpu_custom_call" | custom-call | flops 1610612736 | bytes 2097152 | tf_op jit(solution)/shard_map/pallas_call | solution.py:177
  178.6 3.6 %all-to-all-start.2 = ((bf16[16,128,128]{2,1,0:T(8,128)(2,1)}), bf16[16,128,128]{2,1,0:T(8,128)(2,1)S(1)}, u32[]{:S(2)}, u32[]{:S(2)}) async-start(bf16[16,128,128]{2,1,0:T(8,128)(2,1)} %bitcast.11), calls=%async_computation.2 | async-start | bytes 1048576 | tf_op jit(solution)/shard_map/all_to_all | solution.py:315
  182.3 12.0 %all-to-all-done.2.attn_ref = bf16[16,128,128]{2,1,0:T(8,128)(2,1)S(1)} async-done(((bf16[16,128,128]{2,1,0:T(8,128)(2,1)}), bf16[16,128,128]{2,1,0:T(8,128)(2,1)S(1)}, u32[]{:S(2)}, u32[]{:S(2)}) %all-to-all-start.2) | async-done | bytes 524320 | tf_op jit(solution)/shard_map/all_to_all | solution.py:315
  194.4 5.7 %shard_map.109 = (bf16[128,2048]{1,0:T(8,128)(2,1)}, bf16[128,2048]{1,0:T(8,128)(2,1)S(1)}) custom-call(s32[7]{0:T(128)S(1)} %stack.107.where_ref, bf16[16,128,128]{2,1,0:T(8,128)(2,1)S(1)} %all-to-all-done.2.attn_ref, bf16[128,2048]{1,0:T(8,128)(2,1)S(1)} %copy-done.4, bf16[1,2048]{1,0:T(2,128)(2,1)S(1)} %reshape.41.gain_ref, ...), custom_call_target="tpu_custom_call" | custom-call | flops 1073741824 | bytes 8388608 | tf_op jit(solution)/shard_map/pallas_call | solution.py:231
  200.1 10.4 %collective-permute-done.23.refs_0_ = bf16[128,2048]{1,0:T(8,128)(2,1)S(1)} collective-permute-done((bf16[128,2048]{1,0:T(8,128)(2,1)S(1)}, bf16[128,2048]{1,0:T(8,128)(2,1)S(1)}, u32[]{:S(2)}, u32[]{:S(2)}) %collective-permute-start.23) | collective-permute-done | bytes 524320 | tf_op jit(solution)/shard_map/ppermute | solution.py:36
  210.5 3.2 %collective-permute-start.24 = (bf16[128,2048]{1,0:T(8,128)(2,1)S(1)}, bf16[128,2048]{1,0:T(8,128)(2,1)S(1)}, u32[]{:S(2)}, u32[]{:S(2)}) collective-permute-start(bf16[128,2048]{1,0:T(8,128)(2,1)S(1)} %get-tuple-element.23.refs_0_), channel_id=1, source_target_pairs={{0,3},{1,0},{2,1},{3,2},{16,17},{17,18},{18,19},{19,16},{4,7},{5,4... | collective-permute-start | bytes 1572872 | tf_op jit(solution)/shard_map/ppermute | solution.py:36
  213.8 9.7 %collective-permute-done.28.refs_0_ = bf16[128,2048]{1,0:T(8,128)(2,1)S(1)} collective-permute-done((bf16[128,2048]{1,0:T(8,128)(2,1)S(1)}, bf16[128,2048]{1,0:T(8,128)(2,1)S(1)}, u32[]{:S(2)}, u32[]{:S(2)}) %collective-permute-start.28) | collective-permute-done | bytes 524320 | tf_op jit(solution)/shard_map/ppermute | solution.py:36
  225.4 4.1 %copy-done.1 = bf16[21504,256]{1,0:T(8,128)(2,1)S(1)} copy-done((bf16[21504,256]{1,0:T(8,128)(2,1)S(1)}, bf16[21504,256]{1,0:T(8,128)(2,1)}, u32[]{:S(2)}) %copy-start.1) | copy-done | bytes 11010072
  229.5 3.7 %shard_map.112 = bf16[256,2048]{1,0:T(8,128)(2,1)S(1)} custom-call(bf16[16,3,2,224,256]{4,3,2,1,0:T(8,128)(2,1)S(1)} %bitcast.51, bf16[128,2048]{1,0:T(8,128)(2,1)S(1)} %collective-permute-done.28.refs_0_, bf16[128,2048]{1,0:T(8,128)(2,1)S(1)} %collective-permute-done.29.refs_1_), custom_call_target="tpu_custom_call" | custom-call | flops 2818572288 | bytes 11010048 | tf_op jit(solution)/shard_map/pallas_call | solution.py:277
  233.8 7.7 %shard_map.111 = bf16[512,2048]{1,0:T(8,128)(2,1)S(1)} custom-call(bf16[16,3,2,224,256]{4,3,2,1,0:T(8,128)(2,1)S(1)} %bitcast.52, bf16[128,2048]{1,0:T(8,128)(2,1)S(1)} %collective-permute-done.23.refs_0_, bf16[128,2048]{1,0:T(8,128)(2,1)S(1)} %collective-permute-done.24.refs_1_, bf16[128,2048]{1,0:T(8,128)(2,1)S(1)} %collective-permute-done.25.refs_2_, ...), custom_call_target="tpu_custom_call" | custom-call | flops 5637144576 | bytes 11010048 | tf_op jit(solution)/shard_map/pallas_call | solution.py:277
  242.1 3.8 %shard_map.110 = bf16[256,2048]{1,0:T(8,128)(2,1)S(1)} custom-call(bf16[16,3,2,224,256]{4,3,2,1,0:T(8,128)(2,1)S(1)} %bitcast.55, bf16[128,2048]{1,0:T(8,128)(2,1)S(1)} %get-tuple-element.23.refs_0_, bf16[128,2048]{1,0:T(8,128)(2,1)S(1)} %collective-permute-done.21.refs_1_), custom_call_target="tpu_custom_call" | custom-call | flops 2818572288 | bytes 11010048 | tf_op jit(solution)/shard_map/pallas_call | solution.py:277
  246.4 3.2 %collective-permute-start.32 = (bf16[64,2048]{1,0:T(8,128)(2,1)S(1)}, bf16[64,2048]{1,0:T(8,128)(2,1)S(1)}, u32[]{:S(2)}, u32[]{:S(2)}) collective-permute-start(bf16[64,2048]{1,0:T(8,128)(2,1)S(1)} %get-tuple-element.32), channel_id=1, source_target_pairs={{0,3},{1,0},{2,1},{3,2},{16,17},{17,18},{18,19},{19,16},{4,7},{5,4... | collective-permute-start | bytes 786440 | tf_op jit(solution)/shard_map/ppermute | solution.py:36
  250.1 2.1 collective-permute-start.35
  252.2 4.5 %collective-permute-done.31 = bf16[64,2048]{1,0:T(8,128)(2,1)S(1)} collective-permute-done((bf16[64,2048]{1,0:T(8,128)(2,1)S(1)}, bf16[64,2048]{1,0:T(8,128)(2,1)S(1)}, u32[]{:S(2)}, u32[]{:S(2)}) %collective-permute-start.31) | collective-permute-done | bytes 262176 | tf_op jit(solution)/shard_map/ppermute | solution.py:36
  256.8 2.1 collective-permute-start.36
  259.2 2.0 collective-permute-done.34
  262.3 3.8 %collective-permute-done.36 = bf16[64,2048]{1,0:T(8,128)(2,1)S(1)} collective-permute-done((bf16[64,2048]{1,0:T(8,128)(2,1)S(1)}, bf16[64,2048]{1,0:T(8,128)(2,1)S(1)}, u32[]{:S(2)}, u32[]{:S(2)}) %collective-permute-start.36) | collective-permute-done | bytes 262176 | tf_op jit(solution)/shard_map/ppermute | solution.py:36
  (116 shorter events, 25.0 us)
Async XLA Ops:
  7.2 187.2 %all-gather.2.cloned.1.call-start = ((), (), s32[]{:S(2)}) async-start(), calls=%async_computation.3 | async-start | bytes 11698176 | tf_op jit(solution)/shard_map/all_gather | solution.py:335
  43.8 38.0 %collective-permute-start = (bf16[2048,256]{1,0:T(8,128)(2,1)S(1)}, bf16[2048,256]{1,0:T(8,128)(2,1)}, u32[]{:S(2)}, u32[]{:S(2)}) collective-permute-start(bf16[2048,256]{1,0:T(8,128)(2,1)S(1)} %bitcast.60), channel_id=1, source_target_pairs={{0,1},{1,2},{2,3},{3,0},{16,19},{17,16},{18,17},{19,18},{4,5},{5,6... | collective-permute-start | bytes 3145736 | tf_op jit(solution)/shard_map/ppermute | solution.py:36
  52.7 15.5 %collective-permute-start.11 = (bf16[4,256,128]{2,1,0:T(8,128)(2,1)S(1)}, bf16[4,256,128]{2,1,0:T(8,128)(2,1)S(1)}, u32[]{:S(2)}, u32[]{:S(2)}) collective-permute-start(bf16[4,256,128]{2,1,0:T(8,128)(2,1)S(1)} %pad_maximum_fusion.4), channel_id=1, source_target_pairs={{0,32},{32,64},{64,96},{96,0},{1,33},{33,65},{65,97},{97,1},{2,34}... | collective-permute-start | bytes 786440 | tf_op jit(solution)/shard_map/ppermute | solution.py:31
  52.8 20.4 %collective-permute-start.12 = (bf16[4,256,128]{2,1,0:T(8,128)(2,1)S(1)}, bf16[4,256,128]{2,1,0:T(8,128)(2,1)S(1)}, u32[]{:S(2)}, u32[]{:S(2)}) collective-permute-start(bf16[4,256,128]{2,1,0:T(8,128)(2,1)S(1)} %pad_maximum_fusion.4), channel_id=1, source_target_pairs={{0,64},{32,96},{64,0},{96,32},{1,65},{33,97},{65,1},{97,33},{2,66}... | collective-permute-start | bytes 786440 | tf_op jit(solution)/shard_map/ppermute | solution.py:31
  55.1 22.3 %collective-permute-start.13 = (bf16[4,256,128]{2,1,0:T(8,128)(2,1)S(1)}, bf16[4,256,128]{2,1,0:T(8,128)(2,1)S(1)}, u32[]{:S(2)}, u32[]{:S(2)}) collective-permute-start(bf16[4,256,128]{2,1,0:T(8,128)(2,1)S(1)} %pad_maximum_fusion.4), channel_id=1, source_target_pairs={{0,96},{32,0},{64,32},{96,64},{1,97},{33,1},{65,33},{97,65},{2,98}... | collective-permute-start | bytes 786440 | tf_op jit(solution)/shard_map/ppermute | solution.py:31
  78.6 27.6 %collective-permute-start.15 = (bf16[16,256,128]{2,1,0:T(8,128)(2,1)}, bf16[16,256,128]{2,1,0:T(8,128)(2,1)}, u32[]{:S(2)}, u32[]{:S(2)}) collective-permute-start(bf16[16,256,128]{2,1,0:T(8,128)(2,1)} %bitcast.32.refs_0_), channel_id=1, source_target_pairs={{0,1},{1,2},{2,3},{3,0},{16,19},{17,16},{18,17},{19,18},{4,5},{5,6... | collective-permute-start | bytes 3145736 | tf_op jit(solution)/shard_map/ppermute | solution.py:36
  78.6 27.6 %collective-permute-start.6 = (bf16[2048,256]{1,0:T(8,128)(2,1)S(1)}, bf16[2048,256]{1,0:T(8,128)(2,1)S(1)}, u32[]{:S(2)}, u32[]{:S(2)}) collective-permute-start(bf16[2048,256]{1,0:T(8,128)(2,1)S(1)} %bitcast.61), channel_id=1, source_target_pairs={{0,16},{16,0},{1,17},{17,1},{2,18},{18,2},{3,19},{19,3},{4,20},{20... | collective-permute-start | bytes 3145736 | tf_op jit(solution)/shard_map/ppermute | solution.py:40
  78.6 28.5 %collective-permute-start.3 = (bf16[2048,256]{1,0:T(8,128)(2,1)S(1)}, bf16[2048,256]{1,0:T(8,128)(2,1)}, u32[]{:S(2)}, u32[]{:S(2)}) collective-permute-start(bf16[2048,256]{1,0:T(8,128)(2,1)S(1)} %bitcast.62), channel_id=1, source_target_pairs={{0,3},{1,0},{2,1},{3,2},{16,17},{17,18},{18,19},{19,16},{4,7},{5,4... | collective-permute-start | bytes 3145736 | tf_op jit(solution)/shard_map/ppermute | solution.py:36
  81.8 46.3 %collective-permute-start.1 = (bf16[2048,256]{1,0:T(8,128)(2,1)}, bf16[2048,256]{1,0:T(8,128)(2,1)S(1)}, u32[]{:S(2)}, u32[]{:S(2)}) collective-permute-start(bf16[2048,256]{1,0:T(8,128)(2,1)} %collective-permute-done.refs_0_), channel_id=1, source_target_pairs={{0,1},{1,2},{2,3},{3,0},{16,19},{17,16},{18,17},{19,18},{4,5},{5,6... | collective-permute-start | bytes 3145736 | tf_op jit(solution)/shard_map/ppermute | solution.py:36
  81.8 60.4 %collective-permute-start.16 = (bf16[16,256,128]{2,1,0:T(8,128)(2,1)}, bf16[16,256,128]{2,1,0:T(8,128)(2,1)}, u32[]{:S(2)}, u32[]{:S(2)}) collective-permute-start(bf16[16,256,128]{2,1,0:T(8,128)(2,1)} %bitcast.32.refs_0_), channel_id=1, source_target_pairs={{0,3},{1,0},{2,1},{3,2},{16,17},{17,18},{18,19},{19,16},{4,7},{5,4... | collective-permute-start | bytes 3145736 | tf_op jit(solution)/shard_map/ppermute | solution.py:36
  106.1 36.7 %collective-permute-start.19 = (bf16[16,256,128]{2,1,0:T(8,128)(2,1)}, bf16[16,256,128]{2,1,0:T(8,128)(2,1)}, u32[]{:S(2)}, u32[]{:S(2)}) collective-permute-start(bf16[16,256,128]{2,1,0:T(8,128)(2,1)} %collective-permute-done.15.refs_2_), channel_id=1, source_target_pairs={{0,1},{1,2},{2,3},{3,0},{16,19},{17,16},{18,17},{19,18},{4,5},{5,6... | collective-permute-start | bytes 3145736 | tf_op jit(solution)/shard_map/ppermute | solution.py:36
  107.1 35.8 %collective-permute-start.5 = (bf16[2048,256]{1,0:T(8,128)(2,1)}, bf16[2048,256]{1,0:T(8,128)(2,1)}, u32[]{:S(2)}, u32[]{:S(2)}) collective-permute-start(bf16[2048,256]{1,0:T(8,128)(2,1)} %collective-permute-done.refs_0_), channel_id=1, source_target_pairs={{0,16},{16,0},{1,17},{17,1},{2,18},{18,2},{3,19},{19,3},{4,20},{20... | collective-permute-start | bytes 3145736 | tf_op jit(solution)/shard_map/ppermute | solution.py:40
  107.1 36.2 %collective-permute-start.4 = (bf16[2048,256]{1,0:T(8,128)(2,1)}, bf16[2048,256]{1,0:T(8,128)(2,1)}, u32[]{:S(2)}, u32[]{:S(2)}) collective-permute-start(bf16[2048,256]{1,0:T(8,128)(2,1)} %collective-permute-done.3.refs_2_), channel_id=1, source_target_pairs={{0,16},{16,0},{1,17},{17,1},{2,18},{18,2},{3,19},{19,3},{4,20},{20... | collective-permute-start | bytes 3145736 | tf_op jit(solution)/shard_map/ppermute | solution.py:40
  108.5 19.8 %all-to-all-start = ((bf16[16,128,128]{2,1,0:T(8,128)(2,1)}), bf16[16,128,128]{2,1,0:T(8,128)(2,1)S(1)}, u32[]{:S(2)}, u32[]{:S(2)}) async-start(bf16[16,128,128]{2,1,0:T(8,128)(2,1)} %bitcast_bitcast_fusion), calls=%async_computation | async-start | bytes 1048576 | tf_op jit(solution)/shard_map/all_to_all | solution.py:315
  128.1 35.9 %collective-permute-start.2 = (bf16[2048,256]{1,0:T(8,128)(2,1)S(1)}, bf16[2048,256]{1,0:T(8,128)(2,1)S(1)}, u32[]{:S(2)}, u32[]{:S(2)}) collective-permute-start(bf16[2048,256]{1,0:T(8,128)(2,1)S(1)} %collective-permute-done.1.refs_0_), channel_id=1, source_target_pairs={{0,16},{16,0},{1,17},{17,1},{2,18},{18,2},{3,19},{19,3},{4,20},{20... | collective-permute-start | bytes 3145736 | tf_op jit(solution)/shard_map/ppermute | solution.py:40
  142.2 52.1 %collective-permute-start.14 = (bf16[16,256,128]{2,1,0:T(8,128)(2,1)}, bf16[16,256,128]{2,1,0:T(8,128)(2,1)}, u32[]{:S(2)}, u32[]{:S(2)}) collective-permute-start(bf16[16,256,128]{2,1,0:T(8,128)(2,1)} %bitcast.32.refs_0_), channel_id=1, source_target_pairs={{0,16},{16,0},{1,17},{17,1},{2,18},{18,2},{3,19},{19,3},{4,20},{20... | collective-permute-start | bytes 3145736 | tf_op jit(solution)/shard_map/ppermute | solution.py:40
  142.8 51.6 %collective-permute-start.18 = (bf16[16,256,128]{2,1,0:T(8,128)(2,1)}, bf16[16,256,128]{2,1,0:T(8,128)(2,1)}, u32[]{:S(2)}, u32[]{:S(2)}) collective-permute-start(bf16[16,256,128]{2,1,0:T(8,128)(2,1)} %collective-permute-done.15.refs_2_), channel_id=1, source_target_pairs={{0,16},{16,0},{1,17},{17,1},{2,18},{18,2},{3,19},{19,3},{4,20},{20... | collective-permute-start | bytes 3145736 | tf_op jit(solution)/shard_map/ppermute | solution.py:40
  142.9 51.5 %collective-permute-start.17 = (bf16[16,256,128]{2,1,0:T(8,128)(2,1)}, bf16[16,256,128]{2,1,0:T(8,128)(2,1)}, u32[]{:S(2)}, u32[]{:S(2)}) collective-permute-start(bf16[16,256,128]{2,1,0:T(8,128)(2,1)} %collective-permute-done.16.refs_4_), channel_id=1, source_target_pairs={{0,16},{16,0},{1,17},{17,1},{2,18},{18,2},{3,19},{19,3},{4,20},{20... | collective-permute-start | bytes 3145736 | tf_op jit(solution)/shard_map/ppermute | solution.py:40
  143.3 51.0 %collective-permute-start.20 = (bf16[16,256,128]{2,1,0:T(8,128)(2,1)}, bf16[16,256,128]{2,1,0:T(8,128)(2,1)}, u32[]{:S(2)}, u32[]{:S(2)}) collective-permute-start(bf16[16,256,128]{2,1,0:T(8,128)(2,1)} %collective-permute-done.19.refs_6_), channel_id=1, source_target_pairs={{0,16},{16,0},{1,17},{17,1},{2,18},{18,2},{3,19},{19,3},{4,20},{20... | collective-permute-start | bytes 3145736 | tf_op jit(solution)/shard_map/ppermute | solution.py:40
  178.6 15.7 %all-to-all-start.2 = ((bf16[16,128,128]{2,1,0:T(8,128)(2,1)}), bf16[16,128,128]{2,1,0:T(8,128)(2,1)S(1)}, u32[]{:S(2)}, u32[]{:S(2)}) async-start(bf16[16,128,128]{2,1,0:T(8,128)(2,1)} %bitcast.11), calls=%async_computation.2 | async-start | bytes 1048576 | tf_op jit(solution)/shard_map/all_to_all | solution.py:315
  200.1 10.4 %collective-permute-start.23 = (bf16[128,2048]{1,0:T(8,128)(2,1)S(1)}, bf16[128,2048]{1,0:T(8,128)(2,1)S(1)}, u32[]{:S(2)}, u32[]{:S(2)}) collective-permute-start(bf16[128,2048]{1,0:T(8,128)(2,1)S(1)} %get-tuple-element.23.refs_0_), channel_id=1, source_target_pairs={{0,1},{1,2},{2,3},{3,0},{16,19},{17,16},{18,17},{19,18},{4,5},{5,6... | collective-permute-start | bytes 1572872 | tf_op jit(solution)/shard_map/ppermute | solution.py:36
  210.5 13.0 %collective-permute-start.28 = (bf16[128,2048]{1,0:T(8,128)(2,1)S(1)}, bf16[128,2048]{1,0:T(8,128)(2,1)S(1)}, u32[]{:S(2)}, u32[]{:S(2)}) collective-permute-start(bf16[128,2048]{1,0:T(8,128)(2,1)S(1)} %collective-permute-done.23.refs_0_), channel_id=1, source_target_pairs={{0,1},{1,2},{2,3},{3,0},{16,19},{17,16},{18,17},{19,18},{4,5},{5,6... | collective-permute-start | bytes 1572872 | tf_op jit(solution)/shard_map/ppermute | solution.py:36
  210.5 13.0 %collective-permute-start.24 = (bf16[128,2048]{1,0:T(8,128)(2,1)S(1)}, bf16[128,2048]{1,0:T(8,128)(2,1)S(1)}, u32[]{:S(2)}, u32[]{:S(2)}) collective-permute-start(bf16[128,2048]{1,0:T(8,128)(2,1)S(1)} %get-tuple-element.23.refs_0_), channel_id=1, source_target_pairs={{0,3},{1,0},{2,1},{3,2},{16,17},{17,18},{18,19},{19,16},{4,7},{5,4... | collective-permute-start | bytes 1572872 | tf_op jit(solution)/shard_map/ppermute | solution.py:36
  223.5 10.3 %collective-permute-start.25 = (bf16[128,2048]{1,0:T(8,128)(2,1)S(1)}, bf16[128,2048]{1,0:T(8,128)(2,1)S(1)}, u32[]{:S(2)}, u32[]{:S(2)}) collective-permute-start(bf16[128,2048]{1,0:T(8,128)(2,1)S(1)} %collective-permute-done.24.refs_1_), channel_id=1, source_target_pairs={{0,16},{16,0},{1,17},{17,1},{2,18},{18,2},{3,19},{19,3},{4,20},{20... | collective-permute-start | bytes 1572872 | tf_op jit(solution)/shard_map/ppermute | solution.py:40
  224.0 9.8 %collective-permute-start.26 = (bf16[128,2048]{1,0:T(8,128)(2,1)S(1)}, bf16[128,2048]{1,0:T(8,128)(2,1)S(1)}, u32[]{:S(2)}, u32[]{:S(2)}) collective-permute-start(bf16[128,2048]{1,0:T(8,128)(2,1)S(1)} %collective-permute-done.23.refs_0_), channel_id=1, source_target_pairs={{0,16},{16,0},{1,17},{17,1},{2,18},{18,2},{3,19},{19,3},{4,20},{20... | collective-permute-start | bytes 1572872 | tf_op jit(solution)/shard_map/ppermute | solution.py:40
  224.0 18.0 %collective-permute-start.21 = (bf16[128,2048]{1,0:T(8,128)(2,1)S(1)}, bf16[128,2048]{1,0:T(8,128)(2,1)S(1)}, u32[]{:S(2)}, u32[]{:S(2)}) collective-permute-start(bf16[128,2048]{1,0:T(8,128)(2,1)S(1)} %get-tuple-element.23.refs_0_), channel_id=1, source_target_pairs={{0,16},{16,0},{1,17},{17,1},{2,18},{18,2},{3,19},{19,3},{4,20},{20... | collective-permute-start | bytes 1572872 | tf_op jit(solution)/shard_map/ppermute | solution.py:40
  233.4 12.7 %collective-permute-start.30 = (bf16[128,2048]{1,0:T(8,128)(2,1)S(1)}, bf16[128,2048]{1,0:T(8,128)(2,1)S(1)}, u32[]{:S(2)}, u32[]{:S(2)}) collective-permute-start(bf16[128,2048]{1,0:T(8,128)(2,1)S(1)} %slice.78), channel_id=1, source_target_pairs={{0,16},{16,0},{1,17},{17,1},{2,18},{18,2},{3,19},{19,3},{4,20},{20... | collective-permute-start | bytes 1572872 | tf_op jit(solution)/shard_map/ppermute | solution.py:40
  245.9 13.2 %collective-permute-start.22 = (bf16[128,2048]{1,0:T(8,128)(2,1)S(1)}, bf16[128,2048]{1,0:T(8,128)(2,1)S(1)}, u32[]{:S(2)}, u32[]{:S(2)}) collective-permute-start(bf16[128,2048]{1,0:T(8,128)(2,1)S(1)} %slice.71), channel_id=1, source_target_pairs={{0,16},{16,0},{1,17},{17,1},{2,18},{18,2},{3,19},{19,3},{4,20},{20... | collective-permute-start | bytes 1572872 | tf_op jit(solution)/shard_map/ppermute | solution.py:40
  246.3 10.5 %collective-permute-start.31 = (bf16[64,2048]{1,0:T(8,128)(2,1)S(1)}, bf16[64,2048]{1,0:T(8,128)(2,1)S(1)}, u32[]{:S(2)}, u32[]{:S(2)}) collective-permute-start(bf16[64,2048]{1,0:T(8,128)(2,1)S(1)} %get-tuple-element.33), channel_id=1, source_target_pairs={{0,1},{1,2},{2,3},{3,0},{16,19},{17,16},{18,17},{19,18},{4,5},{5,6... | collective-permute-start | bytes 786440 | tf_op jit(solution)/shard_map/ppermute | solution.py:36
  246.4 10.4 %collective-permute-start.32 = (bf16[64,2048]{1,0:T(8,128)(2,1)S(1)}, bf16[64,2048]{1,0:T(8,128)(2,1)S(1)}, u32[]{:S(2)}, u32[]{:S(2)}) collective-permute-start(bf16[64,2048]{1,0:T(8,128)(2,1)S(1)} %get-tuple-element.32), channel_id=1, source_target_pairs={{0,3},{1,0},{2,1},{3,2},{16,17},{17,18},{18,19},{19,16},{4,7},{5,4... | collective-permute-start | bytes 786440 | tf_op jit(solution)/shard_map/ppermute | solution.py:36
  250.0 11.2 %collective-permute-start.34 = (bf16[64,2048]{1,0:T(8,128)(2,1)S(1)}, bf16[64,2048]{1,0:T(8,128)(2,1)S(1)}, u32[]{:S(2)}, u32[]{:S(2)}) collective-permute-start(bf16[64,2048]{1,0:T(8,128)(2,1)S(1)} %slice.104), channel_id=1, source_target_pairs={{0,3},{1,0},{2,1},{3,2},{16,17},{17,18},{18,19},{19,16},{4,7},{5,4... | collective-permute-start | bytes 786440 | tf_op jit(solution)/shard_map/ppermute | solution.py:36
  250.1 12.2 %collective-permute-start.35 = (bf16[64,2048]{1,0:T(8,128)(2,1)S(1)}, bf16[64,2048]{1,0:T(8,128)(2,1)S(1)}, u32[]{:S(2)}, u32[]{:S(2)}) collective-permute-start(bf16[64,2048]{1,0:T(8,128)(2,1)S(1)} %slice.103), channel_id=1, source_target_pairs={{0,1},{1,2},{2,3},{3,0},{16,19},{17,16},{18,17},{19,18},{4,5},{5,6... | collective-permute-start | bytes 786440 | tf_op jit(solution)/shard_map/ppermute | solution.py:36
  (23 other events, 289.5 us)
Sparse Core Ops, SparseCore 0:
  11.4 98.4 all-gather.1
